TPU v7x, 256 devices: a whole 4x4x8 slice. The times are simulated.
256 devices in a mesh: section: 2 (over core), seq: 128 (over x, z, y).
Axes of the slice: x: 4, y: 4, z: 8, core: 2. Of those that a mesh axis runs over, the one named last changes fastest.
Arguments:
- acts: bfloat16 [2, 32768, 2048], P('section', 'seq'), may hold values from -6 to 6
- in_proj: bfloat16 [2, 2048, 4640], P('section', 'seq'), may hold values from -0.125 to 0.125
- out_proj: bfloat16 [2, 2048, 2048], P('section'), may hold values from -0.125 to 0.125
- conv_weight: float32 [2, 4, 2304], P('section'), may hold values from -3 to 3
- conv_bias: float32 [2, 2304], P('section'), may hold values from -3 to 3
- dt_bias: float32 [2, 32], P('section'), may hold values from -4 to -1
- decay_rate: float32 [2, 32], P('section'), may hold values from 0.0001 to 0.5
- skip_gain: float32 [2, 32], P('section'), may hold values from -4 to 4
- level_bias: float32 [2, 256], P('section'), may hold values from -4 to 4
- norm_gain: float32 [2, 2048], P('section'), may hold values from 0.5 to 1.5
- gate_gain: float32 [2, 2048], P('section'), may hold values from 0.5 to 1.5
Outputs:
- handoff: bfloat16 [2, 32768, 2048], P('section', 'seq')
All inputs are finite; a program needn't handle non-finite values.
Results may differ from a plain program's by a relative error of at most 0.006.
Values may be sent and summed in bfloat16 or wider, within the bound.
No kernel may reach another device: no remote copies, remote signals or barrier semaphores. Data moves between devices by JAX's collectives and lax.ppermute only.
A program may use at most 128 MiB of HBM per device.

v0:
```python
import jax
import jax.numpy as jnp
from jax import lax
from jax.experimental import pallas as pl
from jax.experimental.pallas import tpu as pltpu
from jax.sharding import PartitionSpec as P

EPS = 1e-05
F32 = jnp.float32
BF = jnp.bfloat16


NX, NZ, NY = 4, 8, 4
ROWS = 256
HEADS = 8
HD = 64
XW = HEADS * HD
NS = 128
HALO = 16
WA, WB = 768, 640
EXT = ROWS + HALO
SPLIT = 144
KX = 512


def route(move):
    pairs = []
    for x in range(NX):
        for z in range(NZ):
            for y in range(NY):
                a, b, c = move(x, z, y)
                pairs.append(
                    ((x * NZ + z) * NY + y, ((a % NX) * NZ + b % NZ) * NY + c % NY)
                )
    return pairs


X_UP = route(lambda x, z, y: (x + 1, z, y))
X_DOWN = route(lambda x, z, y: (x - 1, z, y))
Z_UP = route(lambda x, z, y: (x, z + 1, y))
Z_DOWN = route(lambda x, z, y: (x, z - 1, y))
Y_UP = route(lambda x, z, y: (x, z, y + 1))
Y_DOWN = route(lambda x, z, y: (x, z, y - 1))
Y_TWO = route(lambda x, z, y: (x, z, y + 2))
HALO_NEXT = [(i, i + 1) for i in range(NX * NZ * NY - 1)]
EXCHANGES = [
    route(lambda x, z, y: (x, z ^ 1, y)),
    route(lambda x, z, y: (x, z ^ 2, y)),
    route(lambda x, z, y: (x, 7 - z, y)),
    route(lambda x, z, y: (x ^ 1, z, y)),
    route(lambda x, z, y: (3 - x, z, y)),
]


def sent(value, pairs):
    return lax.ppermute(value, "seq", pairs)


def spread(first, stride):
    row = lax.broadcasted_iota(jnp.int32, (128, XW), 0)
    col = lax.broadcasted_iota(jnp.int32, (128, XW), 1)
    return jnp.where(row == first + stride * (col // HD), 1.0, 0.0).astype(BF)


def mm(a, b):
    return jnp.dot(a.astype(BF), b.astype(BF), preferred_element_type=F32)


def softplus(v):
    return jnp.maximum(v, 0.0) + jnp.log1p(jnp.exp(-jnp.abs(v)))


def silu(v):
    half = 0.5 * v
    return half + half * jnp.tanh(half)


def conv_block(wide, taps, bias):
    mixed = bias[0:1, :] + taps[0:1, :] * wide[HALO - 3 : HALO - 3 + ROWS, :]
    for k in range(1, 4):
        mixed = mixed + taps[k : k + 1, :] * wide[HALO - 3 + k : HALO - 3 + k + ROWS, :]
    return silu(mixed)


def shape_of(dtype, *shape):
    return pltpu.VMEM(shape, dtype)


def near(value):
    return pltpu.with_memory_space_constraint(value, pltpu.VMEM)


def run(kernel, scalars, arrays, outs, scratch=()):
    smem = pl.BlockSpec(memory_space=pltpu.SMEM)
    vmem = pl.BlockSpec(memory_space=pltpu.VMEM)
    return pl.pallas_call(
        kernel,
        in_specs=[smem] * len(scalars) + [vmem] * len(arrays),
        out_specs=[vmem] * len(outs),
        out_shape=outs,
        scratch_shapes=list(scratch),
        compiler_params=pltpu.CompilerParams(vmem_limit_bytes=10 << 20),
    )(*scalars, *map(near, arrays))


def each_block(body):
    def step(j, carry):
        body(j)
        return carry

    lax.fori_loop(0, NY, step, 0)


def part_kernel(rows_ref, own_ref, below_ref, above_ref, out_ref):
    def block(j):
        total = None
        for k, w_ref in enumerate((own_ref, below_ref, above_ref)):
            there = rows_ref[j, :, k * KX : (k + 1) * KX]
            part = jnp.dot(there, w_ref[...], preferred_element_type=F32)
            total = part if total is None else total + part
        out_ref[j] = total

    each_block(block)


def run_part(rows, own, below, above):
    width = own.shape[1]
    return run(part_kernel, (), (rows, own, below, above), [shape_of(F32, NY, EXT, width)])[0]


def stack_kernel(y_ref, own_ref, below_ref, above_ref, lo_ref, hi_ref, out_ref):
    y = y_ref[0]
    out_ref[y] = own_ref[...]
    out_ref[(y + 3) % NY] = below_ref[...]
    out_ref[(y + 1) % NY] = above_ref[...]
    out_ref[(y + 2) % NY, 0:SPLIT, :] = lo_ref[...]
    out_ref[(y + 2) % NY, SPLIT:, :] = hi_ref[...]


def finished(part_ref, rows_ref, fa_ref, fb_ref, j):
    total = (
        part_ref[j]
        + jnp.dot(rows_ref[j, :, 3 * KX : 3 * KX + KX // 2], fa_ref[...], preferred_element_type=F32)
        + jnp.dot(rows_ref[j, :, 3 * KX + KX // 2 :], fb_ref[...], preferred_element_type=F32)
    )
    return total.astype(BF).astype(F32)


def state_kernel(
    part_ref, rows_ref, fa_ref, fb_ref, taps_ref, bias_ref, small_bias_ref, rate_ref, spread_ref,
    xs_ref, b_ref, sp_ref, cum_ref, e2_ref, sc_ref, row_ref, s_ref, pair_ref, state_ref, logs_ref, msg_ref,
    wide_ref, acc_ref, carry_ref,
):
    acc_ref[...] = jnp.zeros_like(acc_ref)
    carry_ref[...] = jnp.zeros_like(carry_ref)
    logs_ref[...] = jnp.zeros_like(logs_ref)

    def block(j):
        p = finished(part_ref, rows_ref, fa_ref, fb_ref, j)
        wide_ref[...] = p[:, : XW + NS]
        mixed = conv_block(wide_ref, taps_ref, bias_ref)
        xs = mixed[:, :XW]
        b_mat = mixed[:, XW:]
        sp = softplus(p[HALO:, XW + NS :] + small_bias_ref[0:1, :])
        g = -sp * rate_ref[0:1, :]
        row = lax.broadcasted_iota(jnp.int32, (ROWS, ROWS), 0)
        col = lax.broadcasted_iota(jnp.int32, (ROWS, ROWS), 1)
        tri = jnp.where(col <= row, 1.0, 0.0).astype(BF)
        g0 = g.astype(BF)
        r1 = g - g0.astype(F32)
        g1 = r1.astype(BF)
        g2 = r1 - g1.astype(F32)
        cum = mm(tri, g0) + mm(tri, g1) + mm(tri, g2)
        last = cum[ROWS - 1 : ROWS, :]
        tail = jnp.exp(last - cum) * sp
        head_spread = spread_ref[8]
        xt = xs * mm(tail, head_spread)
        state = mm(b_mat.T, xt)
        last8 = jnp.broadcast_to(last, (16, 128))
        hi = last8.astype(BF)
        rest = last8 - hi.astype(F32)
        mid = rest.astype(BF)
        low = rest - mid.astype(F32)
        last_wide = mm(hi, head_spread) + mm(mid, head_spread) + mm(low, head_spread)
        acc = jnp.exp(last_wide[0:1, :]) * acc_ref[...] + state
        acc_ref[...] = acc
        group = carry_ref[0:1, :]
        pair = jnp.where(j == 2, 0.0, carry_ref[1:2, :])
        e2_ref[j] = jnp.exp(cum + pair)
        lane = lax.broadcasted_iota(jnp.int32, (128, 128), 1)
        src = lax.broadcasted_iota(jnp.int32, (128, 128), 0)
        to_levels = jnp.where(src - HEADS * 8 == lane // 8, 1.0, 0.0)
        sc_ref[j] = (sp * mm(jnp.exp(cum + group), to_levels)).astype(BF)
        carry_ref[0:1, :] = group + last
        carry_ref[1:2, :] = pair + last
        xs_ref[j] = xs
        b_ref[j] = b_mat.astype(BF)
        sp_ref[j] = sp
        cum_ref[j] = cum
        row_ref[j] = cum.T[HEADS * 8 : HEADS * 9, :]
        s_ref[j] = state.astype(BF)
        logs_ref[0:1, :] = logs_ref[0:1, :] + last_wide[0:1, :]

        @pl.when(j == 1)
        def _():
            pair_ref[...] = acc.astype(BF)

        @pl.when(j == NY - 1)
        def _():
            state_ref[...] = acc
            pack_message(msg_ref, acc, logs_ref[0:1, :])

    each_block(block)


def pack_message(msg_ref, state, log):
    msg_ref[0:NS, :] = state.astype(BF)
    hi = log.astype(BF).astype(F32)
    row = lax.broadcasted_iota(jnp.int32, (16, XW), 0)
    both = jnp.where(row == 0, hi, jnp.where(row == 1, log - hi, 0.0))
    msg_ref[NS:, :] = both.astype(BF)


def run_state(part, rows, far_a, far_b, taps, bias, small_bias, rate, spreads):
    return run(
        state_kernel,
        (),
        (part, rows, far_a, far_b, taps, bias, small_bias, rate, spreads),
        [
            shape_of(F32, NY, ROWS, XW), shape_of(BF, NY, ROWS, NS), shape_of(F32, NY, ROWS, 128),
            shape_of(F32, NY, ROWS, 128), shape_of(F32, NY, ROWS, 128), shape_of(BF, NY, ROWS, 128),
            shape_of(F32, NY, HEADS, ROWS), shape_of(BF, NY, NS, XW),
            shape_of(BF, NS, XW), shape_of(F32, NS, XW), shape_of(F32, 8, XW), shape_of(BF, NS + 16, XW),
        ],
        [
            pltpu.VMEM((EXT, XW + NS), F32),
            pltpu.VMEM((NS, XW), F32),
            pltpu.VMEM((8, 128), F32),
        ],
    )


def intra_kernel(
    part_ref, rows_ref, fa_ref, fb_ref, taps_ref, bias_ref, skip_ref,
    xs_ref, b_ref, sp_ref, cum_ref, e2_ref, row_ref, s1_ref, s2_ref, spread_ref,
    y_ref, c_ref, z_ref, wide_ref,
):
    def block(j):
        p = finished(part_ref, rows_ref, fa_ref, fb_ref, j)
        z_ref[j] = p[HALO:, :XW].astype(BF)
        wide_ref[...] = p[:, XW:]
        c_mat = conv_block(wide_ref, taps_ref, bias_ref).astype(BF)
        c_ref[j] = c_mat
        xs = xs_ref[j]
        sp = sp_ref[j].astype(BF)
        cum = cum_ref[j]
        scores = lax.dot_general(
            c_mat, b_ref[j], (((1,), (1,)), ((), ())), preferred_element_type=F32
        )
        row = lax.broadcasted_iota(jnp.int32, (ROWS, ROWS), 0)
        col = lax.broadcasted_iota(jnp.int32, (ROWS, ROWS), 1)
        causal = col <= row
        head_spread = spread_ref[8]
        xd = (xs * mm(sp, head_spread)).astype(BF)
        parts = []
        for h in range(HEADS):
            lane = HEADS * 8 + h
            diff = cum[:, lane : lane + 1] - row_ref[j, h : h + 1, :]
            decay = jnp.exp(jnp.where(causal, diff, -1e30)) * scores
            parts.append(mm(decay, xd[:, h * HD : (h + 1) * HD]))
        y = jnp.concatenate(parts, axis=1) * mm(sp, spread_ref[0])
        y = y + skip_ref[0:1, :] * xs
        odd = (j % 2).astype(F32)
        late = (j // 2).astype(F32)
        one = mm(sp, spread_ref[1]) * mm(jnp.exp(cum), head_spread)
        y = y + mm(c_mat, s1_ref[(j // 2) * 2]) * (one * odd)
        two = mm(sp, spread_ref[2]) * mm(e2_ref[j], head_spread)
        y = y + mm(c_mat, s2_ref[...]) * (two * late)
        y_ref[j] = y

    each_block(block)


def run_intra(part, rows, far_a, far_b, taps, bias, skip, xs, b_mat, sp, cum, e2, row, states, pair, spreads):
    return run(
        intra_kernel,
        (),
        (part, rows, far_a, far_b, taps, bias, skip, xs, b_mat, sp, cum, e2, row, states, pair, spreads),
        [shape_of(F32, NY, ROWS, XW), shape_of(BF, NY, ROWS, NS), shape_of(BF, NY, ROWS, XW)],
        [pltpu.VMEM((EXT, NS), F32)],
    )


def merge_kernel(bit_ref, got_ref, state_ref, logs_ref, msg_ref, new_ref, new_logs_ref, bucket_ref):
    upper = bit_ref[0] == 1
    other = got_ref[0:NS, :].astype(F32)
    tail = got_ref[NS:, :].astype(F32)
    other_log = tail[0:1, :] + tail[1:2, :]
    log = logs_ref[0:1, :]
    before = logs_ref[1:2, :]
    bucket = jnp.where(upper, jnp.exp(before), 0.0) * other
    bucket_ref[...] = bucket.astype(BF)
    state = (
        jnp.where(upper, jnp.exp(log), 1.0) * other
        + jnp.where(upper, 1.0, jnp.exp(other_log)) * state_ref[...]
    )
    new_ref[...] = state
    log = log + other_log
    new_logs_ref[...] = jnp.zeros_like(new_logs_ref)
    new_logs_ref[0:1, :] = log
    new_logs_ref[1:2, :] = jnp.where(upper, before + other_log, before)
    pack_message(msg_ref, state, log)


def run_merge(bit, got, state, logs):
    return run(
        merge_kernel,
        (bit.reshape(1),),
        (got, state, logs),
        [shape_of(BF, NS + 16, XW), shape_of(F32, NS, XW), shape_of(F32, 8, XW), shape_of(BF, NS, XW)],
    )


def cross_kernel(at_ref, y_ref, c_ref, sc_ref, z_ref, k3, k4, k5, k6, k7, spread_ref, *q_refs):
    for k, q_ref in enumerate(q_refs):
        j = at_ref[k]
        c_mat = c_ref[j]
        scale = sc_ref[j]
        y = y_ref[j]
        for level, bucket in ((3, k3), (4, k4), (5, k5), (6, k6), (7, k7)):
            y = y + mm(c_mat, bucket[...]) * mm(scale, spread_ref[level])
        q_ref[...] = (y * silu(z_ref[j].astype(F32))).astype(BF)


def run_cross(at, y, c_mat, sc, z, buckets, spreads):
    return run(
        cross_kernel,
        (jnp.stack(at),),
        (y, c_mat, sc, z, *buckets, spreads),
        [shape_of(BF, ROWS, XW)] * len(at),
    )


def out_kernel(at_ref, q0, q1, q2, q3, gain_ref, w_ref, acts_ref, out_ref, acc_ref):
    blocks = (q0, q1, q2, q3)
    square = sum(
        jnp.sum(jnp.square(q[...].astype(F32)), axis=1, keepdims=True) for q in blocks
    )
    scale = lax.rsqrt(square / (NY * XW) + EPS)
    acc_ref[...] = acts_ref[...].astype(F32)
    for k, q in enumerate(blocks):
        there = pl.ds(pl.multiple_of(at_ref[k] * XW, XW), XW)
        n = q[...].astype(F32) * scale * gain_ref[0:1, there]
        acc_ref[...] += jnp.dot(n.astype(BF), w_ref[there, :], preferred_element_type=F32)
    out_ref[...] = acc_ref[...].astype(BF)


def run_out(at, blocks, gain, weight, acts):
    width = weight.shape[1]
    return run(
        out_kernel,
        (at,),
        (*blocks, gain, weight, acts),
        [shape_of(BF, ROWS, width)],
        [pltpu.VMEM((ROWS, width), F32)],
    )[0]


def norm_kernel(at_ref, halo_ref, acts_ref, gain_ref, out_ref, full_ref):
    for start, ref in ((0, halo_ref), (HALO, acts_ref)):
        v = ref[...].astype(F32)
        scale = lax.rsqrt(jnp.mean(v * v, axis=1, keepdims=True) + EPS)
        full_ref[start : start + v.shape[0], :] = v * scale * gain_ref[0:1, :]
    for k in range(NX):
        start = pl.multiple_of(at_ref[k] * KX, KX)
        part = pltpu.roll(full_ref[:, pl.ds(start, KX)], at_ref[NX], 1)
        out_ref[:, k * KX : (k + 1) * KX] = part.astype(BF)


def run_norm(at, halo, acts, gain):
    width = acts.shape[1]
    return run(
        norm_kernel,
        (at,),
        (halo, acts, gain),
        [shape_of(BF, EXT, width)],
        [pltpu.VMEM((EXT, width), F32)],
    )[0]


def columns_kernel(y_ref, shard_ref, o0, o1, o2, o3, all_ref):
    shard = shard_ref[...]
    for t in range(NY):
        x0, z0 = t * XW, 2304 + t * XW
        dt0, lv0 = 4352 + t * HEADS, 4384 + t * HEADS * 8
        all_ref[t, :, 0:XW] = shard[:, x0 : x0 + XW]
        all_ref[t, :, XW : XW + NS] = shard[:, 2048 : 2048 + NS]
        all_ref[t, :, XW + NS : WA] = jnp.concatenate(
            [
                shard[:, lv0 : lv0 + HEADS * 8].astype(F32),
                shard[:, dt0 : dt0 + HEADS].astype(F32),
                jnp.zeros((shard.shape[0], 128 - HEADS * 9), F32),
            ],
            axis=1,
        ).astype(BF)
        all_ref[t, :, WA : WA + XW] = shard[:, z0 : z0 + XW]
        all_ref[t, :, WA + XW :] = shard[:, 2048 + NS : 2304]
    for k, out in enumerate((o0, o1, o2, o3)):
        out[...] = all_ref[(y_ref[0] + k) % NY]


def run_columns(y, shard):
    rows = shard.shape[0]
    return run(
        columns_kernel,
        (y.reshape(1),),
        (shard,),
        [shape_of(BF, rows, WA + WB)] * 4,
        [pltpu.VMEM((NY, rows, WA + WB), BF)],
    )


def join_kernel(y_ref, b0, b1, b2, b3, out_ref):
    rows = b0.shape[0]
    for back, block in ((0, b0), (3, b1), (2, b2), (1, b3)):
        start = pl.multiple_of(((y_ref[0] + back) % NY) * rows, rows)
        out_ref[pl.ds(start, rows), :] = block[...]


def run_join(y, blocks):
    rows, width = blocks[0].shape
    return run(join_kernel, (y.reshape(1),), blocks, [shape_of(BF, NY * rows, width)])[0]


def gather_kernel(*refs):
    *blocks, a_ref, b_ref = refs
    rows = blocks[0].shape[0]
    for k, block in enumerate(blocks):
        a_ref[k * rows : (k + 1) * rows, :] = block[:, :WA]
        b_ref[k * rows : (k + 1) * rows, :] = block[:, WA:]


def together(*values):
    return lax.optimization_barrier(values)


def ring_z(block):
    up, down = [block], [block]
    for k in range(4):
        up.append(sent(up[-1], Z_UP))
        if k < 3:
            down.append(sent(down[-1], Z_DOWN))
    return down + [up[4], up[3], up[2], up[1]]


def ring_four(block, up, down):
    below = sent(block, up)
    above = sent(block, down)
    half = block.shape[0] // 2
    return below, above, lambda: (sent(below[:half], up), sent(above[half:], down))


def layer(
    acts,
    in_proj,
    out_proj,
    conv_weight,
    conv_bias,
    dt_bias,
    decay_rate,
    skip_gain,
    level_bias,
    norm_gain,
    gate_gain,
):
    index = lax.axis_index("seq")
    y = index % NY
    z = (index // NY) % NZ
    x = index // (NY * NZ)
    w0, w1, w2, w3 = run_columns(y, in_proj[0])
    columns = run_join(y, (w0, sent(w1, Y_UP), sent(w2, Y_TWO), sent(w3, Y_DOWN)))
    tail, _ = together(acts[0, ROWS - HALO :], w1)
    halo = sent(tail, HALO_NEXT)
    order = jnp.stack([x, (x + 3) % NX, (x + 1) % NX, (x + 2) % NX, (512 - 64 * z) % 512])
    u = run_norm(order, halo, acts[0], norm_gain)

    blocks = ring_z(columns)
    u, _ = together(u, columns)
    below, above, _ = ring_four(u, Y_UP, Y_DOWN)
    lo, hi, _ = together(below[:SPLIT], above[SPLIT:], blocks[3])
    far_lo, far_hi = sent(lo, Y_UP), sent(hi, Y_DOWN)
    rows = run(
        stack_kernel, (y.reshape(1),), (u, below, above, far_lo, far_hi),
        [shape_of(BF, NY, EXT, u.shape[1])],
    )[0]
    depth = len(blocks) * blocks[0].shape[0]
    by_a, by_b = run(gather_kernel, (), blocks, [shape_of(BF, depth, WA), shape_of(BF, depth, WB)])

    y, zero, _ = together(y, jnp.zeros((), jnp.int32), blocks[7])
    piece = lambda v, width: lax.dynamic_slice_in_dim(v, y * width, width, v.ndim - 1)
    taps_a = jnp.concatenate(
        [piece(conv_weight[0, :, :2048], XW), conv_weight[0, :, 2048 : 2048 + NS]], axis=1
    )
    bias_a = jnp.concatenate(
        [piece(conv_bias[:, :2048], XW), conv_bias[:, 2048 : 2048 + NS]], axis=1
    )
    pad = jnp.zeros((1, 128 - HEADS * 9), F32)
    small_bias = jnp.concatenate(
        [piece(level_bias, HEADS * 8), piece(dt_bias, HEADS), pad], axis=1
    )
    rate = jnp.concatenate(
        [jnp.zeros((1, HEADS * 8), F32), piece(decay_rate, HEADS), pad], axis=1
    )
    skip = jnp.repeat(piece(skip_gain, HEADS), HD, axis=1)
    spreads = jnp.stack([spread(zero + k, 8) for k in range(8)] + [spread(zero + HEADS * 8, 1)])

    a_below, a_above, a_far = ring_four(by_a, X_UP, X_DOWN)
    fa_a, fb_a = a_far()
    part_a = run_part(rows, by_a, a_below, a_above)

    by_b, fa_a, fb_a = together(by_b, fa_a, fb_a)
    b_below, b_above, b_far = ring_four(by_b, X_UP, X_DOWN)
    xs, b_mat, sp, cum, e2, sc, row, states, pair, state, logs, message = run_state(
        part_a, rows, fa_a, fb_a, taps_a, bias_a, small_bias, rate, spreads
    )
    fa_b, fb_b = b_far()
    part_b = run_part(rows, by_b, b_below, b_above)

    bits = [z & 1, (z >> 1) & 1, (z >> 2) & 1, x & 1, (x >> 1) & 1]
    buckets = []
    for bit, pairs in zip(bits, EXCHANGES, strict=True):
        got = sent(message, pairs)
        message, state, logs, bucket = run_merge(bit, got, state, logs)
        buckets.append(bucket)

    y_part, c_mat, z_cols = run_intra(
        part_b, rows, fa_b, fb_b, conv_weight[0, :, 2048 + NS :], conv_bias[:, 2048 + NS :], skip,
        xs, b_mat, sp, cum, e2, row, states, pair, spreads,
    )
    block = lambda k: (y + k) % NY
    q2, q1 = run_cross((block(2), block(1)), y_part, c_mat, sc, z_cols, buckets, spreads)
    q3, q0 = run_cross((block(3), block(0)), y_part, c_mat, sc, z_cols, buckets, spreads)
    blocks = (q0, sent(q1, Y_UP), sent(q2, Y_TWO), sent(q3, Y_DOWN))
    heads_at = jnp.stack([block(0), block(3), block(2), block(1)])
    result = run_out(heads_at, blocks, gate_gain, out_proj[0], acts[0])
    return lax.ppermute(result, "section", [(0, 1), (1, 0)])[None]


def solution(mesh):
    return jax.shard_map(
        layer,
        mesh=mesh,
        in_specs=(
            P("section", "seq", None),
            P("section", "seq", None),
            P("section", None, None),
            P("section", None, None),
            P("section", None),
            P("section", None),
            P("section", None),
            P("section", None),
            P("section", None),
            P("section", None),
            P("section", None),
        ),
        out_specs=P("section", "seq", None),
        check_vma=False,
    )
```

profile of v0, /device:TPU:1, one launch (start us, length us, event | category | flops | bytes accessed | tf_op | source)
XLA Modules:
  0.0 202.1 jit_solution(5175463100416666658)
XLA Ops:
  1.0 2.2 %collective-permute-start = (bf16[16,1408]{1,0:T(8,128)(2,1)S(1)}, bf16[16,1408]{1,0:T(8,128)(2,1)S(1)}, u32[]{:S(2)}, u32[]{:S(2)}) collective-permute-start(bf16[16,1408]{1,0:T(8,128)(2,1)S(1)} %get-tuple-element.57), channel_id=1, source_target_pairs={{0,1},{1,2},{2,3},{3,0},{4,5},{5,6},{6,7},{7,4},{8,9},{9,10},{10,1... | collective-permute-start | bytes 135176 | tf_op jit(solution)/shard_map/ppermute | solution.py:56
  4.1 3.2 %collective-permute-start.4 = (bf16[16,2048]{1,0:T(8,128)(2,1)S(1)}, bf16[16,2048]{1,0:T(8,128)(2,1)S(1)}, u32[]{:S(2)}, u32[]{:S(2)}) collective-permute-start(bf16[16,2048]{1,0:T(8,128)(2,1)S(1)} %slice_bitcast_fusion), channel_id=1, source_target_pairs={{0,1},{1,2},{2,3},{3,4},{4,5},{5,6},{6,7},{7,8},{8,9},{9,10},{10,1... | collective-permute-start | bytes 196616 | tf_op jit(solution)/shard_map/ppermute | solution.py:56
  7.3 1.4 collective-permute-start.1
  8.7 2.1 %collective-permute-start.2 = (bf16[16,1408]{1,0:T(8,128)(2,1)S(1)}, bf16[16,1408]{1,0:T(8,128)(2,1)S(1)}, u32[]{:S(2)}, u32[]{:S(2)}) collective-permute-start(bf16[16,1408]{1,0:T(8,128)(2,1)S(1)} %get-tuple-element.59), channel_id=1, source_target_pairs={{0,3},{1,0},{2,1},{3,2},{4,7},{5,4},{6,5},{7,6},{8,11},{9,8},{10,9... | collective-permute-start | bytes 135176 | tf_op jit(solution)/shard_map/ppermute | solution.py:56
  13.3 1.9 collective-permute-start.3
  15.2 3.5 %collective-permute-start.7 = (bf16[64,1408]{1,0:T(8,128)(2,1)}, bf16[64,1408]{1,0:T(8,128)(2,1)}, u32[]{:S(2)}, u32[]{:S(2)}) collective-permute-start(bf16[64,1408]{1,0:T(8,128)(2,1)} %shard_map.110.refs_0_), channel_id=1, source_target_pairs={{0,28},{1,29},{2,30},{3,31},{4,0},{5,1},{6,2},{7,3},{8,4},{9,5},{1... | collective-permute-start | bytes 540680 | tf_op jit(solution)/shard_map/ppermute | solution.py:56
  18.7 1.2 copy-done.4
  20.6 1.6 shard_map.111.own_ref
  22.8 2.3 %collective-permute-start.6 = (bf16[272,2048]{1,0:T(8,128)(2,1)S(1)}, bf16[272,2048]{1,0:T(8,128)(2,1)}, u32[]{:S(2)}, u32[]{:S(2)}) collective-permute-start(bf16[272,2048]{1,0:T(8,128)(2,1)S(1)} %shard_map.111.own_ref), channel_id=1, source_target_pairs={{0,3},{1,0},{2,1},{3,2},{4,7},{5,4},{6,5},{7,6},{8,11},{9,8},{10,9... | collective-permute-start | bytes 3342344 | tf_op jit(solution)/shard_map/ppermute | solution.py:56
  25.3 2.7 %collective-permute-start.8 = (bf16[64,1408]{1,0:T(8,128)(2,1)}, bf16[64,1408]{1,0:T(8,128)(2,1)S(1)}, u32[]{:S(2)}, u32[]{:S(2)}) collective-permute-start(bf16[64,1408]{1,0:T(8,128)(2,1)} %collective-permute-done.7.refs_1_), channel_id=1, source_target_pairs={{0,28},{1,29},{2,30},{3,31},{4,0},{5,1},{6,2},{7,3},{8,4},{9,5},{1... | collective-permute-start | bytes 540680 | tf_op jit(solution)/shard_map/ppermute | solution.py:56
  28.0 3.2 %collective-permute-done.12.refs_6_ = bf16[64,1408]{1,0:T(8,128)(2,1)S(1)} collective-permute-done((bf16[64,1408]{1,0:T(8,128)(2,1)}, bf16[64,1408]{1,0:T(8,128)(2,1)S(1)}, u32[]{:S(2)}, u32[]{:S(2)}) %collective-permute-start.12) | collective-permute-done | bytes 180256 | tf_op jit(solution)/shard_map/ppermute | solution.py:56
  31.3 2.7 %collective-permute-start.9 = (bf16[64,1408]{1,0:T(8,128)(2,1)S(1)}, bf16[64,1408]{1,0:T(8,128)(2,1)S(1)}, u32[]{:S(2)}, u32[]{:S(2)}) collective-permute-start(bf16[64,1408]{1,0:T(8,128)(2,1)S(1)} %collective-permute-done.8.refs_2_), channel_id=1, source_target_pairs={{0,28},{1,29},{2,30},{3,31},{4,0},{5,1},{6,2},{7,3},{8,4},{9,5},{1... | collective-permute-start | bytes 540680 | tf_op jit(solution)/shard_map/ppermute | solution.py:56
  34.1 3.1 %collective-permute-done.13.refs_5_ = bf16[64,1408]{1,0:T(8,128)(2,1)S(1)} collective-permute-done((bf16[64,1408]{1,0:T(8,128)(2,1)S(1)}, bf16[64,1408]{1,0:T(8,128)(2,1)S(1)}, u32[]{:S(2)}, u32[]{:S(2)}) %collective-permute-start.13) | collective-permute-done | bytes 180256 | tf_op jit(solution)/shard_map/ppermute | solution.py:56
  37.2 6.3 %collective-permute-done.14.refs_4_ = bf16[64,1408]{1,0:T(8,128)(2,1)S(1)} collective-permute-done((bf16[64,1408]{1,0:T(8,128)(2,1)S(1)}, bf16[64,1408]{1,0:T(8,128)(2,1)S(1)}, u32[]{:S(2)}, u32[]{:S(2)}) %collective-permute-start.14) | collective-permute-done | bytes 180256 | tf_op jit(solution)/shard_map/ppermute | solution.py:56
  46.8 1.5 collective-permute-start.17
  49.2 1.9 slice.53
  51.2 9.0 %collective-permute-done.15.below_ref = bf16[512,768]{1,0:T(8,128)(2,1)S(1)} collective-permute-done((bf16[512,768]{1,0:T(8,128)(2,1)S(1)}, bf16[512,768]{1,0:T(8,128)(2,1)S(1)}, u32[]{:S(2)}, u32[]{:S(2)}) %collective-permute-start.15) | collective-permute-done | bytes 786464 | tf_op jit(solution)/shard_map/ppermute | solution.py:56
  63.5 2.7 %collective-permute-start.18 = (bf16[256,768]{1,0:T(8,128)(2,1)}, bf16[256,768]{1,0:T(8,128)(2,1)}, u32[]{:S(2)}, u32[]{:S(2)}) collective-permute-start(bf16[256,768]{1,0:T(8,128)(2,1)} %slice.55), channel_id=1, source_target_pairs={{0,96},{1,97},{2,98},{3,99},{4,100},{5,101},{6,102},{7,103},{8,104... | collective-permute-start | bytes 1179656 | tf_op jit(solution)/shard_map/ppermute | solution.py:56
  66.2 1.7 collective-permute-start.11
  68.1 2.3 %collective-permute-done.16.fa_ref = bf16[256,768]{1,0:T(8,128)(2,1)} collective-permute-done((bf16[256,768]{1,0:T(8,128)(2,1)}, bf16[256,768]{1,0:T(8,128)(2,1)}, u32[]{:S(2)}, u32[]{:S(2)}) %collective-permute-start.16) | collective-permute-done | bytes 393248 | tf_op jit(solution)/shard_map/ppermute | solution.py:56
  71.6 2.7 %collective-permute-start.20 = (bf16[512,640]{1,0:T(8,128)(2,1)}, bf16[512,640]{1,0:T(8,128)(2,1)}, u32[]{:S(2)}, u32[]{:S(2)}) collective-permute-start(bf16[512,640]{1,0:T(8,128)(2,1)} %copy-done.12), channel_id=1, source_target_pairs={{0,96},{1,97},{2,98},{3,99},{4,100},{5,101},{6,102},{7,103},{8,104... | collective-permute-start | bytes 1966088 | tf_op jit(solution)/shard_map/ppermute | solution.py:56
  74.9 1.9 shard_map.112.rows_ref
  76.9 3.3 %shard_map.115.part_ref = f32[4,272,768]{2,1,0:T(8,128)S(1)} custom-call(bf16[4,272,2048]{2,1,0:T(8,128)(2,1)S(1)} %shard_map.112.rows_ref, bf16[512,768]{1,0:T(8,128)(2,1)S(1)} %copy-done.11, bf16[512,768]{1,0:T(8,128)(2,1)S(1)} %copy-done.7, bf16[512,768]{1,0:T(8,128)(2,1)S(1)} %copy-done.9), custom_call_target="tpu_custom_call" | custom-call | tf_op jit(solution)/shard_map/pallas_call | solution.py:96
  80.2 8.2 %shard_map.116 = (f32[4,256,512]{2,1,0:T(8,128)S(1)}, bf16[4,256,128]{2,1,0:T(8,128)(2,1)S(1)}, f32[4,256,128]{2,1,0:T(8,128)S(1)}, f32[4,256,128]{2,1,0:T(8,128...) custom-call(f32[4,272,768]{2,1,0:T(8,128)S(1)} %shard_map.115.part_r, ...), custom_call_target="tpu_custom_call" | custom-call | tf_op jit(solution)/shard_map/pallas_call | solution.py:96
  95.0 4.3 %collective-permute-done.23.got_ref = bf16[144,512]{1,0:T(8,128)(2,1)} collective-permute-done((bf16[144,512]{1,0:T(8,128)(2,1)}, bf16[144,512]{1,0:T(8,128)(2,1)}, u32[]{:S(2)}, u32[]{:S(2)}) %collective-permute-start.23) | collective-permute-done | bytes 147488 | tf_op jit(solution)/shard_map/ppermute | solution.py:56
  101.0 1.6 shard_map.118
  104.5 6.5 %collective-permute-done.24.got_ref = bf16[144,512]{1,0:T(8,128)(2,1)} collective-permute-done((bf16[144,512]{1,0:T(8,128)(2,1)}, bf16[144,512]{1,0:T(8,128)(2,1)}, u32[]{:S(2)}, u32[]{:S(2)}) %collective-permute-start.24) | collective-permute-done | bytes 147488 | tf_op jit(solution)/shard_map/ppermute | solution.py:56
  112.7 1.6 shard_map.119
  116.3 1.3 collective-permute-start.25
  117.6 5.3 %collective-permute-done.25.got_ref = bf16[144,512]{1,0:T(8,128)(2,1)} collective-permute-done((bf16[144,512]{1,0:T(8,128)(2,1)}, bf16[144,512]{1,0:T(8,128)(2,1)}, u32[]{:S(2)}, u32[]{:S(2)}) %collective-permute-start.25) | collective-permute-done | bytes 147488 | tf_op jit(solution)/shard_map/ppermute | solution.py:56
  124.6 1.6 shard_map.120
  128.2 1.7 slice.56
  129.9 1.5 collective-permute-start.21
  131.4 1.7 slice.57
  133.1 1.2 collective-permute-start.22
  136.0 1.6 shard_map.121
  141.8 2.3 %copy-done.2 = bf16[4,272,2048]{2,1,0:T(8,128)(2,1)S(1)} copy-done((bf16[4,272,2048]{2,1,0:T(8,128)(2,1)S(1)}, bf16[4,272,2048]{2,1,0:T(8,128)(2,1)}, u32[]{:S(2)}) %copy-start.2) | copy-done | bytes 4456472
  145.2 4.7 %shard_map.114.part_ref = f32[4,272,640]{2,1,0:T(8,128)S(1)} custom-call(bf16[4,272,2048]{2,1,0:T(8,128)(2,1)S(1)} %copy-done.2, bf16[512,640]{1,0:T(8,128)(2,1)S(1)} %copy-done.13, bf16[512,640]{1,0:T(8,128)(2,1)} %collective-permute-done.19.below_ref, bf16[512,640]{1,0:T(8,128)(2,1)} %collective-permute-done.20.above_ref), custom_call_target="tpu_custom_call" | custom-call | tf_op jit(solution)/shard_map/pallas_call | solution.py:96
  150.0 1.7 shard_map.122
  151.8 2.3 %copy-done.3 = bf16[4,272,2048]{2,1,0:T(8,128)(2,1)S(1)} copy-done((bf16[4,272,2048]{2,1,0:T(8,128)(2,1)S(1)}, bf16[4,272,2048]{2,1,0:T(8,128)(2,1)}, u32[]{:S(2)}) %copy-start.3) | copy-done | bytes 4456472
  154.1 8.8 %shard_map.117 = (f32[4,256,512]{2,1,0:T(8,128)S(1)}, bf16[4,256,128]{2,1,0:T(8,128)(2,1)S(1)}, bf16[4,256,512]{2,1,0:T(8,128)(2,1)S(1)}) custom-call(f32[4,272,640]{2,1,0:T(8,128)S(1)} %shard_map.114.part_ref, bf16[4,272,2048]{2,1,0:T(8,128)(2,1)S(1)} %copy-done.3, bf16[256,640]{1,0:T(8,128)(2,1)} %collective-permute-done.21.fa_ref, ...), custom_call_target="tpu_custom_call" | custom-call | tf_op jit(solution)/shard_map/pallas_call | solution.py:96
  162.9 2.2 %shard_map.124 = (bf16[256,512]{1,0:T(8,128)(2,1)S(1)}, bf16[256,512]{1,0:T(8,128)(2,1)S(1)}) custom-call(s32[2]{0:T(128)S(1)} %get-tuple-element.114.at_ref, f32[4,256,512]{2,1,0:T(8,128)S(1)} %get-tuple-element.79.y_ref, bf16[4,256,128]{2,1,0:T(8,128)(2,1)S(1)} %get-tuple-element.80.c_ref, bf16[4,256,128]{2,1,0:T(8,128)(2,1)S(1)} %get-tuple-element.81.sc_ref, ...), custom_call_target="tpu_custom_call" | custom-call | tf_op jit(solution)/shard_map/pallas_call | solution.py:96
  165.2 3.9 %collective-permute-start.29 = (bf16[256,512]{1,0:T(8,128)(2,1)S(1)}, bf16[256,512]{1,0:T(8,128)(2,1)S(1)}, u32[]{:S(2)}, u32[]{:S(2)}) collective-permute-start(bf16[256,512]{1,0:T(8,128)(2,1)S(1)} %get-tuple-element.105), channel_id=1, source_target_pairs={{0,2},{1,3},{2,0},{3,1},{4,6},{5,7},{6,4},{7,5},{8,10},{9,11},{10,... | collective-permute-start | bytes 786440 | tf_op jit(solution)/shard_map/ppermute | solution.py:56
  169.1 2.2 %shard_map.123 = (bf16[256,512]{1,0:T(8,128)(2,1)S(1)}, bf16[256,512]{1,0:T(8,128)(2,1)S(1)}) custom-call(s32[2]{0:T(128)S(1)} %get-tuple-element.113.at_ref, f32[4,256,512]{2,1,0:T(8,128)S(1)} %get-tuple-element.79.y_ref, bf16[4,256,128]{2,1,0:T(8,128)(2,1)S(1)} %get-tuple-element.80.c_ref, bf16[4,256,128]{2,1,0:T(8,128)(2,1)S(1)} %get-tuple-element.81.sc_ref, ...), custom_call_target="tpu_custom_call" | custom-call | tf_op jit(solution)/shard_map/pallas_call | solution.py:96
  171.7 4.0 %collective-permute-done.29.q2 = bf16[256,512]{1,0:T(8,128)(2,1)S(1)} collective-permute-done((bf16[256,512]{1,0:T(8,128)(2,1)S(1)}, bf16[256,512]{1,0:T(8,128)(2,1)S(1)}, u32[]{:S(2)}, u32[]{:S(2)}) %collective-permute-start.29) | collective-permute-done | bytes 262176 | tf_op jit(solution)/shard_map/ppermute | solution.py:56
  176.6 3.1 %shard_map.125 = bf16[256,2048]{1,0:T(8,128)(2,1)S(1)} custom-call(s32[4]{0:T(128)S(1)} %pad_add_fusion.at_ref, bf16[256,512]{1,0:T(8,128)(2,1)S(1)} %get-tuple-element.103.q0, bf16[256,512]{1,0:T(8,128)(2,1)S(1)} %collective-permute-done.28.q1, bf16[256,512]{1,0:T(8,128)(2,1)S(1)} %collective-permute-done.29.q2, ...), custom_call_target="tpu_custom_call" | custom-call | tf_op jit(solution)/shard_map/pallas_call | solution.py:96
  179.7 19.1 %collective-permute-start.31 = (bf16[256,2048]{1,0:T(8,128)(2,1)S(1)}, bf16[256,2048]{1,0:T(8,128)(2,1)S(1)}, u32[]{:S(2)}, u32[]{:S(2)}) collective-permute-start(bf16[256,2048]{1,0:T(8,128)(2,1)S(1)} %shard_map.125), channel_id=1, source_target_pairs={{0,128},{128,0},{1,129},{129,1},{2,130},{130,2},{3,131},{131,3},{4... | collective-permute-start | bytes 3145736 | tf_op jit(solution)/shard_map/ppermute | solution.py:546
  198.8 2.3 %collective-permute-done.31 = bf16[256,2048]{1,0:T(8,128)(2,1)S(1)} collective-permute-done((bf16[256,2048]{1,0:T(8,128)(2,1)S(1)}, bf16[256,2048]{1,0:T(8,128)(2,1)S(1)}, u32[]{:S(2)}, u32[]{:S(2)}) %collective-permute-start.31) | collective-permute-done | bytes 1048608 | tf_op jit(solution)/shard_map/ppermute | solution.py:546
  (200 shorter events, 42.2 us)
Async XLA Ops:
  0.0 68.0 %copy-start = (f32[1,256]{1,0:T(1,128)S(1)}, f32[1,256]{1,0:T(1,128)}, u32[]{:S(2)}) copy-start(f32[1,256]{1,0:T(1,128)} %param.19) | copy-start | bytes 3076
  1.0 11.2 %collective-permute-start = (bf16[16,1408]{1,0:T(8,128)(2,1)S(1)}, bf16[16,1408]{1,0:T(8,128)(2,1)S(1)}, u32[]{:S(2)}, u32[]{:S(2)}) collective-permute-start(bf16[16,1408]{1,0:T(8,128)(2,1)S(1)} %get-tuple-element.57), channel_id=1, source_target_pairs={{0,1},{1,2},{2,3},{3,0},{4,5},{5,6},{6,7},{7,4},{8,9},{9,10},{10,1... | collective-permute-start | bytes 135176 | tf_op jit(solution)/shard_map/ppermute | solution.py:56
  4.1 14.6 %collective-permute-start.4 = (bf16[16,2048]{1,0:T(8,128)(2,1)S(1)}, bf16[16,2048]{1,0:T(8,128)(2,1)S(1)}, u32[]{:S(2)}, u32[]{:S(2)}) collective-permute-start(bf16[16,2048]{1,0:T(8,128)(2,1)S(1)} %slice_bitcast_fusion), channel_id=1, source_target_pairs={{0,1},{1,2},{2,3},{3,4},{4,5},{5,6},{6,7},{7,8},{8,9},{9,10},{10,1... | collective-permute-start | bytes 196616 | tf_op jit(solution)/shard_map/ppermute | solution.py:56
  7.3 4.9 %collective-permute-start.1 = (bf16[16,1408]{1,0:T(8,128)(2,1)S(1)}, bf16[16,1408]{1,0:T(8,128)(2,1)S(1)}, u32[]{:S(2)}, u32[]{:S(2)}) collective-permute-start(bf16[16,1408]{1,0:T(8,128)(2,1)S(1)} %get-tuple-element.58), channel_id=1, source_target_pairs={{0,2},{1,3},{2,0},{3,1},{4,6},{5,7},{6,4},{7,5},{8,10},{9,11},{10,... | collective-permute-start | bytes 135176 | tf_op jit(solution)/shard_map/ppermute | solution.py:56
  8.7 3.9 %collective-permute-start.2 = (bf16[16,1408]{1,0:T(8,128)(2,1)S(1)}, bf16[16,1408]{1,0:T(8,128)(2,1)S(1)}, u32[]{:S(2)}, u32[]{:S(2)}) collective-permute-start(bf16[16,1408]{1,0:T(8,128)(2,1)S(1)} %get-tuple-element.59), channel_id=1, source_target_pairs={{0,3},{1,0},{2,1},{3,2},{4,7},{5,4},{6,5},{7,6},{8,11},{9,8},{10,9... | collective-permute-start | bytes 135176 | tf_op jit(solution)/shard_map/ppermute | solution.py:56
  13.3 11.8 %collective-permute-start.3 = (bf16[64,1408]{1,0:T(8,128)(2,1)}, bf16[64,1408]{1,0:T(8,128)(2,1)}, u32[]{:S(2)}, u32[]{:S(2)}) collective-permute-start(bf16[64,1408]{1,0:T(8,128)(2,1)} %shard_map.110.refs_0_), channel_id=1, source_target_pairs={{0,4},{1,5},{2,6},{3,7},{4,8},{5,9},{6,10},{7,11},{8,12},{9,13},{1... | collective-permute-start | bytes 540680 | tf_op jit(solution)/shard_map/ppermute | solution.py:56
  15.2 10.1 %collective-permute-start.7 = (bf16[64,1408]{1,0:T(8,128)(2,1)}, bf16[64,1408]{1,0:T(8,128)(2,1)}, u32[]{:S(2)}, u32[]{:S(2)}) collective-permute-start(bf16[64,1408]{1,0:T(8,128)(2,1)} %shard_map.110.refs_0_), channel_id=1, source_target_pairs={{0,28},{1,29},{2,30},{3,31},{4,0},{5,1},{6,2},{7,3},{8,4},{9,5},{1... | collective-permute-start | bytes 540680 | tf_op jit(solution)/shard_map/ppermute | solution.py:56
  20.6 10.6 %slice-start.2 = ((f32[1,4,2304]{2,1,0:T(4,128)}), f32[1,4,2048]{2,1,0:T(4,128)S(1)}, s32[]{:S(2)}) async-start(f32[1,4,2304]{2,1,0:T(4,128)} %param.14), calls=%async_computation.2 | async-start | bytes 65536 | tf_op jit(solution)/shard_map/slice | solution.py:502
  20.6 10.6 %slice-start.3 = ((f32[1,2304]{1,0:T(1,128)}), f32[1,2048]{1,0:T(1,128)S(1)}, s32[]{:S(2)}) async-start(f32[1,2304]{1,0:T(1,128)} %param.15), calls=%async_computation.3 | async-start | bytes 16384 | tf_op jit(solution)/shard_map/slice | solution.py:505
  22.3 26.1 %collective-permute-start.5 = (bf16[272,2048]{1,0:T(8,128)(2,1)S(1)}, bf16[272,2048]{1,0:T(8,128)(2,1)S(1)}, u32[]{:S(2)}, u32[]{:S(2)}) collective-permute-start(bf16[272,2048]{1,0:T(8,128)(2,1)S(1)} %shard_map.111.own_ref), channel_id=1, source_target_pairs={{0,1},{1,2},{2,3},{3,0},{4,5},{5,6},{6,7},{7,4},{8,9},{9,10},{10,1... | collective-permute-start | bytes 3342344 | tf_op jit(solution)/shard_map/ppermute | solution.py:56
  22.8 26.5 %collective-permute-start.6 = (bf16[272,2048]{1,0:T(8,128)(2,1)S(1)}, bf16[272,2048]{1,0:T(8,128)(2,1)}, u32[]{:S(2)}, u32[]{:S(2)}) collective-permute-start(bf16[272,2048]{1,0:T(8,128)(2,1)S(1)} %shard_map.111.own_ref), channel_id=1, source_target_pairs={{0,3},{1,0},{2,1},{3,2},{4,7},{5,4},{6,5},{7,6},{8,11},{9,8},{10,9... | collective-permute-start | bytes 3342344 | tf_op jit(solution)/shard_map/ppermute | solution.py:56
  25.1 6.1 %collective-permute-start.12 = (bf16[64,1408]{1,0:T(8,128)(2,1)}, bf16[64,1408]{1,0:T(8,128)(2,1)S(1)}, u32[]{:S(2)}, u32[]{:S(2)}) collective-permute-start(bf16[64,1408]{1,0:T(8,128)(2,1)} %collective-permute-done.3.refs_7_), channel_id=1, source_target_pairs={{0,4},{1,5},{2,6},{3,7},{4,8},{5,9},{6,10},{7,11},{8,12},{9,13},{1... | collective-permute-start | bytes 540680 | tf_op jit(solution)/shard_map/ppermute | solution.py:56
  25.3 6.0 %collective-permute-start.8 = (bf16[64,1408]{1,0:T(8,128)(2,1)}, bf16[64,1408]{1,0:T(8,128)(2,1)S(1)}, u32[]{:S(2)}, u32[]{:S(2)}) collective-permute-start(bf16[64,1408]{1,0:T(8,128)(2,1)} %collective-permute-done.7.refs_1_), channel_id=1, source_target_pairs={{0,28},{1,29},{2,30},{3,31},{4,0},{5,1},{6,2},{7,3},{8,4},{9,5},{1... | collective-permute-start | bytes 540680 | tf_op jit(solution)/shard_map/ppermute | solution.py:56
  31.3 5.9 %collective-permute-start.13 = (bf16[64,1408]{1,0:T(8,128)(2,1)S(1)}, bf16[64,1408]{1,0:T(8,128)(2,1)S(1)}, u32[]{:S(2)}, u32[]{:S(2)}) collective-permute-start(bf16[64,1408]{1,0:T(8,128)(2,1)S(1)} %collective-permute-done.12.refs_6_), channel_id=1, source_target_pairs={{0,4},{1,5},{2,6},{3,7},{4,8},{5,9},{6,10},{7,11},{8,12},{9,13},{1... | collective-permute-start | bytes 540680 | tf_op jit(solution)/shard_map/ppermute | solution.py:56
  31.3 5.8 %collective-permute-start.9 = (bf16[64,1408]{1,0:T(8,128)(2,1)S(1)}, bf16[64,1408]{1,0:T(8,128)(2,1)S(1)}, u32[]{:S(2)}, u32[]{:S(2)}) collective-permute-start(bf16[64,1408]{1,0:T(8,128)(2,1)S(1)} %collective-permute-done.8.refs_2_), channel_id=1, source_target_pairs={{0,28},{1,29},{2,30},{3,31},{4,0},{5,1},{6,2},{7,3},{8,4},{9,5},{1... | collective-permute-start | bytes 540680 | tf_op jit(solution)/shard_map/ppermute | solution.py:56
  37.1 6.4 %collective-permute-start.14 = (bf16[64,1408]{1,0:T(8,128)(2,1)S(1)}, bf16[64,1408]{1,0:T(8,128)(2,1)S(1)}, u32[]{:S(2)}, u32[]{:S(2)}) collective-permute-start(bf16[64,1408]{1,0:T(8,128)(2,1)S(1)} %collective-permute-done.13.refs_5_), channel_id=1, source_target_pairs={{0,4},{1,5},{2,6},{3,7},{4,8},{5,9},{6,10},{7,11},{8,12},{9,13},{1... | collective-permute-start | bytes 540680 | tf_op jit(solution)/shard_map/ppermute | solution.py:56
  45.6 14.6 %collective-permute-start.15 = (bf16[512,768]{1,0:T(8,128)(2,1)S(1)}, bf16[512,768]{1,0:T(8,128)(2,1)S(1)}, u32[]{:S(2)}, u32[]{:S(2)}) collective-permute-start(bf16[512,768]{1,0:T(8,128)(2,1)S(1)} %get-tuple-element.66.own_ref), channel_id=1, source_target_pairs={{0,32},{1,33},{2,34},{3,35},{4,36},{5,37},{6,38},{7,39},{8,40},{9,... | collective-permute-start | bytes 2359304 | tf_op jit(solution)/shard_map/ppermute | solution.py:56
  46.8 15.1 %collective-permute-start.17 = (bf16[512,768]{1,0:T(8,128)(2,1)S(1)}, bf16[512,768]{1,0:T(8,128)(2,1)S(1)}, u32[]{:S(2)}, u32[]{:S(2)}) collective-permute-start(bf16[512,768]{1,0:T(8,128)(2,1)S(1)} %get-tuple-element.66.own_ref), channel_id=1, source_target_pairs={{0,96},{1,97},{2,98},{3,99},{4,100},{5,101},{6,102},{7,103},{8,104... | collective-permute-start | bytes 2359304 | tf_op jit(solution)/shard_map/ppermute | solution.py:56
  49.2 16.9 %copy-start.59 = (f32[1,32]{1,0:T(1,128)S(1)}, f32[1,32]{1,0:T(1,128)}, u32[]{:S(2)}) copy-start(f32[1,32]{1,0:T(1,128)} %param.17) | copy-start | bytes 388
  49.2 16.9 %copy-start.60 = (f32[1,32]{1,0:T(1,128)S(1)}, f32[1,32]{1,0:T(1,128)}, u32[]{:S(2)}) copy-start(f32[1,32]{1,0:T(1,128)} %param.16) | copy-start | bytes 388
  51.2 23.8 %collective-permute-start.10 = (bf16[144,2048]{1,0:T(8,128)(2,1)}, bf16[144,2048]{1,0:T(8,128)(2,1)}, u32[]{:S(2)}, u32[]{:S(2)}) collective-permute-start(bf16[144,2048]{1,0:T(8,128)(2,1)} %slice.52), channel_id=1, source_target_pairs={{0,1},{1,2},{2,3},{3,0},{4,5},{5,6},{6,7},{7,4},{8,9},{9,10},{10,1... | collective-permute-start | bytes 1769480 | tf_op jit(solution)/shard_map/ppermute | solution.py:56
  61.8 8.5 %collective-permute-start.16 = (bf16[256,768]{1,0:T(8,128)(2,1)}, bf16[256,768]{1,0:T(8,128)(2,1)}, u32[]{:S(2)}, u32[]{:S(2)}) collective-permute-start(bf16[256,768]{1,0:T(8,128)(2,1)} %slice.54), channel_id=1, source_target_pairs={{0,32},{1,33},{2,34},{3,35},{4,36},{5,37},{6,38},{7,39},{8,40},{9,... | collective-permute-start | bytes 1179656 | tf_op jit(solution)/shard_map/ppermute | solution.py:56
  63.5 7.7 %collective-permute-start.18 = (bf16[256,768]{1,0:T(8,128)(2,1)}, bf16[256,768]{1,0:T(8,128)(2,1)}, u32[]{:S(2)}, u32[]{:S(2)}) collective-permute-start(bf16[256,768]{1,0:T(8,128)(2,1)} %slice.55), channel_id=1, source_target_pairs={{0,96},{1,97},{2,98},{3,99},{4,100},{5,101},{6,102},{7,103},{8,104... | collective-permute-start | bytes 1179656 | tf_op jit(solution)/shard_map/ppermute | solution.py:56
  66.2 8.7 %collective-permute-start.11 = (bf16[128,2048]{1,0:T(8,128)(2,1)}, bf16[128,2048]{1,0:T(8,128)(2,1)S(1)}, u32[]{:S(2)}, u32[]{:S(2)}) collective-permute-start(bf16[128,2048]{1,0:T(8,128)(2,1)} %slice.53), channel_id=1, source_target_pairs={{0,3},{1,0},{2,1},{3,2},{4,7},{5,4},{6,5},{7,6},{8,11},{9,8},{10,9... | collective-permute-start | bytes 1572872 | tf_op jit(solution)/shard_map/ppermute | solution.py:56
  71.2 57.0 %collective-permute-start.19 = (bf16[512,640]{1,0:T(8,128)(2,1)}, bf16[512,640]{1,0:T(8,128)(2,1)}, u32[]{:S(2)}, u32[]{:S(2)}) collective-permute-start(bf16[512,640]{1,0:T(8,128)(2,1)} %copy-done.12), channel_id=1, source_target_pairs={{0,32},{1,33},{2,34},{3,35},{4,36},{5,37},{6,38},{7,39},{8,40},{9,... | collective-permute-start | bytes 1966088 | tf_op jit(solution)/shard_map/ppermute | solution.py:56
  71.6 59.8 %collective-permute-start.20 = (bf16[512,640]{1,0:T(8,128)(2,1)}, bf16[512,640]{1,0:T(8,128)(2,1)}, u32[]{:S(2)}, u32[]{:S(2)}) collective-permute-start(bf16[512,640]{1,0:T(8,128)(2,1)} %copy-done.12), channel_id=1, source_target_pairs={{0,96},{1,97},{2,98},{3,99},{4,100},{5,101},{6,102},{7,103},{8,104... | collective-permute-start | bytes 1966088 | tf_op jit(solution)/shard_map/ppermute | solution.py:56
  95.0 4.3 %collective-permute-start.23 = (bf16[144,512]{1,0:T(8,128)(2,1)}, bf16[144,512]{1,0:T(8,128)(2,1)}, u32[]{:S(2)}, u32[]{:S(2)}) collective-permute-start(bf16[144,512]{1,0:T(8,128)(2,1)} %get-tuple-element.83), channel_id=1, source_target_pairs={{0,4},{1,5},{2,6},{3,7},{4,0},{5,1},{6,2},{7,3},{8,12},{9,13},{10,... | collective-permute-start | bytes 442376 | tf_op jit(solution)/shard_map/ppermute | solution.py:56
  104.5 6.5 %collective-permute-start.24 = (bf16[144,512]{1,0:T(8,128)(2,1)}, bf16[144,512]{1,0:T(8,128)(2,1)}, u32[]{:S(2)}, u32[]{:S(2)}) collective-permute-start(bf16[144,512]{1,0:T(8,128)(2,1)} %get-tuple-element.87), channel_id=1, source_target_pairs={{0,8},{1,9},{2,10},{3,11},{4,12},{5,13},{6,14},{7,15},{8,0},{9,1},... | collective-permute-start | bytes 442376 | tf_op jit(solution)/shard_map/ppermute | solution.py:56
  116.3 6.7 %collective-permute-start.25 = (bf16[144,512]{1,0:T(8,128)(2,1)}, bf16[144,512]{1,0:T(8,128)(2,1)}, u32[]{:S(2)}, u32[]{:S(2)}) collective-permute-start(bf16[144,512]{1,0:T(8,128)(2,1)} %get-tuple-element.91), channel_id=1, source_target_pairs={{0,28},{1,29},{2,30},{3,31},{4,24},{5,25},{6,26},{7,27},{8,20},{9,... | collective-permute-start | bytes 442376 | tf_op jit(solution)/shard_map/ppermute | solution.py:56
  128.2 6.1 %collective-permute-start.26 = (bf16[144,512]{1,0:T(8,128)(2,1)}, bf16[144,512]{1,0:T(8,128)(2,1)}, u32[]{:S(2)}, u32[]{:S(2)}) collective-permute-start(bf16[144,512]{1,0:T(8,128)(2,1)} %get-tuple-element.95), channel_id=1, source_target_pairs={{0,32},{1,33},{2,34},{3,35},{4,36},{5,37},{6,38},{7,39},{8,40},{9,... | collective-permute-start | bytes 442376 | tf_op jit(solution)/shard_map/ppermute | solution.py:56
  129.9 21.8 %collective-permute-start.21 = (bf16[256,640]{1,0:T(8,128)(2,1)}, bf16[256,640]{1,0:T(8,128)(2,1)}, u32[]{:S(2)}, u32[]{:S(2)}) collective-permute-start(bf16[256,640]{1,0:T(8,128)(2,1)} %slice.56), channel_id=1, source_target_pairs={{0,32},{1,33},{2,34},{3,35},{4,36},{5,37},{6,38},{7,39},{8,40},{9,... | collective-permute-start | bytes 983048 | tf_op jit(solution)/shard_map/ppermute | solution.py:56
  133.1 18.6 %collective-permute-start.22 = (bf16[256,640]{1,0:T(8,128)(2,1)}, bf16[256,640]{1,0:T(8,128)(2,1)}, u32[]{:S(2)}, u32[]{:S(2)}) collective-permute-start(bf16[256,640]{1,0:T(8,128)(2,1)} %slice.57), channel_id=1, source_target_pairs={{0,96},{1,97},{2,98},{3,99},{4,100},{5,101},{6,102},{7,103},{8,104... | collective-permute-start | bytes 983048 | tf_op jit(solution)/shard_map/ppermute | solution.py:56
  139.6 10.4 %collective-permute-start.27 = (bf16[144,512]{1,0:T(8,128)(2,1)}, bf16[144,512]{1,0:T(8,128)(2,1)}, u32[]{:S(2)}, u32[]{:S(2)}) collective-permute-start(bf16[144,512]{1,0:T(8,128)(2,1)} %get-tuple-element.99), channel_id=1, source_target_pairs={{0,96},{1,97},{2,98},{3,99},{4,100},{5,101},{6,102},{7,103},{8,104... | collective-permute-start | bytes 442376 | tf_op jit(solution)/shard_map/ppermute | solution.py:56
  145.1 6.6 %copy-start.19 = (f32[4,256,128]{2,1,0:T(8,128)S(1)}, f32[4,256,128]{2,1,0:T(8,128)}, u32[]{:S(2)}) copy-start(f32[4,256,128]{2,1,0:T(8,128)} %copy-done.18) | copy-start | bytes 1572868
  145.2 6.6 %copy-start.21 = (bf16[4,128,512]{2,1,0:T(8,128)(2,1)S(1)}, bf16[4,128,512]{2,1,0:T(8,128)(2,1)}, u32[]{:S(2)}) copy-start(bf16[4,128,512]{2,1,0:T(8,128)(2,1)} %copy-done.20) | copy-start | bytes 1572868
  145.2 6.6 %copy-start.31 = (bf16[4,256,128]{2,1,0:T(8,128)(2,1)S(1)}, bf16[4,256,128]{2,1,0:T(8,128)(2,1)}, u32[]{:S(2)}) copy-start(bf16[4,256,128]{2,1,0:T(8,128)(2,1)} %copy-done.30) | copy-start | bytes 786436
  145.2 31.4 %slice-start = ((s8[8388608]{0:T(1024)(128)(4,1)}), s8[4194304]{0:T(1024)(128)(4,1)S(1)}, s32[]{:S(2)}) async-start(s8[8388608]{0:T(1024)(128)(4,1)} %bitcast.36), calls=%async_computation | async-start | bytes 8388608
  154.0 8.8 %copy-start.23 = (bf16[128,512]{1,0:T(8,128)(2,1)S(1)}, bf16[128,512]{1,0:T(8,128)(2,1)}, u32[]{:S(2)}) copy-start(bf16[128,512]{1,0:T(8,128)(2,1)} %copy-done.22) | copy-start | bytes 393220
  154.0 8.8 %copy-start.25 = (bf16[128,512]{1,0:T(8,128)(2,1)S(1)}, bf16[128,512]{1,0:T(8,128)(2,1)}, u32[]{:S(2)}) copy-start(bf16[128,512]{1,0:T(8,128)(2,1)} %copy-done.24) | copy-start | bytes 393220
  154.0 8.8 %copy-start.27 = (bf16[128,512]{1,0:T(8,128)(2,1)S(1)}, bf16[128,512]{1,0:T(8,128)(2,1)}, u32[]{:S(2)}) copy-start(bf16[128,512]{1,0:T(8,128)(2,1)} %copy-done.26) | copy-start | bytes 393220
  154.1 8.8 %copy-start.29 = (bf16[128,512]{1,0:T(8,128)(2,1)S(1)}, bf16[128,512]{1,0:T(8,128)(2,1)}, u32[]{:S(2)}) copy-start(bf16[128,512]{1,0:T(8,128)(2,1)} %copy-done.28) | copy-start | bytes 393220
  154.1 22.5 %slice-start.1 = ((s8[8388608]{0:T(1024)(128)(4,1)}), s8[4194304]{0:T(1024)(128)(4,1)S(1)}, s32[]{:S(2)}) async-start(s8[8388608]{0:T(1024)(128)(4,1)} %bitcast.36), calls=%async_computation.1 | async-start | bytes 8388608
  165.1 6.6 %collective-permute-start.28 = (bf16[256,512]{1,0:T(8,128)(2,1)S(1)}, bf16[256,512]{1,0:T(8,128)(2,1)S(1)}, u32[]{:S(2)}, u32[]{:S(2)}) collective-permute-start(bf16[256,512]{1,0:T(8,128)(2,1)S(1)} %get-tuple-element.104), channel_id=1, source_target_pairs={{0,1},{1,2},{2,3},{3,0},{4,5},{5,6},{6,7},{7,4},{8,9},{9,10},{10,1... | collective-permute-start | bytes 786440 | tf_op jit(solution)/shard_map/ppermute | solution.py:56
  165.2 10.5 %collective-permute-start.29 = (bf16[256,512]{1,0:T(8,128)(2,1)S(1)}, bf16[256,512]{1,0:T(8,128)(2,1)S(1)}, u32[]{:S(2)}, u32[]{:S(2)}) collective-permute-start(bf16[256,512]{1,0:T(8,128)(2,1)S(1)} %get-tuple-element.105), channel_id=1, source_target_pairs={{0,2},{1,3},{2,0},{3,1},{4,6},{5,7},{6,4},{7,5},{8,10},{9,11},{10,... | collective-permute-start | bytes 786440 | tf_op jit(solution)/shard_map/ppermute | solution.py:56
  169.1 7.5 %copy-start.5 = (bf16[1,256,2048]{2,1,0:T(8,128)(2,1)S(1)}, bf16[1,256,2048]{2,1,0:T(8,128)(2,1)}, u32[]{:S(2)}) copy-start(bf16[1,256,2048]{2,1,0:T(8,128)(2,1)} %param.11) | copy-start | bytes 3145732
  169.1 7.5 %copy-start.58 = (f32[1,2048]{1,0:T(1,128)S(1)}, f32[1,2048]{1,0:T(1,128)}, u32[]{:S(2)}) copy-start(f32[1,2048]{1,0:T(1,128)} %gain_ref.3) | copy-start | bytes 24580
  171.3 5.3 %collective-permute-start.30 = (bf16[256,512]{1,0:T(8,128)(2,1)S(1)}, bf16[256,512]{1,0:T(8,128)(2,1)S(1)}, u32[]{:S(2)}, u32[]{:S(2)}) collective-permute-start(bf16[256,512]{1,0:T(8,128)(2,1)S(1)} %get-tuple-element.106), channel_id=1, source_target_pairs={{0,3},{1,0},{2,1},{3,2},{4,7},{5,4},{6,5},{7,6},{8,11},{9,8},{10,9... | collective-permute-start | bytes 786440 | tf_op jit(solution)/shard_map/ppermute | solution.py:56
  179.7 21.3 %collective-permute-start.31 = (bf16[256,2048]{1,0:T(8,128)(2,1)S(1)}, bf16[256,2048]{1,0:T(8,128)(2,1)S(1)}, u32[]{:S(2)}, u32[]{:S(2)}) collective-permute-start(bf16[256,2048]{1,0:T(8,128)(2,1)S(1)} %shard_map.125), channel_id=1, source_target_pairs={{0,128},{128,0},{1,129},{129,1},{2,130},{130,2},{3,131},{131,3},{4... | collective-permute-start | bytes 3145736 | tf_op jit(solution)/shard_map/ppermute | solution.py:546
  (49 other events, 84.2 us)
where the time goes:
time: 203 us; the launch traced here: 202 us
  starting transfers between devices  60 us (30%)
  waiting for transfers between devices  49.2 us (24%)
  Pallas kernels  46.3 us (23%)
  local copies, waits for them, and re-layouts  45.5 us (22%)
    ppermute x31, waiting for transfers between devices, sent(): return lax.ppermute(value, 'seq', pairs)  46.9 us
    pallas_call x17, Pallas kernels, run(): pl.pallas_call(kernel, in_specs=[smem] * len(scalars) + [vmem] * len(arra...  46.3 us
    ppermute x31, starting transfers between devices, sent(): return lax.ppermute(value, 'seq', pairs)  40.9 us
    unnamed x127, local copies, waits for them, and re-layouts  33.1 us
    ppermute x1, starting transfers between devices, layer(): return lax.ppermute(result, 'section', [(0, 1), (1, 0)])[None]  19.1 us
  transfers between devices with their start and end apart: 32, of which 15 were waited for; matrix products, arithmetic and copies ran while one was open for 6% of the time, Pallas kernels for 16%

commit v1 on v0

--- a/solution.py
+++ b/solution.py
@@ -1,3 +1,5 @@
+import functools
+
 import jax
 import jax.numpy as jnp
 from jax import lax
@@ -53,7 +55,7 @@
 
 
 def sent(value, pairs):
-    return lax.ppermute(value, "seq", pairs)
+    return lax.ppermute(getattr(value, "value", value), "seq", pairs)
 
 
 def spread(first, stride):
@@ -86,21 +88,41 @@
     return pltpu.VMEM(shape, dtype)
 
 
+class Kept:
+    def __init__(self, value, out):
+        self.value = self.loose = value
+        if out.memory_space == pltpu.HBM:
+            self.value = far(value)
+        self.shape = value.shape
+        self.dtype = value.dtype
+
+
+def plain(dtype, *shape):
+    return pltpu.HBM(shape, dtype)
+
+
 def near(value):
     return pltpu.with_memory_space_constraint(value, pltpu.VMEM)
 
 
-def run(kernel, scalars, arrays, outs, scratch=()):
+def far(value):
+    return pltpu.with_memory_space_constraint(value, pltpu.HBM)
+
+
+def run(kernel, scalars, arrays, outs, scratch=(), place=near, loose=False):
     smem = pl.BlockSpec(memory_space=pltpu.SMEM)
     vmem = pl.BlockSpec(memory_space=pltpu.VMEM)
-    return pl.pallas_call(
+    kept = lambda v: v.loose if loose else v.value
+    arrays = [kept(v) if isinstance(v, Kept) else place(v) for v in arrays]
+    results = pl.pallas_call(
         kernel,
         in_specs=[smem] * len(scalars) + [vmem] * len(arrays),
         out_specs=[vmem] * len(outs),
         out_shape=outs,
         scratch_shapes=list(scratch),
         compiler_params=pltpu.CompilerParams(vmem_limit_bytes=10 << 20),
-    )(*scalars, *map(near, arrays))
+    )(*scalars, *arrays)
+    return [Kept(v, out) for v, out in zip(results, outs, strict=True)]
 
 
 def each_block(body):
@@ -123,32 +145,34 @@
     each_block(block)
 
 
-def run_part(rows, own, below, above):
-    width = own.shape[1]
-    return run(part_kernel, (), (rows, own, below, above), [shape_of(F32, NY, EXT, width)])[0]
-
-
-def stack_kernel(y_ref, own_ref, below_ref, above_ref, lo_ref, hi_ref, out_ref):
+def run_part(rows, own, below, above, where):
+    out = where(F32, NY, EXT, own.shape[1])
+    return run(part_kernel, (), (rows, own, below, above), [out])[0]
+
+
+def stack_kernel(y_ref, own_ref, below_ref, above_ref, lo_ref, hi_ref, near_ref, far_ref):
     y = y_ref[0]
-    out_ref[y] = own_ref[...]
-    out_ref[(y + 3) % NY] = below_ref[...]
-    out_ref[(y + 1) % NY] = above_ref[...]
-    out_ref[(y + 2) % NY, 0:SPLIT, :] = lo_ref[...]
-    out_ref[(y + 2) % NY, SPLIT:, :] = hi_ref[...]
+    edge = 3 * KX
+    for out_ref, a, b in ((near_ref, 0, edge), (far_ref, edge, edge + KX)):
+        out_ref[y] = own_ref[:, a:b]
+        out_ref[(y + 3) % NY] = below_ref[:, a:b]
+        out_ref[(y + 1) % NY] = above_ref[:, a:b]
+        out_ref[(y + 2) % NY, 0:SPLIT, :] = lo_ref[:, a:b]
+        out_ref[(y + 2) % NY, SPLIT:, :] = hi_ref[:, a:b]
 
 
 def finished(part_ref, rows_ref, fa_ref, fb_ref, j):
     total = (
         part_ref[j]
-        + jnp.dot(rows_ref[j, :, 3 * KX : 3 * KX + KX // 2], fa_ref[...], preferred_element_type=F32)
-        + jnp.dot(rows_ref[j, :, 3 * KX + KX // 2 :], fb_ref[...], preferred_element_type=F32)
+        + jnp.dot(rows_ref[j, :, : KX // 2], fa_ref[...], preferred_element_type=F32)
+        + jnp.dot(rows_ref[j, :, KX // 2 :], fb_ref[...], preferred_element_type=F32)
     )
     return total.astype(BF).astype(F32)
 
 
 def state_kernel(
     part_ref, rows_ref, fa_ref, fb_ref, taps_ref, bias_ref, small_bias_ref, rate_ref, spread_ref,
-    xs_ref, b_ref, sp_ref, cum_ref, e2_ref, sc_ref, row_ref, s_ref, pair_ref, state_ref, logs_ref, msg_ref,
+    xs_ref, b_ref, sp_ref, cum_ref, e2_ref, sc_ref, row_ref, s_ref, pair_ref, logs_ref, msg_ref,
     wide_ref, acc_ref, carry_ref,
 ):
     acc_ref[...] = jnp.zeros_like(acc_ref)
@@ -207,7 +231,6 @@
 
         @pl.when(j == NY - 1)
         def _():
-            state_ref[...] = acc
             pack_message(msg_ref, acc, logs_ref[0:1, :])
 
     each_block(block)
@@ -227,10 +250,10 @@
         (),
         (part, rows, far_a, far_b, taps, bias, small_bias, rate, spreads),
         [
-            shape_of(F32, NY, ROWS, XW), shape_of(BF, NY, ROWS, NS), shape_of(F32, NY, ROWS, 128),
-            shape_of(F32, NY, ROWS, 128), shape_of(F32, NY, ROWS, 128), shape_of(BF, NY, ROWS, 128),
-            shape_of(F32, NY, HEADS, ROWS), shape_of(BF, NY, NS, XW),
-            shape_of(BF, NS, XW), shape_of(F32, NS, XW), shape_of(F32, 8, XW), shape_of(BF, NS + 16, XW),
+            plain(F32, NY, ROWS, XW), plain(BF, NY, ROWS, NS), plain(F32, NY, ROWS, 128),
+            plain(F32, NY, ROWS, 128), plain(F32, NY, ROWS, 128), plain(BF, NY, ROWS, 128),
+            plain(F32, NY, HEADS, ROWS), plain(BF, NY, NS, XW),
+            plain(BF, NS, XW), shape_of(F32, 16, XW), shape_of(BF, NS + 16, XW),
         ],
         [
             pltpu.VMEM((EXT, XW + NS), F32),
@@ -286,84 +309,108 @@
         intra_kernel,
         (),
         (part, rows, far_a, far_b, taps, bias, skip, xs, b_mat, sp, cum, e2, row, states, pair, spreads),
-        [shape_of(F32, NY, ROWS, XW), shape_of(BF, NY, ROWS, NS), shape_of(BF, NY, ROWS, XW)],
+        [plain(F32, NY, ROWS, XW), plain(BF, NY, ROWS, NS), plain(BF, NY, ROWS, XW)],
         [pltpu.VMEM((EXT, NS), F32)],
-    )
-
-
-def merge_kernel(bit_ref, got_ref, state_ref, logs_ref, msg_ref, new_ref, new_logs_ref, bucket_ref):
-    upper = bit_ref[0] == 1
+        place=lambda v: v,
+        loose=True,
+    )
+
+
+def merge_kernel(mask_ref, got_ref, own_ref, logs_ref, msg_ref, new_logs_ref, *, k):
+    upper = mask_ref[k : k + 1, :] == 1
     other = got_ref[0:NS, :].astype(F32)
     tail = got_ref[NS:, :].astype(F32)
     other_log = tail[0:1, :] + tail[1:2, :]
     log = logs_ref[0:1, :]
     before = logs_ref[1:2, :]
-    bucket = jnp.where(upper, jnp.exp(before), 0.0) * other
-    bucket_ref[...] = bucket.astype(BF)
     state = (
         jnp.where(upper, jnp.exp(log), 1.0) * other
-        + jnp.where(upper, 1.0, jnp.exp(other_log)) * state_ref[...]
-    )
-    new_ref[...] = state
+        + jnp.where(upper, 1.0, jnp.exp(other_log)) * own_ref[0:NS, :].astype(F32)
+    )
     log = log + other_log
-    new_logs_ref[...] = jnp.zeros_like(new_logs_ref)
+    new_logs_ref[...] = logs_ref[...]
     new_logs_ref[0:1, :] = log
     new_logs_ref[1:2, :] = jnp.where(upper, before + other_log, before)
+    new_logs_ref[8 + k : 9 + k, :] = jnp.where(upper, jnp.exp(before), 0.0)
     pack_message(msg_ref, state, log)
 
 
-def run_merge(bit, got, state, logs):
+def run_merge(k, masks, got, own, logs):
     return run(
-        merge_kernel,
-        (bit.reshape(1),),
-        (got, state, logs),
-        [shape_of(BF, NS + 16, XW), shape_of(F32, NS, XW), shape_of(F32, 8, XW), shape_of(BF, NS, XW)],
-    )
-
-
-def cross_kernel(at_ref, y_ref, c_ref, sc_ref, z_ref, k3, k4, k5, k6, k7, spread_ref, *q_refs):
-    for k, q_ref in enumerate(q_refs):
+        functools.partial(merge_kernel, k=k),
+        (),
+        (masks, got, own, logs),
+        [shape_of(BF, NS + 16, XW), shape_of(F32, 16, XW)],
+    )
+
+
+def cross_kernel(
+    at_ref, y_ref, c_ref, sc_ref, z_ref, g3, g4, g5, g6, g7, logs_ref, spread_ref,
+    q0, q1, q2, q3, bucket_ref,
+):
+    for k, got in enumerate((g3, g4, g5, g6, g7)):
+        scaled = got[0:NS, :].astype(F32) * logs_ref[8 + k : 9 + k, :]
+        bucket_ref[k] = scaled.astype(BF)
+    for k, q_ref in enumerate((q0, q1, q2, q3)):
         j = at_ref[k]
         c_mat = c_ref[j]
         scale = sc_ref[j]
         y = y_ref[j]
-        for level, bucket in ((3, k3), (4, k4), (5, k5), (6, k6), (7, k7)):
-            y = y + mm(c_mat, bucket[...]) * mm(scale, spread_ref[level])
+        for level in range(3, 8):
+            y = y + mm(c_mat, bucket_ref[level - 3]) * mm(scale, spread_ref[level])
         q_ref[...] = (y * silu(z_ref[j].astype(F32))).astype(BF)
 
 
-def run_cross(at, y, c_mat, sc, z, buckets, spreads):
+def run_cross(at, y, c_mat, sc, z, gots, logs, spreads):
     return run(
         cross_kernel,
-        (jnp.stack(at),),
-        (y, c_mat, sc, z, *buckets, spreads),
-        [shape_of(BF, ROWS, XW)] * len(at),
-    )
-
-
-def out_kernel(at_ref, q0, q1, q2, q3, gain_ref, w_ref, acts_ref, out_ref, acc_ref):
+        (at,),
+        (y, c_mat, sc, z, *gots, logs, spreads),
+        [shape_of(BF, ROWS, XW)] * NY,
+        [pltpu.VMEM((5, NS, XW), BF)],
+        place=lambda v: v,
+    )
+
+
+def out_kernel(at_ref, q0, q1, q2, q3, gain_ref, acts_ref, w_ref, out_ref, acc_ref, w_vmem, sems):
     blocks = (q0, q1, q2, q3)
+    rows = [pl.ds(pl.multiple_of(at_ref[k] * XW, XW), XW) for k in range(NY)]
+    copies = [
+        pltpu.make_async_copy(w_ref.at[rows[k], :], w_vmem.at[k], sems.at[k]) for k in range(NY)
+    ]
+    for copy in copies:
+        copy.start()
     square = sum(
         jnp.sum(jnp.square(q[...].astype(F32)), axis=1, keepdims=True) for q in blocks
     )
     scale = lax.rsqrt(square / (NY * XW) + EPS)
     acc_ref[...] = acts_ref[...].astype(F32)
     for k, q in enumerate(blocks):
-        there = pl.ds(pl.multiple_of(at_ref[k] * XW, XW), XW)
-        n = q[...].astype(F32) * scale * gain_ref[0:1, there]
-        acc_ref[...] += jnp.dot(n.astype(BF), w_ref[there, :], preferred_element_type=F32)
+        n = q[...].astype(F32) * scale * gain_ref[0:1, rows[k]]
+        copies[k].wait()
+        acc_ref[...] += jnp.dot(n.astype(BF), w_vmem[k], preferred_element_type=F32)
     out_ref[...] = acc_ref[...].astype(BF)
 
 
 def run_out(at, blocks, gain, weight, acts):
     width = weight.shape[1]
-    return run(
+    vmem = pl.BlockSpec(memory_space=pltpu.VMEM)
+    blocks = [v.value if isinstance(v, Kept) else near(v) for v in blocks]
+    return pl.pallas_call(
         out_kernel,
-        (at,),
-        (*blocks, gain, weight, acts),
-        [shape_of(BF, ROWS, width)],
-        [pltpu.VMEM((ROWS, width), F32)],
-    )[0]
+        in_specs=[pl.BlockSpec(memory_space=pltpu.SMEM)]
+        + [vmem] * 6
+        + [pl.BlockSpec(memory_space=pltpu.HBM)],
+        out_specs=vmem,
+        out_shape=shape_of(BF, ROWS, width),
+        scratch_shapes=[
+            pltpu.VMEM((ROWS, width), F32),
+            pltpu.VMEM((NY, XW, width), BF),
+            pltpu.SemaphoreType.DMA((NY,)),
+        ],
+        compiler_params=pltpu.CompilerParams(vmem_limit_bytes=28 << 20),
+        name="gate_out",
+    )(at, *blocks, gain, acts, far(weight))
 
 
 def norm_kernel(at_ref, halo_ref, acts_ref, gain_ref, out_ref, full_ref):
@@ -385,6 +432,7 @@
         (halo, acts, gain),
         [shape_of(BF, EXT, width)],
         [pltpu.VMEM((EXT, width), F32)],
+        place=lambda v: v,
     )[0]
 
 
@@ -417,6 +465,7 @@
         (shard,),
         [shape_of(BF, rows, WA + WB)] * 4,
         [pltpu.VMEM((NY, rows, WA + WB), BF)],
+        place=lambda v: v,
     )
 
 
@@ -453,11 +502,27 @@
     return down + [up[4], up[3], up[2], up[1]]
 
 
-def ring_four(block, up, down):
-    below = sent(block, up)
-    above = sent(block, down)
-    half = block.shape[0] // 2
-    return below, above, lambda: (sent(below[:half], up), sent(above[half:], down))
+def half_kernel(block_ref, out_ref, *, start):
+    out_ref[...] = block_ref[start : start + out_ref.shape[0], :]
+
+
+def rows_from(block, start, count):
+    kernel = functools.partial(half_kernel, start=start)
+    return run(kernel, (), (block,), [shape_of(BF, count, block.shape[1])])[0]
+
+
+def near_pair(block, up, down):
+    return sent(block, up), sent(block, down)
+
+
+def far_pair(below, above, up, down, split):
+    rest = above.shape[0] - split
+    return sent(rows_from(below, 0, split), up), sent(rows_from(above, split, rest), down)
+
+
+def mask_kernel(bits_ref, out_ref):
+    for k in range(8):
+        out_ref[k : k + 1, :] = jnp.full((1, XW), bits_ref[k], jnp.int32)
 
 
 def layer(
@@ -478,23 +543,21 @@
     z = (index // NY) % NZ
     x = index // (NY * NZ)
     w0, w1, w2, w3 = run_columns(y, in_proj[0])
-    columns = run_join(y, (w0, sent(w1, Y_UP), sent(w2, Y_TWO), sent(w3, Y_DOWN)))
-    tail, _ = together(acts[0, ROWS - HALO :], w1)
-    halo = sent(tail, HALO_NEXT)
+    shared = (w0, sent(w1, Y_UP), sent(w2, Y_TWO), sent(w3, Y_DOWN))
+    columns = run_join(y, shared)
+    halo = sent(acts[0, ROWS - HALO :], HALO_NEXT)
     order = jnp.stack([x, (x + 3) % NX, (x + 1) % NX, (x + 2) % NX, (512 - 64 * z) % 512])
     u = run_norm(order, halo, acts[0], norm_gain)
 
     blocks = ring_z(columns)
-    u, _ = together(u, columns)
-    below, above, _ = ring_four(u, Y_UP, Y_DOWN)
-    lo, hi, _ = together(below[:SPLIT], above[SPLIT:], blocks[3])
-    far_lo, far_hi = sent(lo, Y_UP), sent(hi, Y_DOWN)
-    rows = run(
+    below, above = near_pair(u, Y_UP, Y_DOWN)
+    far_lo, far_hi = far_pair(below, above, Y_UP, Y_DOWN, SPLIT)
+    rows, rows_far = run(
         stack_kernel, (y.reshape(1),), (u, below, above, far_lo, far_hi),
-        [shape_of(BF, NY, EXT, u.shape[1])],
-    )[0]
-    depth = len(blocks) * blocks[0].shape[0]
-    by_a, by_b = run(gather_kernel, (), blocks, [shape_of(BF, depth, WA), shape_of(BF, depth, WB)])
+        [plain(BF, NY, EXT, 3 * KX), plain(BF, NY, EXT, KX)],
+    )
+    depth = len(blocks) * blocks[1].shape[0]
+    by_a, by_b = run(gather_kernel, (), blocks, [shape_of(BF, depth, WA), plain(BF, depth, WB)])
 
     y, zero, _ = together(y, jnp.zeros((), jnp.int32), blocks[7])
     piece = lambda v, width: lax.dynamic_slice_in_dim(v, y * width, width, v.ndim - 1)
@@ -514,32 +577,33 @@
     skip = jnp.repeat(piece(skip_gain, HEADS), HD, axis=1)
     spreads = jnp.stack([spread(zero + k, 8) for k in range(8)] + [spread(zero + HEADS * 8, 1)])
 
-    a_below, a_above, a_far = ring_four(by_a, X_UP, X_DOWN)
-    fa_a, fb_a = a_far()
-    part_a = run_part(rows, by_a, a_below, a_above)
-
-    by_b, fa_a, fb_a = together(by_b, fa_a, fb_a)
-    b_below, b_above, b_far = ring_four(by_b, X_UP, X_DOWN)
-    xs, b_mat, sp, cum, e2, sc, row, states, pair, state, logs, message = run_state(
-        part_a, rows, fa_a, fb_a, taps_a, bias_a, small_bias, rate, spreads
-    )
-    fa_b, fb_b = b_far()
-    part_b = run_part(rows, by_b, b_below, b_above)
-
-    bits = [z & 1, (z >> 1) & 1, (z >> 2) & 1, x & 1, (x >> 1) & 1]
-    buckets = []
-    for bit, pairs in zip(bits, EXCHANGES, strict=True):
+    bits = jnp.stack([z & 1, (z >> 1) & 1, (z >> 2) & 1, x & 1, (x >> 1) & 1, zero, zero, zero])
+    masks = run(mask_kernel, (bits,), (), [shape_of(jnp.int32, 8, XW)])[0]
+
+    a_below, a_above = near_pair(by_a, X_UP, X_DOWN)
+    fa_a, fb_a = far_pair(a_below, a_above, X_UP, X_DOWN, KX // 2)
+    part_a = run_part(rows, by_a, a_below, a_above, shape_of)
+
+    b_below, b_above = near_pair(by_b, X_UP, X_DOWN)
+    xs, b_mat, sp, cum, e2, sc, row, states, pair, logs, message = run_state(
+        part_a, rows_far, fa_a, fb_a, taps_a, bias_a, small_bias, rate, spreads
+    )
+    fa_b, fb_b = far_pair(b_below, b_above, X_UP, X_DOWN, KX // 2)
+    part_b = run_part(rows, by_b, b_below, b_above, plain)
+
+    gots = []
+    for k, pairs in enumerate(EXCHANGES):
         got = sent(message, pairs)
-        message, state, logs, bucket = run_merge(bit, got, state, logs)
-        buckets.append(bucket)
+        message, logs = run_merge(k, masks, got, message, logs)
+        gots.append(got)
 
     y_part, c_mat, z_cols = run_intra(
-        part_b, rows, fa_b, fb_b, conv_weight[0, :, 2048 + NS :], conv_bias[:, 2048 + NS :], skip,
+        part_b, rows_far, fa_b, fb_b, conv_weight[0, :, 2048 + NS :], conv_bias[:, 2048 + NS :], skip,
         xs, b_mat, sp, cum, e2, row, states, pair, spreads,
     )
     block = lambda k: (y + k) % NY
-    q2, q1 = run_cross((block(2), block(1)), y_part, c_mat, sc, z_cols, buckets, spreads)
-    q3, q0 = run_cross((block(3), block(0)), y_part, c_mat, sc, z_cols, buckets, spreads)
+    order = jnp.stack([block(k) for k in range(NY)])
+    q0, q1, q2, q3 = run_cross(order, y_part, c_mat, sc, z_cols, gots, logs, spreads)
     blocks = (q0, sent(q1, Y_UP), sent(q2, Y_TWO), sent(q3, Y_DOWN))
     heads_at = jnp.stack([block(0), block(3), block(2), block(1)])
     result = run_out(heads_at, blocks, gate_gain, out_proj[0], acts[0])

time: 203 us -> 168 us (0.83)
  local copies, waits for them, and re-layouts: 45.5 us -> 8.43 us
  Pallas kernels: 46.3 us -> 60.5 us
  starting transfers between devices: 60 us -> 54.1 us
  waiting for transfers between devices: 49.2 us -> 43.8 us
    unnamed x127 -> x39, local copies, waits for them, and re-layouts: 33.1 us -> 5.66 us
    pallas_call x17 -> x22, Pallas kernels: 46.3 us -> 55.6 us  [run(): pl.pallas_call(kernel, in_specs=[smem] * len(scalars) + [vmem] * len(arra...]
    slice x6 -> x0, local copies, waits for them, and re-layouts: 7.79 us -> none  [the longest x2 2.78 us: layer(): lo, hi, _ = together(below[:SPLIT], above[SPLIT:], blocks[3])]
    ppermute x1, starting transfers between devices: 19.1 us -> 13.4 us  [layer(): return lax.ppermute(result, 'section', [(0, 1), (1, 0)])[None]]
    ppermute x31, waiting for transfers between devices: 46.9 us -> 41.5 us  [sent(): return lax.ppermute(getattr(value, 'value', value), 'seq', pairs)]
    pallas_call x0 -> x1, Pallas kernels: none -> 4.92 us  [run_out(): pl.pallas_call(out_kernel, in_specs=[pl.BlockSpec(memory_space=pltpu.SMEM...]
  transfers between devices with their start and end apart: 32 -> 32, of which waited for: 15 -> 10; matrix products, arithmetic and copies ran while one was open for 6% -> 2% of each run, Pallas kernels for 16% -> 30%
where the time goes in v1:
time: 168 us
  Pallas kernels  60.5 us (36%)
  starting transfers between devices  54.1 us (32%)
  waiting for transfers between devices  43.8 us (26%)
  local copies, waits for them, and re-layouts  8.43 us (5%)
    pallas_call x22, Pallas kernels, run(): pl.pallas_call(kernel, in_specs=[smem] * len(scalars) + [vmem] * len(arra...  55.6 us
    ppermute x31, waiting for transfers between devices, sent(): return lax.ppermute(getattr(value, 'value', value), 'seq', pairs)  41.5 us
    ppermute x31, starting transfers between devices, sent(): return lax.ppermute(getattr(value, 'value', value), 'seq', pairs)  40.7 us
    ppermute x1, starting transfers between devices, layer(): return lax.ppermute(result, 'section', [(0, 1), (1, 0)])[None]  13.4 us
    unnamed x39, local copies, waits for them, and re-layouts  5.66 us
    pallas_call x1, Pallas kernels, run_out(): pl.pallas_call(out_kernel, in_specs=[pl.BlockSpec(memory_space=pltpu.SMEM...  4.92 us
  transfers between devices with their start and end apart: 32, of which 10 were waited for; matrix products, arithmetic and copies ran while one was open for 2% of the time, Pallas kernels for 30%

profile of v1, /device:TPU:1, one launch (start us, length us, event | category | flops | bytes accessed | tf_op | source)
XLA Modules:
  0.0 167.8 jit_solution(8801477966415049369)
XLA Ops:
  0.0 0.9 copy-done.11
  1.0 2.2 %collective-permute-start = (bf16[16,1408]{1,0:T(8,128)(2,1)S(1)}, bf16[16,1408]{1,0:T(8,128)(2,1)S(1)}, u32[]{:S(2)}, u32[]{:S(2)}) collective-permute-start(bf16[16,1408]{1,0:T(8,128)(2,1)S(1)} %get-tuple-element.43), channel_id=1, source_target_pairs={{0,1},{1,2},{2,3},{3,0},{4,5},{5,6},{6,7},{7,4},{8,9},{9,10},{10,1... | collective-permute-start | bytes 135176 | tf_op jit(solution)/shard_map/ppermute | solution.py:58
  3.2 2.6 %collective-permute-start.1 = (bf16[16,1408]{1,0:T(8,128)(2,1)S(1)}, bf16[16,1408]{1,0:T(8,128)(2,1)S(1)}, u32[]{:S(2)}, u32[]{:S(2)}) collective-permute-start(bf16[16,1408]{1,0:T(8,128)(2,1)S(1)} %get-tuple-element.44), channel_id=1, source_target_pairs={{0,2},{1,3},{2,0},{3,1},{4,6},{5,7},{6,4},{7,5},{8,10},{9,11},{10,... | collective-permute-start | bytes 135176 | tf_op jit(solution)/shard_map/ppermute | solution.py:58
  5.8 1.1 collective-permute-start.2
  7.8 2.3 %collective-permute-start.4 = (bf16[16,2048]{1,0:T(8,128)(2,1)S(1)}, bf16[16,2048]{1,0:T(8,128)(2,1)S(1)}, u32[]{:S(2)}, u32[]{:S(2)}) collective-permute-start(bf16[16,2048]{1,0:T(8,128)(2,1)S(1)} %slice_bitcast_fusion), channel_id=1, source_target_pairs={{0,1},{1,2},{2,3},{3,4},{4,5},{5,6},{6,7},{7,8},{8,9},{9,10},{10,1... | collective-permute-start | bytes 196616 | tf_op jit(solution)/shard_map/ppermute | solution.py:58
  12.2 1.6 collective-permute-start.3
  13.9 4.0 %collective-permute-start.9 = (bf16[64,1408]{1,0:T(8,128)(2,1)}, bf16[64,1408]{1,0:T(8,128)(2,1)}, u32[]{:S(2)}, u32[]{:S(2)}) collective-permute-start(bf16[64,1408]{1,0:T(8,128)(2,1)} %shard_map.110.refs_0_), channel_id=1, source_target_pairs={{0,28},{1,29},{2,30},{3,31},{4,0},{5,1},{6,2},{7,3},{8,4},{9,5},{1... | collective-permute-start | bytes 540680 | tf_op jit(solution)/shard_map/ppermute | solution.py:58
  17.9 1.2 copy-done.2
  19.8 1.6 shard_map.111.own_ref
  21.6 2.7 %collective-permute-start.6 = (bf16[272,2048]{1,0:T(8,128)(2,1)S(1)}, bf16[272,2048]{1,0:T(8,128)(2,1)S(1)}, u32[]{:S(2)}, u32[]{:S(2)}) collective-permute-start(bf16[272,2048]{1,0:T(8,128)(2,1)S(1)} %shard_map.111.own_ref), channel_id=1, source_target_pairs={{0,3},{1,0},{2,1},{3,2},{4,7},{5,4},{6,5},{7,6},{8,11},{9,8},{10,9... | collective-permute-start | bytes 3342344 | tf_op jit(solution)/shard_map/ppermute | solution.py:58
  24.5 2.7 %collective-permute-start.10 = (bf16[64,1408]{1,0:T(8,128)(2,1)}, bf16[64,1408]{1,0:T(8,128)(2,1)S(1)}, u32[]{:S(2)}, u32[]{:S(2)}) collective-permute-start(bf16[64,1408]{1,0:T(8,128)(2,1)} %collective-permute-done.9.refs_1_), channel_id=1, source_target_pairs={{0,28},{1,29},{2,30},{3,31},{4,0},{5,1},{6,2},{7,3},{8,4},{9,5},{1... | collective-permute-start | bytes 540680 | tf_op jit(solution)/shard_map/ppermute | solution.py:58
  27.3 3.4 %collective-permute-done.12.refs_6_ = bf16[64,1408]{1,0:T(8,128)(2,1)} collective-permute-done((bf16[64,1408]{1,0:T(8,128)(2,1)}, bf16[64,1408]{1,0:T(8,128)(2,1)}, u32[]{:S(2)}, u32[]{:S(2)}) %collective-permute-start.12) | collective-permute-done | bytes 180256 | tf_op jit(solution)/shard_map/ppermute | solution.py:58
  30.7 2.8 %collective-permute-start.11 = (bf16[64,1408]{1,0:T(8,128)(2,1)S(1)}, bf16[64,1408]{1,0:T(8,128)(2,1)S(1)}, u32[]{:S(2)}, u32[]{:S(2)}) collective-permute-start(bf16[64,1408]{1,0:T(8,128)(2,1)S(1)} %collective-permute-done.10.refs_2_), channel_id=1, source_target_pairs={{0,28},{1,29},{2,30},{3,31},{4,0},{5,1},{6,2},{7,3},{8,4},{9,5},{1... | collective-permute-start | bytes 540680 | tf_op jit(solution)/shard_map/ppermute | solution.py:58
  33.4 3.4 %collective-permute-done.13.refs_5_ = bf16[64,1408]{1,0:T(8,128)(2,1)S(1)} collective-permute-done((bf16[64,1408]{1,0:T(8,128)(2,1)}, bf16[64,1408]{1,0:T(8,128)(2,1)S(1)}, u32[]{:S(2)}, u32[]{:S(2)}) %collective-permute-start.13) | collective-permute-done | bytes 180256 | tf_op jit(solution)/shard_map/ppermute | solution.py:58
  36.8 6.3 %collective-permute-done.14.refs_4_ = bf16[64,1408]{1,0:T(8,128)(2,1)S(1)} collective-permute-done((bf16[64,1408]{1,0:T(8,128)(2,1)S(1)}, bf16[64,1408]{1,0:T(8,128)(2,1)S(1)}, u32[]{:S(2)}, u32[]{:S(2)}) %collective-permute-start.14) | collective-permute-done | bytes 180256 | tf_op jit(solution)/shard_map/ppermute | solution.py:58
  43.1 2.4 %shard_map.115 = (bf16[512,768]{1,0:T(8,128)(2,1)}, bf16[512,640]{1,0:T(8,128)(2,1)}) custom-call(bf16[64,1408]{1,0:T(8,128)(2,1)} %shard_map.110.refs_0_, bf16[64,1408]{1,0:T(8,128)(2,1)} %collective-permute-done.9.refs_1_, bf16[64,1408]{1,0:T(8,128)(2,1)S(1)} %collective-permute-done.10.refs_2_, bf16[64,1408]{1,0:T(8,128)(2,1)S(1)} %collective-permute-done.11.refs_3_, ...), custom_call_target="tpu_custom_call" | custom-call | tf_op jit(solution)/shard_map/pallas_call | solution.py:117
  45.5 1.2 collective-permute-start.19
  46.7 1.5 collective-permute-start.20
  48.3 0.9 shard_map.113
  49.2 0.9 collective-permute-start.8
  50.1 2.1 %shard_map.112 = bf16[144,2048]{1,0:T(8,128)(2,1)} custom-call(bf16[272,2048]{1,0:T(8,128)(2,1)} %collective-permute-done.5.block_ref.below_ref), custom_call_target="tpu_custom_call" | custom-call | tf_op jit(solution)/shard_map/pallas_call | solution.py:117
  52.9 7.8 %collective-permute-done.19.below_ref.block_ref = bf16[512,768]{1,0:T(8,128)(2,1)} collective-permute-done((bf16[512,768]{1,0:T(8,128)(2,1)}, bf16[512,768]{1,0:T(8,128)(2,1)}, u32[]{:S(2)}, u32[]{:S(2)}) %collective-permute-start.19) | collective-permute-done | bytes 786464 | tf_op jit(solution)/shard_map/ppermute | solution.py:58
  60.7 1.2 shard_map.120
  62.0 1.2 shard_map.121
  63.1 2.7 %collective-permute-start.22 = (bf16[256,768]{1,0:T(8,128)(2,1)S(1)}, bf16[256,768]{1,0:T(8,128)(2,1)S(1)}, u32[]{:S(2)}, u32[]{:S(2)}) collective-permute-start(bf16[256,768]{1,0:T(8,128)(2,1)S(1)} %shard_map.121), channel_id=1, source_target_pairs={{0,96},{1,97},{2,98},{3,99},{4,100},{5,101},{6,102},{7,103},{8,104... | collective-permute-start | bytes 1179656 | tf_op jit(solution)/shard_map/ppermute | solution.py:58
  66.0 2.7 %collective-permute-start.16 = (bf16[512,640]{1,0:T(8,128)(2,1)}, bf16[512,640]{1,0:T(8,128)(2,1)}, u32[]{:S(2)}, u32[]{:S(2)}) collective-permute-start(bf16[512,640]{1,0:T(8,128)(2,1)} %get-tuple-element.48.own_ref), channel_id=1, source_target_pairs={{0,96},{1,97},{2,98},{3,99},{4,100},{5,101},{6,102},{7,103},{8,104... | collective-permute-start | bytes 1966088 | tf_op jit(solution)/shard_map/ppermute | solution.py:58
  68.8 3.9 %shard_map.114 = (bf16[4,272,1536]{2,1,0:T(8,128)(2,1)}, bf16[4,272,512]{2,1,0:T(8,128)(2,1)}) custom-call(s32[1]{0:T(128)} %bitcast.y_ref, bf16[272,2048]{1,0:T(8,128)(2,1)S(1)} %shard_map.111.own_ref, bf16[272,2048]{1,0:T(8,128)(2,1)} %collective-permute-done.5.block_ref.below_ref, bf16[272,2048]{1,0:T(8,128)(2,1)S(1)} %collective-permute-done.6.block_ref.above_ref, ...), custom_call_target="tpu_custom_call" | custom-call | tf_op jit(solution)/shard_map/pallas_call | solution.py:117
  72.7 5.9 %shard_map.119.part_ref = f32[4,272,768]{2,1,0:T(8,128)S(1)} custom-call(bf16[4,272,1536]{2,1,0:T(8,128)(2,1)} %get-tuple-element.47.rows_ref, bf16[512,768]{1,0:T(8,128)(2,1)} %get-tuple-element.50.own_ref, bf16[512,768]{1,0:T(8,128)(2,1)} %collective-permute-done.19.below_ref.block_ref, bf16[512,768]{1,0:T(8,128)(2,1)} %collective-permute-done.20.above_ref.block_ref), custom_call_target="tpu_custom_call" | custom-call | tf_op jit(solution)/shard_map/pallas_call | solution.py:117
  78.6 9.9 %shard_map.122 = (f32[4,256,512]{2,1,0:T(8,128)}, bf16[4,256,128]{2,1,0:T(8,128)(2,1)}, f32[4,256,128]{2,1,0:T(8,128)}, f32[4,256,128]{2,1,0:T(8,128)}, f32[4,25...) custom-call(f32[4,272,768]{2,1,0:T(8,128)S(1)} %shard_map.119.part_r, ...), custom_call_target="tpu_custom_call" | custom-call | tf_op jit(solution)/shard_map/pallas_call | solution.py:117
  89.2 3.3 %collective-permute-done.23.got_ref.g3 = bf16[144,512]{1,0:T(8,128)(2,1)S(1)} collective-permute-done((bf16[144,512]{1,0:T(8,128)(2,1)S(1)}, bf16[144,512]{1,0:T(8,128)(2,1)S(1)}, u32[]{:S(2)}, u32[]{:S(2)}) %collective-permute-start.23) | collective-permute-done | bytes 147488 | tf_op jit(solution)/shard_map/ppermute | solution.py:58
  93.3 5.6 %collective-permute-done.24.got_ref.g4 = bf16[144,512]{1,0:T(8,128)(2,1)S(1)} collective-permute-done((bf16[144,512]{1,0:T(8,128)(2,1)S(1)}, bf16[144,512]{1,0:T(8,128)(2,1)S(1)}, u32[]{:S(2)}, u32[]{:S(2)}) %collective-permute-start.24) | collective-permute-done | bytes 147488 | tf_op jit(solution)/shard_map/ppermute | solution.py:58
  99.0 2.2 %collective-permute-start.25 = (bf16[144,512]{1,0:T(8,128)(2,1)S(1)}, bf16[144,512]{1,0:T(8,128)(2,1)S(1)}, u32[]{:S(2)}, u32[]{:S(2)}) collective-permute-start(bf16[144,512]{1,0:T(8,128)(2,1)S(1)} %get-tuple-element.68.own_ref), channel_id=1, source_target_pairs={{0,28},{1,29},{2,30},{3,31},{4,24},{5,25},{6,26},{7,27},{8,20},{9,... | collective-permute-start | bytes 442376 | tf_op jit(solution)/shard_map/ppermute | solution.py:58
  101.2 4.6 %collective-permute-done.25.got_ref.g5 = bf16[144,512]{1,0:T(8,128)(2,1)S(1)} collective-permute-done((bf16[144,512]{1,0:T(8,128)(2,1)S(1)}, bf16[144,512]{1,0:T(8,128)(2,1)S(1)}, u32[]{:S(2)}, u32[]{:S(2)}) %collective-permute-start.25) | collective-permute-done | bytes 147488 | tf_op jit(solution)/shard_map/ppermute | solution.py:58
  105.9 1.1 shard_map.117
  107.1 1.5 collective-permute-start.17
  108.6 1.1 shard_map.118
  109.7 1.3 collective-permute-start.18
  111.8 7.5 %shard_map.116.part_ref = f32[4,272,640]{2,1,0:T(8,128)} custom-call(bf16[4,272,1536]{2,1,0:T(8,128)(2,1)} %get-tuple-element.47.rows_ref, bf16[512,640]{1,0:T(8,128)(2,1)} %get-tuple-element.48.own_ref, bf16[512,640]{1,0:T(8,128)(2,1)} %collective-permute-done.15.below_ref.block_ref, bf16[512,640]{1,0:T(8,128)(2,1)} %collective-permute-done.16.above_ref.block_ref), custom_call_target="tpu_custom_call" | custom-call | tf_op jit(solution)/shard_map/pallas_call | solution.py:117
  119.4 1.8 %copy-done.1 = f32[4,272,640]{2,1,0:T(8,128)S(1)} copy-done((f32[4,272,640]{2,1,0:T(8,128)S(1)}, f32[4,272,640]{2,1,0:T(8,128)}, u32[]{:S(2)}) %copy-start.1) | copy-done | bytes 2785304
  121.2 9.1 %shard_map.123 = (f32[4,256,512]{2,1,0:T(8,128)}, bf16[4,256,128]{2,1,0:T(8,128)(2,1)}, bf16[4,256,512]{2,1,0:T(8,128)(2,1)}) custom-call(f32[4,272,640]{2,1,0:T(8,128)S(1)} %copy-done.1, bf16[4,272,512]{2,1,0:T(8,128)(2,1)S(1)} %copy-done.4, bf16[256,640]{1,0:T(8,128)(2,1)S(1)} %collective-permute-done.17.fa_ref, ...), custom_call_target="tpu_custom_call" | custom-call | tf_op jit(solution)/shard_map/pallas_call | solution.py:117
  131.0 5.3 %shard_map.130 = (bf16[256,512]{1,0:T(8,128)(2,1)S(1)}, bf16[256,512]{1,0:T(8,128)(2,1)S(1)}, bf16[256,512]{1,0:T(8,128)(2,1)S(1)}, bf16[256,512]{1,0:T(8,128)(2,1)S(1)}) custom-call(s32[4]{0:T(128)S(1)} %pad_add_fusion.1.at_ref, f32[4,256,512]{2,1,0:T(8,128)} %get-tuple-element.60.y_ref, bf16[4,256,128]{2,1,0:T(8,128)(2,1)} %get-tuple-element.61.c_ref, ...), custom_call_target="tpu_custom_call" | custom-call | tf_op jit(solution)/shard_map/pallas_call | solution.py:117
  136.4 1.0 collective-permute-start.29
  137.3 1.7 %collective-permute-start.30 = (bf16[256,512]{1,0:T(8,128)(2,1)S(1)}, bf16[256,512]{1,0:T(8,128)(2,1)S(1)}, u32[]{:S(2)}, u32[]{:S(2)}) collective-permute-start(bf16[256,512]{1,0:T(8,128)(2,1)S(1)} %get-tuple-element.78), channel_id=1, source_target_pairs={{0,3},{1,0},{2,1},{3,2},{4,7},{5,4},{6,5},{7,6},{8,11},{9,8},{10,9... | collective-permute-start | bytes 786440 | tf_op jit(solution)/shard_map/ppermute | solution.py:58
  139.1 6.5 %collective-permute-done.28.q1 = bf16[256,512]{1,0:T(8,128)(2,1)S(1)} collective-permute-done((bf16[256,512]{1,0:T(8,128)(2,1)S(1)}, bf16[256,512]{1,0:T(8,128)(2,1)S(1)}, u32[]{:S(2)}, u32[]{:S(2)}) %collective-permute-start.28) | collective-permute-done | bytes 262176 | tf_op jit(solution)/shard_map/ppermute | solution.py:58
  146.2 4.9 %gate_out.1 = bf16[256,2048]{1,0:T(8,128)(2,1)S(1)} custom-call(s32[4]{0:T(128)S(1)} %pad_add_fusion.at_ref, bf16[256,512]{1,0:T(8,128)(2,1)S(1)} %get-tuple-element.75.q0, bf16[256,512]{1,0:T(8,128)(2,1)S(1)} %collective-permute-done.28.q1, bf16[256,512]{1,0:T(8,128)(2,1)S(1)} %collective-permute-done.29.q2, ...), custom_call_target="tpu_custom_call" | custom-call | tf_op jit(solution)/shard_map/gate_out/pallas_call | solution.py:399
  151.1 13.4 %collective-permute-start.31 = (bf16[256,2048]{1,0:T(8,128)(2,1)S(1)}, bf16[256,2048]{1,0:T(8,128)(2,1)S(1)}, u32[]{:S(2)}, u32[]{:S(2)}) collective-permute-start(bf16[256,2048]{1,0:T(8,128)(2,1)S(1)} %gate_out.1), channel_id=1, source_target_pairs={{0,128},{128,0},{1,129},{129,1},{2,130},{130,2},{3,131},{131,3},{4... | collective-permute-start | bytes 3145736 | tf_op jit(solution)/shard_map/ppermute | solution.py:610
  164.6 2.3 %collective-permute-done.31 = bf16[256,2048]{1,0:T(8,128)(2,1)S(1)} collective-permute-done((bf16[256,2048]{1,0:T(8,128)(2,1)S(1)}, bf16[256,2048]{1,0:T(8,128)(2,1)S(1)}, u32[]{:S(2)}, u32[]{:S(2)}) %collective-permute-start.31) | collective-permute-done | bytes 1048608 | tf_op jit(solution)/shard_map/ppermute | solution.py:610
  166.8 1.0 copy.21
  (112 shorter events, 9.1 us)
Async XLA Ops:
  0.0 65.9 %copy-start = (f32[1,256]{1,0:T(1,128)S(1)}, f32[1,256]{1,0:T(1,128)}, u32[]{:S(2)}) copy-start(f32[1,256]{1,0:T(1,128)} %param.19) | copy-start | bytes 3076
  1.0 10.5 %collective-permute-start = (bf16[16,1408]{1,0:T(8,128)(2,1)S(1)}, bf16[16,1408]{1,0:T(8,128)(2,1)S(1)}, u32[]{:S(2)}, u32[]{:S(2)}) collective-permute-start(bf16[16,1408]{1,0:T(8,128)(2,1)S(1)} %get-tuple-element.43), channel_id=1, source_target_pairs={{0,1},{1,2},{2,3},{3,0},{4,5},{5,6},{6,7},{7,4},{8,9},{9,10},{10,1... | collective-permute-start | bytes 135176 | tf_op jit(solution)/shard_map/ppermute | solution.py:58
  3.2 8.3 %collective-permute-start.1 = (bf16[16,1408]{1,0:T(8,128)(2,1)S(1)}, bf16[16,1408]{1,0:T(8,128)(2,1)S(1)}, u32[]{:S(2)}, u32[]{:S(2)}) collective-permute-start(bf16[16,1408]{1,0:T(8,128)(2,1)S(1)} %get-tuple-element.44), channel_id=1, source_target_pairs={{0,2},{1,3},{2,0},{3,1},{4,6},{5,7},{6,4},{7,5},{8,10},{9,11},{10,... | collective-permute-start | bytes 135176 | tf_op jit(solution)/shard_map/ppermute | solution.py:58
  5.8 5.7 %collective-permute-start.2 = (bf16[16,1408]{1,0:T(8,128)(2,1)S(1)}, bf16[16,1408]{1,0:T(8,128)(2,1)S(1)}, u32[]{:S(2)}, u32[]{:S(2)}) collective-permute-start(bf16[16,1408]{1,0:T(8,128)(2,1)S(1)} %get-tuple-element.45), channel_id=1, source_target_pairs={{0,3},{1,0},{2,1},{3,2},{4,7},{5,4},{6,5},{7,6},{8,11},{9,8},{10,9... | collective-permute-start | bytes 135176 | tf_op jit(solution)/shard_map/ppermute | solution.py:58
  7.8 10.2 %collective-permute-start.4 = (bf16[16,2048]{1,0:T(8,128)(2,1)S(1)}, bf16[16,2048]{1,0:T(8,128)(2,1)S(1)}, u32[]{:S(2)}, u32[]{:S(2)}) collective-permute-start(bf16[16,2048]{1,0:T(8,128)(2,1)S(1)} %slice_bitcast_fusion), channel_id=1, source_target_pairs={{0,1},{1,2},{2,3},{3,4},{4,5},{5,6},{6,7},{7,8},{8,9},{9,10},{10,1... | collective-permute-start | bytes 196616 | tf_op jit(solution)/shard_map/ppermute | solution.py:58
  12.2 12.0 %collective-permute-start.3 = (bf16[64,1408]{1,0:T(8,128)(2,1)}, bf16[64,1408]{1,0:T(8,128)(2,1)}, u32[]{:S(2)}, u32[]{:S(2)}) collective-permute-start(bf16[64,1408]{1,0:T(8,128)(2,1)} %shard_map.110.refs_0_), channel_id=1, source_target_pairs={{0,4},{1,5},{2,6},{3,7},{4,8},{5,9},{6,10},{7,11},{8,12},{9,13},{1... | collective-permute-start | bytes 540680 | tf_op jit(solution)/shard_map/ppermute | solution.py:58
  13.9 10.6 %collective-permute-start.9 = (bf16[64,1408]{1,0:T(8,128)(2,1)}, bf16[64,1408]{1,0:T(8,128)(2,1)}, u32[]{:S(2)}, u32[]{:S(2)}) collective-permute-start(bf16[64,1408]{1,0:T(8,128)(2,1)} %shard_map.110.refs_0_), channel_id=1, source_target_pairs={{0,28},{1,29},{2,30},{3,31},{4,0},{5,1},{6,2},{7,3},{8,4},{9,5},{1... | collective-permute-start | bytes 540680 | tf_op jit(solution)/shard_map/ppermute | solution.py:58
  21.5 28.7 %collective-permute-start.5 = (bf16[272,2048]{1,0:T(8,128)(2,1)S(1)}, bf16[272,2048]{1,0:T(8,128)(2,1)}, u32[]{:S(2)}, u32[]{:S(2)}) collective-permute-start(bf16[272,2048]{1,0:T(8,128)(2,1)S(1)} %shard_map.111.own_ref), channel_id=1, source_target_pairs={{0,1},{1,2},{2,3},{3,0},{4,5},{5,6},{6,7},{7,4},{8,9},{9,10},{10,1... | collective-permute-start | bytes 3342344 | tf_op jit(solution)/shard_map/ppermute | solution.py:58
  21.6 26.7 %collective-permute-start.6 = (bf16[272,2048]{1,0:T(8,128)(2,1)S(1)}, bf16[272,2048]{1,0:T(8,128)(2,1)S(1)}, u32[]{:S(2)}, u32[]{:S(2)}) collective-permute-start(bf16[272,2048]{1,0:T(8,128)(2,1)S(1)} %shard_map.111.own_ref), channel_id=1, source_target_pairs={{0,3},{1,0},{2,1},{3,2},{4,7},{5,4},{6,5},{7,6},{8,11},{9,8},{10,9... | collective-permute-start | bytes 3342344 | tf_op jit(solution)/shard_map/ppermute | solution.py:58
  24.4 6.2 %collective-permute-start.12 = (bf16[64,1408]{1,0:T(8,128)(2,1)}, bf16[64,1408]{1,0:T(8,128)(2,1)}, u32[]{:S(2)}, u32[]{:S(2)}) collective-permute-start(bf16[64,1408]{1,0:T(8,128)(2,1)} %collective-permute-done.3.refs_7_), channel_id=1, source_target_pairs={{0,4},{1,5},{2,6},{3,7},{4,8},{5,9},{6,10},{7,11},{8,12},{9,13},{1... | collective-permute-start | bytes 540680 | tf_op jit(solution)/shard_map/ppermute | solution.py:58
  24.5 6.1 %collective-permute-start.10 = (bf16[64,1408]{1,0:T(8,128)(2,1)}, bf16[64,1408]{1,0:T(8,128)(2,1)S(1)}, u32[]{:S(2)}, u32[]{:S(2)}) collective-permute-start(bf16[64,1408]{1,0:T(8,128)(2,1)} %collective-permute-done.9.refs_1_), channel_id=1, source_target_pairs={{0,28},{1,29},{2,30},{3,31},{4,0},{5,1},{6,2},{7,3},{8,4},{9,5},{1... | collective-permute-start | bytes 540680 | tf_op jit(solution)/shard_map/ppermute | solution.py:58
  30.6 6.2 %collective-permute-start.13 = (bf16[64,1408]{1,0:T(8,128)(2,1)}, bf16[64,1408]{1,0:T(8,128)(2,1)S(1)}, u32[]{:S(2)}, u32[]{:S(2)}) collective-permute-start(bf16[64,1408]{1,0:T(8,128)(2,1)} %collective-permute-done.12.refs_6_), channel_id=1, source_target_pairs={{0,4},{1,5},{2,6},{3,7},{4,8},{5,9},{6,10},{7,11},{8,12},{9,13},{1... | collective-permute-start | bytes 540680 | tf_op jit(solution)/shard_map/ppermute | solution.py:58
  30.7 6.2 %collective-permute-start.11 = (bf16[64,1408]{1,0:T(8,128)(2,1)S(1)}, bf16[64,1408]{1,0:T(8,128)(2,1)S(1)}, u32[]{:S(2)}, u32[]{:S(2)}) collective-permute-start(bf16[64,1408]{1,0:T(8,128)(2,1)S(1)} %collective-permute-done.10.refs_2_), channel_id=1, source_target_pairs={{0,28},{1,29},{2,30},{3,31},{4,0},{5,1},{6,2},{7,3},{8,4},{9,5},{1... | collective-permute-start | bytes 540680 | tf_op jit(solution)/shard_map/ppermute | solution.py:58
  36.8 6.3 %collective-permute-start.14 = (bf16[64,1408]{1,0:T(8,128)(2,1)S(1)}, bf16[64,1408]{1,0:T(8,128)(2,1)S(1)}, u32[]{:S(2)}, u32[]{:S(2)}) collective-permute-start(bf16[64,1408]{1,0:T(8,128)(2,1)S(1)} %collective-permute-done.13.refs_5_), channel_id=1, source_target_pairs={{0,4},{1,5},{2,6},{3,7},{4,8},{5,9},{6,10},{7,11},{8,12},{9,13},{1... | collective-permute-start | bytes 540680 | tf_op jit(solution)/shard_map/ppermute | solution.py:58
  45.5 4.6 %slice-start.1 = ((f32[1,2304]{1,0:T(1,128)}), f32[1,2048]{1,0:T(1,128)S(1)}, s32[]{:S(2)}) async-start(f32[1,2304]{1,0:T(1,128)} %param.15), calls=%async_computation.1 | async-start | bytes 16384 | tf_op jit(solution)/shard_map/slice | solution.py:568
  45.5 15.2 %collective-permute-start.19 = (bf16[512,768]{1,0:T(8,128)(2,1)}, bf16[512,768]{1,0:T(8,128)(2,1)}, u32[]{:S(2)}, u32[]{:S(2)}) collective-permute-start(bf16[512,768]{1,0:T(8,128)(2,1)} %get-tuple-element.50.own_ref), channel_id=1, source_target_pairs={{0,32},{1,33},{2,34},{3,35},{4,36},{5,37},{6,38},{7,39},{8,40},{9,... | collective-permute-start | bytes 2359304 | tf_op jit(solution)/shard_map/ppermute | solution.py:58
  46.7 15.2 %collective-permute-start.20 = (bf16[512,768]{1,0:T(8,128)(2,1)}, bf16[512,768]{1,0:T(8,128)(2,1)}, u32[]{:S(2)}, u32[]{:S(2)}) collective-permute-start(bf16[512,768]{1,0:T(8,128)(2,1)} %get-tuple-element.50.own_ref), channel_id=1, source_target_pairs={{0,96},{1,97},{2,98},{3,99},{4,100},{5,101},{6,102},{7,103},{8,104... | collective-permute-start | bytes 2359304 | tf_op jit(solution)/shard_map/ppermute | solution.py:58
  49.2 3.6 %copy-start.17 = (f32[1,32]{1,0:T(1,128)S(1)}, f32[1,32]{1,0:T(1,128)}, u32[]{:S(2)}) copy-start(f32[1,32]{1,0:T(1,128)} %param.16) | copy-start | bytes 388
  49.2 16.8 %collective-permute-start.8 = (bf16[128,2048]{1,0:T(8,128)(2,1)}, bf16[128,2048]{1,0:T(8,128)(2,1)}, u32[]{:S(2)}, u32[]{:S(2)}) collective-permute-start(bf16[128,2048]{1,0:T(8,128)(2,1)} %shard_map.113), channel_id=1, source_target_pairs={{0,3},{1,0},{2,1},{3,2},{4,7},{5,4},{6,5},{7,6},{8,11},{9,8},{10,9... | collective-permute-start | bytes 1572872 | tf_op jit(solution)/shard_map/ppermute | solution.py:58
  52.3 16.5 %collective-permute-start.7 = (bf16[144,2048]{1,0:T(8,128)(2,1)}, bf16[144,2048]{1,0:T(8,128)(2,1)}, u32[]{:S(2)}, u32[]{:S(2)}) collective-permute-start(bf16[144,2048]{1,0:T(8,128)(2,1)} %shard_map.112), channel_id=1, source_target_pairs={{0,1},{1,2},{2,3},{3,0},{4,5},{5,6},{6,7},{7,4},{8,9},{9,10},{10,1... | collective-permute-start | bytes 1769480 | tf_op jit(solution)/shard_map/ppermute | solution.py:58
  52.9 13.1 %slice-start = ((f32[1,4,2304]{2,1,0:T(4,128)}), f32[1,4,2048]{2,1,0:T(4,128)S(1)}, s32[]{:S(2)}) async-start(f32[1,4,2304]{2,1,0:T(4,128)} %param.14), calls=%async_computation | async-start | bytes 65536 | tf_op jit(solution)/shard_map/slice | solution.py:565
  61.9 16.7 %collective-permute-start.21 = (bf16[256,768]{1,0:T(8,128)(2,1)S(1)}, bf16[256,768]{1,0:T(8,128)(2,1)S(1)}, u32[]{:S(2)}, u32[]{:S(2)}) collective-permute-start(bf16[256,768]{1,0:T(8,128)(2,1)S(1)} %shard_map.120), channel_id=1, source_target_pairs={{0,32},{1,33},{2,34},{3,35},{4,36},{5,37},{6,38},{7,39},{8,40},{9,... | collective-permute-start | bytes 1179656 | tf_op jit(solution)/shard_map/ppermute | solution.py:58
  63.1 15.5 %collective-permute-start.22 = (bf16[256,768]{1,0:T(8,128)(2,1)S(1)}, bf16[256,768]{1,0:T(8,128)(2,1)S(1)}, u32[]{:S(2)}, u32[]{:S(2)}) collective-permute-start(bf16[256,768]{1,0:T(8,128)(2,1)S(1)} %shard_map.121), channel_id=1, source_target_pairs={{0,96},{1,97},{2,98},{3,99},{4,100},{5,101},{6,102},{7,103},{8,104... | collective-permute-start | bytes 1179656 | tf_op jit(solution)/shard_map/ppermute | solution.py:58
  65.9 40.0 %collective-permute-start.15 = (bf16[512,640]{1,0:T(8,128)(2,1)}, bf16[512,640]{1,0:T(8,128)(2,1)}, u32[]{:S(2)}, u32[]{:S(2)}) collective-permute-start(bf16[512,640]{1,0:T(8,128)(2,1)} %get-tuple-element.48.own_ref), channel_id=1, source_target_pairs={{0,32},{1,33},{2,34},{3,35},{4,36},{5,37},{6,38},{7,39},{8,40},{9,... | collective-permute-start | bytes 1966088 | tf_op jit(solution)/shard_map/ppermute | solution.py:58
  66.0 42.6 %collective-permute-start.16 = (bf16[512,640]{1,0:T(8,128)(2,1)}, bf16[512,640]{1,0:T(8,128)(2,1)}, u32[]{:S(2)}, u32[]{:S(2)}) collective-permute-start(bf16[512,640]{1,0:T(8,128)(2,1)} %get-tuple-element.48.own_ref), channel_id=1, source_target_pairs={{0,96},{1,97},{2,98},{3,99},{4,100},{5,101},{6,102},{7,103},{8,104... | collective-permute-start | bytes 1966088 | tf_op jit(solution)/shard_map/ppermute | solution.py:58
  88.5 4.0 %collective-permute-start.23 = (bf16[144,512]{1,0:T(8,128)(2,1)S(1)}, bf16[144,512]{1,0:T(8,128)(2,1)S(1)}, u32[]{:S(2)}, u32[]{:S(2)}) collective-permute-start(bf16[144,512]{1,0:T(8,128)(2,1)S(1)} %get-tuple-element.64.own_ref), channel_id=1, source_target_pairs={{0,4},{1,5},{2,6},{3,7},{4,0},{5,1},{6,2},{7,3},{8,12},{9,13},{10,... | collective-permute-start | bytes 442376 | tf_op jit(solution)/shard_map/ppermute | solution.py:58
  92.6 6.3 %collective-permute-start.24 = (bf16[144,512]{1,0:T(8,128)(2,1)S(1)}, bf16[144,512]{1,0:T(8,128)(2,1)S(1)}, u32[]{:S(2)}, u32[]{:S(2)}) collective-permute-start(bf16[144,512]{1,0:T(8,128)(2,1)S(1)} %get-tuple-element.66.own_ref), channel_id=1, source_target_pairs={{0,8},{1,9},{2,10},{3,11},{4,12},{5,13},{6,14},{7,15},{8,0},{9,1},... | collective-permute-start | bytes 442376 | tf_op jit(solution)/shard_map/ppermute | solution.py:58
  99.0 6.8 %collective-permute-start.25 = (bf16[144,512]{1,0:T(8,128)(2,1)S(1)}, bf16[144,512]{1,0:T(8,128)(2,1)S(1)}, u32[]{:S(2)}, u32[]{:S(2)}) collective-permute-start(bf16[144,512]{1,0:T(8,128)(2,1)S(1)} %get-tuple-element.68.own_ref), channel_id=1, source_target_pairs={{0,28},{1,29},{2,30},{3,31},{4,24},{5,25},{6,26},{7,27},{8,20},{9,... | collective-permute-start | bytes 442376 | tf_op jit(solution)/shard_map/ppermute | solution.py:58
  105.8 5.6 %copy-start.18 = (f32[1,32]{1,0:T(1,128)S(1)}, f32[1,32]{1,0:T(1,128)}, u32[]{:S(2)}) copy-start(f32[1,32]{1,0:T(1,128)} %param.18) | copy-start | bytes 388
  105.8 5.2 %collective-permute-start.26 = (bf16[144,512]{1,0:T(8,128)(2,1)S(1)}, bf16[144,512]{1,0:T(8,128)(2,1)S(1)}, u32[]{:S(2)}, u32[]{:S(2)}) collective-permute-start(bf16[144,512]{1,0:T(8,128)(2,1)S(1)} %get-tuple-element.70.own_ref), channel_id=1, source_target_pairs={{0,32},{1,33},{2,34},{3,35},{4,36},{5,37},{6,38},{7,39},{8,40},{9,... | collective-permute-start | bytes 442376 | tf_op jit(solution)/shard_map/ppermute | solution.py:58
  107.1 12.3 %collective-permute-start.17 = (bf16[256,640]{1,0:T(8,128)(2,1)S(1)}, bf16[256,640]{1,0:T(8,128)(2,1)S(1)}, u32[]{:S(2)}, u32[]{:S(2)}) collective-permute-start(bf16[256,640]{1,0:T(8,128)(2,1)S(1)} %shard_map.117), channel_id=1, source_target_pairs={{0,32},{1,33},{2,34},{3,35},{4,36},{5,37},{6,38},{7,39},{8,40},{9,... | collective-permute-start | bytes 983048 | tf_op jit(solution)/shard_map/ppermute | solution.py:58
  109.7 9.6 %collective-permute-start.18 = (bf16[256,640]{1,0:T(8,128)(2,1)S(1)}, bf16[256,640]{1,0:T(8,128)(2,1)S(1)}, u32[]{:S(2)}, u32[]{:S(2)}) collective-permute-start(bf16[256,640]{1,0:T(8,128)(2,1)S(1)} %shard_map.118), channel_id=1, source_target_pairs={{0,96},{1,97},{2,98},{3,99},{4,100},{5,101},{6,102},{7,103},{8,104... | collective-permute-start | bytes 983048 | tf_op jit(solution)/shard_map/ppermute | solution.py:58
  111.1 19.2 %collective-permute-start.27 = (bf16[144,512]{1,0:T(8,128)(2,1)S(1)}, bf16[144,512]{1,0:T(8,128)(2,1)S(1)}, u32[]{:S(2)}, u32[]{:S(2)}) collective-permute-start(bf16[144,512]{1,0:T(8,128)(2,1)S(1)} %get-tuple-element.72.own_ref), channel_id=1, source_target_pairs={{0,96},{1,97},{2,98},{3,99},{4,100},{5,101},{6,102},{7,103},{8,104... | collective-permute-start | bytes 442376 | tf_op jit(solution)/shard_map/ppermute | solution.py:58
  111.7 7.6 %copy-start.4 = (bf16[4,272,512]{2,1,0:T(8,128)(2,1)S(1)}, bf16[4,272,512]{2,1,0:T(8,128)(2,1)}, u32[]{:S(2)}) copy-start(bf16[4,272,512]{2,1,0:T(8,128)(2,1)} %get-tuple-element.49.rows_ref) | copy-start | bytes 3342340
  111.7 7.6 %copy-start.5 = (f32[4,256,512]{2,1,0:T(8,128)S(1)}, f32[4,256,512]{2,1,0:T(8,128)}, u32[]{:S(2)}) copy-start(f32[4,256,512]{2,1,0:T(8,128)} %get-tuple-element.52.xs_ref) | copy-start | bytes 6291460
  111.7 7.6 %copy-start.6 = (f32[4,256,128]{2,1,0:T(8,128)S(1)}, f32[4,256,128]{2,1,0:T(8,128)}, u32[]{:S(2)}) copy-start(f32[4,256,128]{2,1,0:T(8,128)} %get-tuple-element.54.sp_ref) | copy-start | bytes 1572868
  111.7 7.6 %copy-start.7 = (f32[4,256,128]{2,1,0:T(8,128)S(1)}, f32[4,256,128]{2,1,0:T(8,128)}, u32[]{:S(2)}) copy-start(f32[4,256,128]{2,1,0:T(8,128)} %get-tuple-element.55.cum_ref) | copy-start | bytes 1572868
  111.7 7.6 %copy-start.8 = (f32[4,256,128]{2,1,0:T(8,128)S(1)}, f32[4,256,128]{2,1,0:T(8,128)}, u32[]{:S(2)}) copy-start(f32[4,256,128]{2,1,0:T(8,128)} %get-tuple-element.56.e2_ref) | copy-start | bytes 1572868
  111.7 7.6 %copy-start.9 = (bf16[4,128,512]{2,1,0:T(8,128)(2,1)S(1)}, bf16[4,128,512]{2,1,0:T(8,128)(2,1)}, u32[]{:S(2)}) copy-start(bf16[4,128,512]{2,1,0:T(8,128)(2,1)} %get-tuple-element.58.s1_ref) | copy-start | bytes 1572868
  111.8 7.6 %copy-start.10 = (bf16[4,256,128]{2,1,0:T(8,128)(2,1)S(1)}, bf16[4,256,128]{2,1,0:T(8,128)(2,1)}, u32[]{:S(2)}) copy-start(bf16[4,256,128]{2,1,0:T(8,128)(2,1)} %get-tuple-element.53.b_ref) | copy-start | bytes 786436
  111.8 7.6 %copy-start.12 = (bf16[128,512]{1,0:T(8,128)(2,1)S(1)}, bf16[128,512]{1,0:T(8,128)(2,1)}, u32[]{:S(2)}) copy-start(bf16[128,512]{1,0:T(8,128)(2,1)} %get-tuple-element.59.s2_ref) | copy-start | bytes 393220
  111.8 7.6 %copy-start.13 = (f32[4,8,256]{2,1,0:T(8,128)S(1)}, f32[4,8,256]{2,1,0:T(8,128)}, u32[]{:S(2)}) copy-start(f32[4,8,256]{2,1,0:T(8,128)} %get-tuple-element.57.row_ref) | copy-start | bytes 98308
  131.0 15.2 %copy-start.3 = (bf16[1,256,2048]{2,1,0:T(8,128)(2,1)S(1)}, bf16[1,256,2048]{2,1,0:T(8,128)(2,1)}, u32[]{:S(2)}) copy-start(bf16[1,256,2048]{2,1,0:T(8,128)(2,1)} %param.11) | copy-start | bytes 3145732
  131.0 15.2 %copy-start.15 = (f32[1,2048]{1,0:T(1,128)S(1)}, f32[1,2048]{1,0:T(1,128)}, u32[]{:S(2)}) copy-start(f32[1,2048]{1,0:T(1,128)} %gain_ref.3) | copy-start | bytes 24580
  136.3 9.3 %collective-permute-start.28 = (bf16[256,512]{1,0:T(8,128)(2,1)S(1)}, bf16[256,512]{1,0:T(8,128)(2,1)S(1)}, u32[]{:S(2)}, u32[]{:S(2)}) collective-permute-start(bf16[256,512]{1,0:T(8,128)(2,1)S(1)} %get-tuple-element.76), channel_id=1, source_target_pairs={{0,1},{1,2},{2,3},{3,0},{4,5},{5,6},{6,7},{7,4},{8,9},{9,10},{10,1... | collective-permute-start | bytes 786440 | tf_op jit(solution)/shard_map/ppermute | solution.py:58
  136.4 9.2 %collective-permute-start.29 = (bf16[256,512]{1,0:T(8,128)(2,1)S(1)}, bf16[256,512]{1,0:T(8,128)(2,1)S(1)}, u32[]{:S(2)}, u32[]{:S(2)}) collective-permute-start(bf16[256,512]{1,0:T(8,128)(2,1)S(1)} %get-tuple-element.77), channel_id=1, source_target_pairs={{0,2},{1,3},{2,0},{3,1},{4,6},{5,7},{6,4},{7,5},{8,10},{9,11},{10,... | collective-permute-start | bytes 786440 | tf_op jit(solution)/shard_map/ppermute | solution.py:58
  137.3 8.9 %collective-permute-start.30 = (bf16[256,512]{1,0:T(8,128)(2,1)S(1)}, bf16[256,512]{1,0:T(8,128)(2,1)S(1)}, u32[]{:S(2)}, u32[]{:S(2)}) collective-permute-start(bf16[256,512]{1,0:T(8,128)(2,1)S(1)} %get-tuple-element.78), channel_id=1, source_target_pairs={{0,3},{1,0},{2,1},{3,2},{4,7},{5,4},{6,5},{7,6},{8,11},{9,8},{10,9... | collective-permute-start | bytes 786440 | tf_op jit(solution)/shard_map/ppermute | solution.py:58
  151.1 15.7 %collective-permute-start.31 = (bf16[256,2048]{1,0:T(8,128)(2,1)S(1)}, bf16[256,2048]{1,0:T(8,128)(2,1)S(1)}, u32[]{:S(2)}, u32[]{:S(2)}) collective-permute-start(bf16[256,2048]{1,0:T(8,128)(2,1)S(1)} %gate_out.1), channel_id=1, source_target_pairs={{0,128},{128,0},{1,129},{129,1},{2,130},{130,2},{3,131},{131,3},{4... | collective-permute-start | bytes 3145736 | tf_op jit(solution)/shard_map/ppermute | solution.py:610
  (5 other events, 8.2 us)

commit v2 on v1

--- a/solution.py
+++ b/solution.py
@@ -39,6 +39,7 @@
 
 X_UP = route(lambda x, z, y: (x + 1, z, y))
 X_DOWN = route(lambda x, z, y: (x - 1, z, y))
+X_TWO = route(lambda x, z, y: (x + 2, z, y))
 Z_UP = route(lambda x, z, y: (x, z + 1, y))
 Z_DOWN = route(lambda x, z, y: (x, z - 1, y))
 Y_UP = route(lambda x, z, y: (x, z, y + 1))
@@ -264,56 +265,69 @@
 
 
 def intra_kernel(
-    part_ref, rows_ref, fa_ref, fb_ref, taps_ref, bias_ref, skip_ref,
+    part_ref, rows_ref, far_ref, taps_ref, bias_ref, skip_ref,
     xs_ref, b_ref, sp_ref, cum_ref, e2_ref, row_ref, s1_ref, s2_ref, spread_ref,
     y_ref, c_ref, z_ref, wide_ref,
 ):
-    def block(j):
-        p = finished(part_ref, rows_ref, fa_ref, fb_ref, j)
-        z_ref[j] = p[HALO:, :XW].astype(BF)
-        wide_ref[...] = p[:, XW:]
-        c_mat = conv_block(wide_ref, taps_ref, bias_ref).astype(BF)
-        c_ref[j] = c_mat
-        xs = xs_ref[j]
-        sp = sp_ref[j].astype(BF)
-        cum = cum_ref[j]
-        scores = lax.dot_general(
-            c_mat, b_ref[j], (((1,), (1,)), ((), ())), preferred_element_type=F32
-        )
-        row = lax.broadcasted_iota(jnp.int32, (ROWS, ROWS), 0)
-        col = lax.broadcasted_iota(jnp.int32, (ROWS, ROWS), 1)
-        causal = col <= row
-        head_spread = spread_ref[8]
-        xd = (xs * mm(sp, head_spread)).astype(BF)
-        parts = []
-        for h in range(HEADS):
-            lane = HEADS * 8 + h
-            diff = cum[:, lane : lane + 1] - row_ref[j, h : h + 1, :]
-            decay = jnp.exp(jnp.where(causal, diff, -1e30)) * scores
-            parts.append(mm(decay, xd[:, h * HD : (h + 1) * HD]))
-        y = jnp.concatenate(parts, axis=1) * mm(sp, spread_ref[0])
-        y = y + skip_ref[0:1, :] * xs
-        odd = (j % 2).astype(F32)
-        late = (j // 2).astype(F32)
-        one = mm(sp, spread_ref[1]) * mm(jnp.exp(cum), head_spread)
-        y = y + mm(c_mat, s1_ref[(j // 2) * 2]) * (one * odd)
-        two = mm(sp, spread_ref[2]) * mm(e2_ref[j], head_spread)
-        y = y + mm(c_mat, s2_ref[...]) * (two * late)
-        y_ref[j] = y
-
-    each_block(block)
-
-
-def run_intra(part, rows, far_a, far_b, taps, bias, skip, xs, b_mat, sp, cum, e2, row, states, pair, spreads):
-    return run(
+    j = pl.program_id(0)
+    p = part_ref[0] + jnp.dot(rows_ref[0], far_ref[...], preferred_element_type=F32)
+    p = p.astype(BF).astype(F32)
+    z_ref[0] = p[HALO:, :XW].astype(BF)
+    wide_ref[...] = p[:, XW:]
+    c_mat = conv_block(wide_ref, taps_ref, bias_ref).astype(BF)
+    c_ref[0] = c_mat
+    xs = xs_ref[0]
+    sp = sp_ref[0].astype(BF)
+    cum = cum_ref[0]
+    scores = lax.dot_general(
+        c_mat, b_ref[0], (((1,), (1,)), ((), ())), preferred_element_type=F32
+    )
+    row = lax.broadcasted_iota(jnp.int32, (ROWS, ROWS), 0)
+    col = lax.broadcasted_iota(jnp.int32, (ROWS, ROWS), 1)
+    causal = col <= row
+    head_spread = spread_ref[8]
+    xd = (xs * mm(sp, head_spread)).astype(BF)
+    parts = []
+    for h in range(HEADS):
+        lane = HEADS * 8 + h
+        diff = cum[:, lane : lane + 1] - row_ref[0, h : h + 1, :]
+        decay = jnp.exp(jnp.where(causal, diff, -1e30)) * scores
+        parts.append(mm(decay, xd[:, h * HD : (h + 1) * HD]))
+    y = jnp.concatenate(parts, axis=1) * mm(sp, spread_ref[0])
+    y = y + skip_ref[0:1, :] * xs
+    odd = (j % 2).astype(F32)
+    late = (j // 2).astype(F32)
+    one = mm(sp, spread_ref[1]) * mm(jnp.exp(cum), head_spread)
+    y = y + mm(c_mat, s1_ref[0]) * (one * odd)
+    two = mm(sp, spread_ref[2]) * mm(e2_ref[0], head_spread)
+    y = y + mm(c_mat, s2_ref[...]) * (two * late)
+    y_ref[0] = y
+
+
+def run_intra(part, rows, w_far, taps, bias, skip, xs, b_mat, sp, cum, e2, row, states, pair, spreads):
+    whole = lambda *shape: pl.BlockSpec(shape, lambda j: (0,) * len(shape))
+    each = lambda a, b: pl.BlockSpec((1, a, b), lambda j: (j, 0, 0))
+    arrays = (part, rows, w_far, taps, bias, skip, xs, b_mat, sp, cum, e2, row, states, pair, spreads)
+    arrays = [v.value if isinstance(v, Kept) else far(v) for v in arrays]
+    outs = [plain(F32, NY, ROWS, XW), plain(BF, NY, ROWS, NS), plain(BF, NY, ROWS, XW)]
+    results = pl.pallas_call(
         intra_kernel,
-        (),
-        (part, rows, far_a, far_b, taps, bias, skip, xs, b_mat, sp, cum, e2, row, states, pair, spreads),
-        [plain(F32, NY, ROWS, XW), plain(BF, NY, ROWS, NS), plain(BF, NY, ROWS, XW)],
-        [pltpu.VMEM((EXT, NS), F32)],
-        place=lambda v: v,
-        loose=True,
-    )
+        grid=(NY,),
+        in_specs=[
+            each(EXT, WB), each(EXT, KX), whole(KX, WB),
+            whole(4, NS), whole(1, NS), whole(1, XW),
+            each(ROWS, XW), each(ROWS, NS), each(ROWS, 128), each(ROWS, 128), each(ROWS, 128),
+            each(HEADS, ROWS),
+            pl.BlockSpec((1, NS, XW), lambda j: ((j // 2) * 2, 0, 0)),
+            whole(NS, XW), whole(9, 128, XW),
+        ],
+        out_specs=[each(ROWS, XW), each(ROWS, NS), each(ROWS, XW)],
+        out_shape=outs,
+        scratch_shapes=[pltpu.VMEM((EXT, NS), F32)],
+        compiler_params=pltpu.CompilerParams(vmem_limit_bytes=28 << 20),
+        name="intra_block",
+    )(*arrays)
+    return [Kept(v, out) for v, out in zip(results, outs, strict=True)]
 
 
 def merge_kernel(mask_ref, got_ref, own_ref, logs_ref, msg_ref, new_logs_ref, *, k):
@@ -585,10 +599,10 @@
     part_a = run_part(rows, by_a, a_below, a_above, shape_of)
 
     b_below, b_above = near_pair(by_b, X_UP, X_DOWN)
+    w_far = sent(by_b, X_TWO)
     xs, b_mat, sp, cum, e2, sc, row, states, pair, logs, message = run_state(
         part_a, rows_far, fa_a, fb_a, taps_a, bias_a, small_bias, rate, spreads
     )
-    fa_b, fb_b = far_pair(b_below, b_above, X_UP, X_DOWN, KX // 2)
     part_b = run_part(rows, by_b, b_below, b_above, plain)
 
     gots = []
@@ -598,13 +612,14 @@
         gots.append(got)
 
     y_part, c_mat, z_cols = run_intra(
-        part_b, rows_far, fa_b, fb_b, conv_weight[0, :, 2048 + NS :], conv_bias[:, 2048 + NS :], skip,
+        part_b, rows_far, w_far, conv_weight[0, :, 2048 + NS :], conv_bias[:, 2048 + NS :], skip,
         xs, b_mat, sp, cum, e2, row, states, pair, spreads,
     )
     block = lambda k: (y + k) % NY
     order = jnp.stack([block(k) for k in range(NY)])
     q0, q1, q2, q3 = run_cross(order, y_part, c_mat, sc, z_cols, gots, logs, spreads)
-    blocks = (q0, sent(q1, Y_UP), sent(q2, Y_TWO), sent(q3, Y_DOWN))
+    back_two = sent(q2, Y_TWO)
+    blocks = (q0, sent(q1, Y_UP), back_two, sent(q3, Y_DOWN))
     heads_at = jnp.stack([block(0), block(3), block(2), block(1)])
     result = run_out(heads_at, blocks, gate_gain, out_proj[0], acts[0])
     return lax.ppermute(result, "section", [(0, 1), (1, 0)])[None]

time: 168 us -> 174 us (1.036)
  waiting for transfers between devices: 43.8 us -> 53.7 us
  starting transfers between devices: 54.1 us -> 48.9 us
    pallas_call x0 -> x1, Pallas kernels: none -> 10.3 us  [run_intra(): pl.pallas_call(intra_kernel, grid=(NY,), in_specs=[each(EXT, WB), each(EX...]
    pallas_call x22 -> x19, Pallas kernels: 55.6 us -> 45.7 us  [run(): pl.pallas_call(kernel, in_specs=[smem] * len(scalars) + [vmem] * len(arra...]
    ppermute x31 -> x30, waiting for transfers between devices: 41.5 us -> 51.4 us  [sent(): return lax.ppermute(getattr(value, 'value', value), 'seq', pairs)]
    ppermute x31 -> x30, starting transfers between devices: 40.7 us -> 37.6 us  [sent(): return lax.ppermute(getattr(value, 'value', value), 'seq', pairs)]
    ppermute x1, starting transfers between devices: 13.4 us -> 11.3 us  [layer(): return lax.ppermute(result, 'section', [(0, 1), (1, 0)])[None]]
    unnamed x39 -> x25, local copies, waits for them, and re-layouts: 5.66 us -> 4.68 us
  transfers between devices with their start and end apart: 32 -> 31, of which waited for: 10 -> 11; matrix products, arithmetic and copies ran while one was open for 2% -> 3% of each run, Pallas kernels for 30% -> 23%
where the time goes in v2:
time: 174 us; the launch traced here: 173 us
  Pallas kernels  60.9 us (35%)
  waiting for transfers between devices  53.7 us (31%)
  starting transfers between devices  48.9 us (28%)
  local copies, waits for them, and re-layouts  9.18 us (5%)
    ppermute x30, waiting for transfers between devices, sent(): return lax.ppermute(getattr(value, 'value', value), 'seq', pairs)  51.4 us
    pallas_call x19, Pallas kernels, run(): pl.pallas_call(kernel, in_specs=[smem] * len(scalars) + [vmem] * len(arra...  45.7 us
    ppermute x30, starting transfers between devices, sent(): return lax.ppermute(getattr(value, 'value', value), 'seq', pairs)  37.6 us
    ppermute x1, starting transfers between devices, layer(): return lax.ppermute(result, 'section', [(0, 1), (1, 0)])[None]  11.3 us
    pallas_call x1, Pallas kernels, run_intra(): pl.pallas_call(intra_kernel, grid=(NY,), in_specs=[each(EXT, WB), each(EX...  10.3 us
    pallas_call x1, Pallas kernels, run_out(): pl.pallas_call(out_kernel, in_specs=[pl.BlockSpec(memory_space=pltpu.SMEM...  4.92 us
    unnamed x25, local copies, waits for them, and re-layouts  4.68 us
  transfers between devices with their start and end apart: 31, of which 11 were waited for; matrix products, arithmetic and copies ran while one was open for 3% of the time, Pallas kernels for 23%

profile of v2, /device:TPU:1, one launch (start us, length us, event | category | flops | bytes accessed | tf_op | source)
XLA Modules:
  0.0 173.5 jit_solution(9467232987607233607)
XLA Ops:
  0.0 0.9 copy-done.5
  1.0 2.2 %collective-permute-start = (bf16[16,1408]{1,0:T(8,128)(2,1)S(1)}, bf16[16,1408]{1,0:T(8,128)(2,1)S(1)}, u32[]{:S(2)}, u32[]{:S(2)}) collective-permute-start(bf16[16,1408]{1,0:T(8,128)(2,1)S(1)} %get-tuple-element.43), channel_id=1, source_target_pairs={{0,1},{1,2},{2,3},{3,0},{4,5},{5,6},{6,7},{7,4},{8,9},{9,10},{10,1... | collective-permute-start | bytes 135176 | tf_op jit(solution)/shard_map/ppermute | solution.py:59
  3.2 2.6 %collective-permute-start.1 = (bf16[16,1408]{1,0:T(8,128)(2,1)S(1)}, bf16[16,1408]{1,0:T(8,128)(2,1)S(1)}, u32[]{:S(2)}, u32[]{:S(2)}) collective-permute-start(bf16[16,1408]{1,0:T(8,128)(2,1)S(1)} %get-tuple-element.44), channel_id=1, source_target_pairs={{0,2},{1,3},{2,0},{3,1},{4,6},{5,7},{6,4},{7,5},{8,10},{9,11},{10,... | collective-permute-start | bytes 135176 | tf_op jit(solution)/shard_map/ppermute | solution.py:59
  5.8 1.1 collective-permute-start.2
  6.9 0.8 slice_bitcast_fusion
  7.8 2.3 %collective-permute-start.4 = (bf16[16,2048]{1,0:T(8,128)(2,1)S(1)}, bf16[16,2048]{1,0:T(8,128)(2,1)S(1)}, u32[]{:S(2)}, u32[]{:S(2)}) collective-permute-start(bf16[16,2048]{1,0:T(8,128)(2,1)S(1)} %slice_bitcast_fusion), channel_id=1, source_target_pairs={{0,1},{1,2},{2,3},{3,4},{4,5},{5,6},{6,7},{7,8},{8,9},{9,10},{10,1... | collective-permute-start | bytes 196616 | tf_op jit(solution)/shard_map/ppermute | solution.py:59
  10.1 1.3 slice_bitcast_fusion.1
  11.4 1.3 fusion.31
  13.4 1.6 collective-permute-start.3
  15.1 4.0 %collective-permute-start.9 = (bf16[64,1408]{1,0:T(8,128)(2,1)}, bf16[64,1408]{1,0:T(8,128)(2,1)}, u32[]{:S(2)}, u32[]{:S(2)}) collective-permute-start(bf16[64,1408]{1,0:T(8,128)(2,1)} %shard_map.110.refs_0_), channel_id=1, source_target_pairs={{0,28},{1,29},{2,30},{3,31},{4,0},{5,1},{6,2},{7,3},{8,4},{9,5},{1... | collective-permute-start | bytes 540680 | tf_op jit(solution)/shard_map/ppermute | solution.py:59
  19.1 1.2 copy-done.3
  21.0 1.6 shard_map.111.own_ref
  22.7 2.7 %collective-permute-start.6 = (bf16[272,2048]{1,0:T(8,128)(2,1)S(1)}, bf16[272,2048]{1,0:T(8,128)(2,1)S(1)}, u32[]{:S(2)}, u32[]{:S(2)}) collective-permute-start(bf16[272,2048]{1,0:T(8,128)(2,1)S(1)} %shard_map.111.own_ref), channel_id=1, source_target_pairs={{0,3},{1,0},{2,1},{3,2},{4,7},{5,4},{6,5},{7,6},{8,11},{9,8},{10,9... | collective-permute-start | bytes 3342344 | tf_op jit(solution)/shard_map/ppermute | solution.py:59
  25.7 2.7 %collective-permute-start.10 = (bf16[64,1408]{1,0:T(8,128)(2,1)}, bf16[64,1408]{1,0:T(8,128)(2,1)S(1)}, u32[]{:S(2)}, u32[]{:S(2)}) collective-permute-start(bf16[64,1408]{1,0:T(8,128)(2,1)} %collective-permute-done.9.refs_1_), channel_id=1, source_target_pairs={{0,28},{1,29},{2,30},{3,31},{4,0},{5,1},{6,2},{7,3},{8,4},{9,5},{1... | collective-permute-start | bytes 540680 | tf_op jit(solution)/shard_map/ppermute | solution.py:59
  28.4 3.4 %collective-permute-done.12.refs_6_ = bf16[64,1408]{1,0:T(8,128)(2,1)S(1)} collective-permute-done((bf16[64,1408]{1,0:T(8,128)(2,1)}, bf16[64,1408]{1,0:T(8,128)(2,1)S(1)}, u32[]{:S(2)}, u32[]{:S(2)}) %collective-permute-start.12) | collective-permute-done | bytes 180256 | tf_op jit(solution)/shard_map/ppermute | solution.py:59
  31.8 2.7 %collective-permute-start.11 = (bf16[64,1408]{1,0:T(8,128)(2,1)S(1)}, bf16[64,1408]{1,0:T(8,128)(2,1)S(1)}, u32[]{:S(2)}, u32[]{:S(2)}) collective-permute-start(bf16[64,1408]{1,0:T(8,128)(2,1)S(1)} %collective-permute-done.10.refs_2_), channel_id=1, source_target_pairs={{0,28},{1,29},{2,30},{3,31},{4,0},{5,1},{6,2},{7,3},{8,4},{9,5},{1... | collective-permute-start | bytes 540680 | tf_op jit(solution)/shard_map/ppermute | solution.py:59
  34.6 3.2 %collective-permute-done.13.refs_5_ = bf16[64,1408]{1,0:T(8,128)(2,1)S(1)} collective-permute-done((bf16[64,1408]{1,0:T(8,128)(2,1)S(1)}, bf16[64,1408]{1,0:T(8,128)(2,1)S(1)}, u32[]{:S(2)}, u32[]{:S(2)}) %collective-permute-start.13) | collective-permute-done | bytes 180256 | tf_op jit(solution)/shard_map/ppermute | solution.py:59
  37.8 5.9 %collective-permute-done.14.refs_4_ = bf16[64,1408]{1,0:T(8,128)(2,1)S(1)} collective-permute-done((bf16[64,1408]{1,0:T(8,128)(2,1)S(1)}, bf16[64,1408]{1,0:T(8,128)(2,1)S(1)}, u32[]{:S(2)}, u32[]{:S(2)}) %collective-permute-start.14) | collective-permute-done | bytes 180256 | tf_op jit(solution)/shard_map/ppermute | solution.py:59
  43.7 2.3 %shard_map.115 = (bf16[512,768]{1,0:T(8,128)(2,1)}, bf16[512,640]{1,0:T(8,128)(2,1)}) custom-call(bf16[64,1408]{1,0:T(8,128)(2,1)} %shard_map.110.refs_0_, bf16[64,1408]{1,0:T(8,128)(2,1)} %collective-permute-done.9.refs_1_, bf16[64,1408]{1,0:T(8,128)(2,1)S(1)} %collective-permute-done.10.refs_2_, bf16[64,1408]{1,0:T(8,128)(2,1)S(1)} %collective-permute-done.11.refs_3_, ...), custom_call_target="tpu_custom_call" | custom-call | tf_op jit(solution)/shard_map/pallas_call | solution.py:118
  46.0 1.2 collective-permute-start.18
  47.2 1.5 collective-permute-start.19
  48.8 2.1 %shard_map.112 = bf16[144,2048]{1,0:T(8,128)(2,1)} custom-call(bf16[272,2048]{1,0:T(8,128)(2,1)} %collective-permute-done.5.block_ref.below_ref), custom_call_target="tpu_custom_call" | custom-call | tf_op jit(solution)/shard_map/pallas_call | solution.py:118
  51.0 0.8 shard_map.113
  51.9 2.7 %collective-permute-start.8 = (bf16[128,2048]{1,0:T(8,128)(2,1)}, bf16[128,2048]{1,0:T(8,128)(2,1)}, u32[]{:S(2)}, u32[]{:S(2)}) collective-permute-start(bf16[128,2048]{1,0:T(8,128)(2,1)} %shard_map.113), channel_id=1, source_target_pairs={{0,3},{1,0},{2,1},{3,2},{4,7},{5,4},{6,5},{7,6},{8,11},{9,8},{10,9... | collective-permute-start | bytes 1572872 | tf_op jit(solution)/shard_map/ppermute | solution.py:59
  54.6 7.1 %collective-permute-done.18.below_ref.block_ref = bf16[512,768]{1,0:T(8,128)(2,1)} collective-permute-done((bf16[512,768]{1,0:T(8,128)(2,1)}, bf16[512,768]{1,0:T(8,128)(2,1)}, u32[]{:S(2)}, u32[]{:S(2)}) %collective-permute-start.18) | collective-permute-done | bytes 786464 | tf_op jit(solution)/shard_map/ppermute | solution.py:59
  61.7 1.9 %shard_map.118 = bf16[256,768]{1,0:T(8,128)(2,1)} custom-call(bf16[512,768]{1,0:T(8,128)(2,1)} %collective-permute-done.18.below_ref.block_ref), custom_call_target="tpu_custom_call" | custom-call | tf_op jit(solution)/shard_map/pallas_call | solution.py:118
  63.7 1.9 %shard_map.119 = bf16[256,768]{1,0:T(8,128)(2,1)} custom-call(bf16[512,768]{1,0:T(8,128)(2,1)} %collective-permute-done.19.above_ref.block_ref), custom_call_target="tpu_custom_call" | custom-call | tf_op jit(solution)/shard_map/pallas_call | solution.py:118
  65.5 2.7 %collective-permute-start.21 = (bf16[256,768]{1,0:T(8,128)(2,1)}, bf16[256,768]{1,0:T(8,128)(2,1)}, u32[]{:S(2)}, u32[]{:S(2)}) collective-permute-start(bf16[256,768]{1,0:T(8,128)(2,1)} %shard_map.119), channel_id=1, source_target_pairs={{0,96},{1,97},{2,98},{3,99},{4,100},{5,101},{6,102},{7,103},{8,104... | collective-permute-start | bytes 1179656 | tf_op jit(solution)/shard_map/ppermute | solution.py:59
  68.4 4.3 %shard_map.114 = (bf16[4,272,1536]{2,1,0:T(8,128)(2,1)}, bf16[4,272,512]{2,1,0:T(8,128)(2,1)}) custom-call(s32[1]{0:T(128)} %bitcast.y_ref, bf16[272,2048]{1,0:T(8,128)(2,1)S(1)} %shard_map.111.own_ref, bf16[272,2048]{1,0:T(8,128)(2,1)} %collective-permute-done.5.block_ref.below_ref, bf16[272,2048]{1,0:T(8,128)(2,1)S(1)} %collective-permute-done.6.block_ref.above_ref, ...), custom_call_target="tpu_custom_call" | custom-call | tf_op jit(solution)/shard_map/pallas_call | solution.py:118
  72.7 5.9 %shard_map.117.part_ref = f32[4,272,768]{2,1,0:T(8,128)S(1)} custom-call(bf16[4,272,1536]{2,1,0:T(8,128)(2,1)} %get-tuple-element.47.rows_ref, bf16[512,768]{1,0:T(8,128)(2,1)} %get-tuple-element.50.own_ref, bf16[512,768]{1,0:T(8,128)(2,1)} %collective-permute-done.18.below_ref.block_ref, bf16[512,768]{1,0:T(8,128)(2,1)} %collective-permute-done.19.above_ref.block_ref), custom_call_target="tpu_custom_call" | custom-call | tf_op jit(solution)/shard_map/pallas_call | solution.py:118
  78.6 10.2 %shard_map.120 = (f32[4,256,512]{2,1,0:T(8,128)}, bf16[4,256,128]{2,1,0:T(8,128)(2,1)}, f32[4,256,128]{2,1,0:T(8,128)}, f32[4,256,128]{2,1,0:T(8,128)}, f32[4,25...) custom-call(f32[4,272,768]{2,1,0:T(8,128)S(1)} %shard_map.117.part_r, ...), custom_call_target="tpu_custom_call" | custom-call | tf_op jit(solution)/shard_map/pallas_call | solution.py:118
  89.5 3.3 %collective-permute-done.22.got_ref.g3 = bf16[144,512]{1,0:T(8,128)(2,1)S(1)} collective-permute-done((bf16[144,512]{1,0:T(8,128)(2,1)S(1)}, bf16[144,512]{1,0:T(8,128)(2,1)S(1)}, u32[]{:S(2)}, u32[]{:S(2)}) %collective-permute-start.22) | collective-permute-done | bytes 147488 | tf_op jit(solution)/shard_map/ppermute | solution.py:59
  93.1 2.7 %collective-permute-start.16 = (bf16[512,640]{1,0:T(8,128)(2,1)}, bf16[512,640]{1,0:T(8,128)(2,1)S(1)}, u32[]{:S(2)}, u32[]{:S(2)}) collective-permute-start(bf16[512,640]{1,0:T(8,128)(2,1)} %get-tuple-element.48.own_ref), channel_id=1, source_target_pairs={{0,96},{1,97},{2,98},{3,99},{4,100},{5,101},{6,102},{7,103},{8,104... | collective-permute-start | bytes 1966088 | tf_op jit(solution)/shard_map/ppermute | solution.py:59
  95.7 3.5 %collective-permute-done.23.got_ref.g4 = bf16[144,512]{1,0:T(8,128)(2,1)S(1)} collective-permute-done((bf16[144,512]{1,0:T(8,128)(2,1)S(1)}, bf16[144,512]{1,0:T(8,128)(2,1)S(1)}, u32[]{:S(2)}, u32[]{:S(2)}) %collective-permute-start.23) | collective-permute-done | bytes 147488 | tf_op jit(solution)/shard_map/ppermute | solution.py:59
  99.3 1.0 collective-permute-start.24
  100.3 5.5 %collective-permute-done.24.got_ref.g5 = bf16[144,512]{1,0:T(8,128)(2,1)S(1)} collective-permute-done((bf16[144,512]{1,0:T(8,128)(2,1)S(1)}, bf16[144,512]{1,0:T(8,128)(2,1)S(1)}, u32[]{:S(2)}, u32[]{:S(2)}) %collective-permute-start.24) | collective-permute-done | bytes 147488 | tf_op jit(solution)/shard_map/ppermute | solution.py:59
  106.0 12.3 %collective-permute-done.25.got_ref.g6 = bf16[144,512]{1,0:T(8,128)(2,1)S(1)} collective-permute-done((bf16[144,512]{1,0:T(8,128)(2,1)S(1)}, bf16[144,512]{1,0:T(8,128)(2,1)S(1)}, u32[]{:S(2)}, u32[]{:S(2)}) %collective-permute-start.25) | collective-permute-done | bytes 147488 | tf_op jit(solution)/shard_map/ppermute | solution.py:59
  119.9 7.0 %shard_map.116.part_ref = f32[4,272,640]{2,1,0:T(8,128)} custom-call(bf16[4,272,1536]{2,1,0:T(8,128)(2,1)} %get-tuple-element.47.rows_ref, bf16[512,640]{1,0:T(8,128)(2,1)} %get-tuple-element.48.own_ref, bf16[512,640]{1,0:T(8,128)(2,1)S(1)} %collective-permute-done.15.below_ref, bf16[512,640]{1,0:T(8,128)(2,1)S(1)} %collective-permute-done.16.above_ref), custom_call_target="tpu_custom_call" | custom-call | tf_op jit(solution)/shard_map/pallas_call | solution.py:118
  126.9 0.8 copy-done.8
  127.7 10.3 %intra_block.1 = (f32[4,256,512]{2,1,0:T(8,128)}, bf16[4,256,128]{2,1,0:T(8,128)(2,1)}, bf16[4,256,512]{2,1,0:T(8,128)(2,1)}) custom-call(f32[4,272,640]{2,1,0:T(8,128)} %shard_map.116.part_ref, bf16[4,272,512]{2,1,0:T(8,128)(2,1)} %get-tuple-element.49.rows_ref, bf16[512,640]{1,0:T(8,128)(2,1)} %copy-done.8, f32[4,128]{1,0:T(4,128)} %get-tuple-element.80.taps_ref, ...), custom_call_target="tpu_custom_call" | custom-call | tf_op jit(solution)/shard_map/intra_block/pallas_call | solution.py:313
  138.0 0.7 shard_map.126
  138.8 5.3 %shard_map.127 = (bf16[256,512]{1,0:T(8,128)(2,1)S(1)}, bf16[256,512]{1,0:T(8,128)(2,1)S(1)}, bf16[256,512]{1,0:T(8,128)(2,1)S(1)}, bf16[256,512]{1,0:T(8,128)(2,1)S(1)}) custom-call(s32[4]{0:T(128)S(1)} %pad_add_fusion.1.at_ref, f32[4,256,512]{2,1,0:T(8,128)} %get-tuple-element.60.y_ref, bf16[4,256,128]{2,1,0:T(8,128)(2,1)} %get-tuple-element.61.c_ref, ...), custom_call_target="tpu_custom_call" | custom-call | tf_op jit(solution)/shard_map/pallas_call | solution.py:118
  144.1 2.2 %collective-permute-start.28 = (bf16[256,512]{1,0:T(8,128)(2,1)S(1)}, bf16[256,512]{1,0:T(8,128)(2,1)S(1)}, u32[]{:S(2)}, u32[]{:S(2)}) collective-permute-start(bf16[256,512]{1,0:T(8,128)(2,1)S(1)} %get-tuple-element.77), channel_id=1, source_target_pairs={{0,2},{1,3},{2,0},{3,1},{4,6},{5,7},{6,4},{7,5},{8,10},{9,11},{10,... | collective-permute-start | bytes 786440 | tf_op jit(solution)/shard_map/ppermute | solution.py:59
  146.9 6.5 %collective-permute-done.27.q1 = bf16[256,512]{1,0:T(8,128)(2,1)S(1)} collective-permute-done((bf16[256,512]{1,0:T(8,128)(2,1)S(1)}, bf16[256,512]{1,0:T(8,128)(2,1)S(1)}, u32[]{:S(2)}, u32[]{:S(2)}) %collective-permute-start.27) | collective-permute-done | bytes 262176 | tf_op jit(solution)/shard_map/ppermute | solution.py:59
  154.0 4.9 %gate_out.1 = bf16[256,2048]{1,0:T(8,128)(2,1)S(1)} custom-call(s32[4]{0:T(128)S(1)} %pad_add_fusion.at_ref, bf16[256,512]{1,0:T(8,128)(2,1)S(1)} %get-tuple-element.75.q0, bf16[256,512]{1,0:T(8,128)(2,1)S(1)} %collective-permute-done.27.q1, bf16[256,512]{1,0:T(8,128)(2,1)S(1)} %collective-permute-done.28.q2, ...), custom_call_target="tpu_custom_call" | custom-call | tf_op jit(solution)/shard_map/gate_out/pallas_call | solution.py:413
  158.9 11.3 %collective-permute-start.30 = (bf16[256,2048]{1,0:T(8,128)(2,1)S(1)}, bf16[256,2048]{1,0:T(8,128)(2,1)S(1)}, u32[]{:S(2)}, u32[]{:S(2)}) collective-permute-start(bf16[256,2048]{1,0:T(8,128)(2,1)S(1)} %gate_out.1), channel_id=1, source_target_pairs={{0,128},{128,0},{1,129},{129,1},{2,130},{130,2},{3,131},{131,3},{4... | collective-permute-start | bytes 3145736 | tf_op jit(solution)/shard_map/ppermute | solution.py:625
  170.2 2.3 %collective-permute-done.30 = bf16[256,2048]{1,0:T(8,128)(2,1)S(1)} collective-permute-done((bf16[256,2048]{1,0:T(8,128)(2,1)S(1)}, bf16[256,2048]{1,0:T(8,128)(2,1)S(1)}, u32[]{:S(2)}, u32[]{:S(2)}) %collective-permute-start.30) | collective-permute-done | bytes 1048608 | tf_op jit(solution)/shard_map/ppermute | solution.py:625
  172.5 1.0 copy.21
  (94 shorter events, 6.4 us)
Async XLA Ops:
  0.0 54.5 %copy-start = (f32[1,256]{1,0:T(1,128)S(1)}, f32[1,256]{1,0:T(1,128)}, u32[]{:S(2)}) copy-start(f32[1,256]{1,0:T(1,128)} %param.19) | copy-start | bytes 3076
  0.0 0.9 copy-start.5
  1.0 11.7 %collective-permute-start = (bf16[16,1408]{1,0:T(8,128)(2,1)S(1)}, bf16[16,1408]{1,0:T(8,128)(2,1)S(1)}, u32[]{:S(2)}, u32[]{:S(2)}) collective-permute-start(bf16[16,1408]{1,0:T(8,128)(2,1)S(1)} %get-tuple-element.43), channel_id=1, source_target_pairs={{0,1},{1,2},{2,3},{3,0},{4,5},{5,6},{6,7},{7,4},{8,9},{9,10},{10,1... | collective-permute-start | bytes 135176 | tf_op jit(solution)/shard_map/ppermute | solution.py:59
  3.2 9.5 %collective-permute-start.1 = (bf16[16,1408]{1,0:T(8,128)(2,1)S(1)}, bf16[16,1408]{1,0:T(8,128)(2,1)S(1)}, u32[]{:S(2)}, u32[]{:S(2)}) collective-permute-start(bf16[16,1408]{1,0:T(8,128)(2,1)S(1)} %get-tuple-element.44), channel_id=1, source_target_pairs={{0,2},{1,3},{2,0},{3,1},{4,6},{5,7},{6,4},{7,5},{8,10},{9,11},{10,... | collective-permute-start | bytes 135176 | tf_op jit(solution)/shard_map/ppermute | solution.py:59
  5.8 6.9 %collective-permute-start.2 = (bf16[16,1408]{1,0:T(8,128)(2,1)S(1)}, bf16[16,1408]{1,0:T(8,128)(2,1)S(1)}, u32[]{:S(2)}, u32[]{:S(2)}) collective-permute-start(bf16[16,1408]{1,0:T(8,128)(2,1)S(1)} %get-tuple-element.45), channel_id=1, source_target_pairs={{0,3},{1,0},{2,1},{3,2},{4,7},{5,4},{6,5},{7,6},{8,11},{9,8},{10,9... | collective-permute-start | bytes 135176 | tf_op jit(solution)/shard_map/ppermute | solution.py:59
  7.8 11.3 %collective-permute-start.4 = (bf16[16,2048]{1,0:T(8,128)(2,1)S(1)}, bf16[16,2048]{1,0:T(8,128)(2,1)S(1)}, u32[]{:S(2)}, u32[]{:S(2)}) collective-permute-start(bf16[16,2048]{1,0:T(8,128)(2,1)S(1)} %slice_bitcast_fusion), channel_id=1, source_target_pairs={{0,1},{1,2},{2,3},{3,4},{4,5},{5,6},{6,7},{7,8},{8,9},{9,10},{10,1... | collective-permute-start | bytes 196616 | tf_op jit(solution)/shard_map/ppermute | solution.py:59
  13.4 12.0 %collective-permute-start.3 = (bf16[64,1408]{1,0:T(8,128)(2,1)}, bf16[64,1408]{1,0:T(8,128)(2,1)}, u32[]{:S(2)}, u32[]{:S(2)}) collective-permute-start(bf16[64,1408]{1,0:T(8,128)(2,1)} %shard_map.110.refs_0_), channel_id=1, source_target_pairs={{0,4},{1,5},{2,6},{3,7},{4,8},{5,9},{6,10},{7,11},{8,12},{9,13},{1... | collective-permute-start | bytes 540680 | tf_op jit(solution)/shard_map/ppermute | solution.py:59
  15.1 10.6 %collective-permute-start.9 = (bf16[64,1408]{1,0:T(8,128)(2,1)}, bf16[64,1408]{1,0:T(8,128)(2,1)}, u32[]{:S(2)}, u32[]{:S(2)}) collective-permute-start(bf16[64,1408]{1,0:T(8,128)(2,1)} %shard_map.110.refs_0_), channel_id=1, source_target_pairs={{0,28},{1,29},{2,30},{3,31},{4,0},{5,1},{6,2},{7,3},{8,4},{9,5},{1... | collective-permute-start | bytes 540680 | tf_op jit(solution)/shard_map/ppermute | solution.py:59
  19.1 1.2 copy-start.3
  20.3 0.7 copy-start.6
  21.0 7.4 %slice-start = ((f32[1,4,2304]{2,1,0:T(4,128)}), f32[1,4,2048]{2,1,0:T(4,128)S(1)}, s32[]{:S(2)}) async-start(f32[1,4,2304]{2,1,0:T(4,128)} %param.14), calls=%async_computation | async-start | bytes 65536 | tf_op jit(solution)/shard_map/slice | solution.py:579
  21.0 7.4 %slice-start.1 = ((f32[1,2304]{1,0:T(1,128)}), f32[1,2048]{1,0:T(1,128)S(1)}, s32[]{:S(2)}) async-start(f32[1,2304]{1,0:T(1,128)} %param.15), calls=%async_computation.1 | async-start | bytes 16384 | tf_op jit(solution)/shard_map/slice | solution.py:582
  22.7 26.2 %collective-permute-start.5 = (bf16[272,2048]{1,0:T(8,128)(2,1)S(1)}, bf16[272,2048]{1,0:T(8,128)(2,1)}, u32[]{:S(2)}, u32[]{:S(2)}) collective-permute-start(bf16[272,2048]{1,0:T(8,128)(2,1)S(1)} %shard_map.111.own_ref), channel_id=1, source_target_pairs={{0,1},{1,2},{2,3},{3,0},{4,5},{5,6},{6,7},{7,4},{8,9},{9,10},{10,1... | collective-permute-start | bytes 3342344 | tf_op jit(solution)/shard_map/ppermute | solution.py:59
  22.7 28.3 %collective-permute-start.6 = (bf16[272,2048]{1,0:T(8,128)(2,1)S(1)}, bf16[272,2048]{1,0:T(8,128)(2,1)S(1)}, u32[]{:S(2)}, u32[]{:S(2)}) collective-permute-start(bf16[272,2048]{1,0:T(8,128)(2,1)S(1)} %shard_map.111.own_ref), channel_id=1, source_target_pairs={{0,3},{1,0},{2,1},{3,2},{4,7},{5,4},{6,5},{7,6},{8,11},{9,8},{10,9... | collective-permute-start | bytes 3342344 | tf_op jit(solution)/shard_map/ppermute | solution.py:59
  25.5 6.2 %collective-permute-start.12 = (bf16[64,1408]{1,0:T(8,128)(2,1)}, bf16[64,1408]{1,0:T(8,128)(2,1)S(1)}, u32[]{:S(2)}, u32[]{:S(2)}) collective-permute-start(bf16[64,1408]{1,0:T(8,128)(2,1)} %collective-permute-done.3.refs_7_), channel_id=1, source_target_pairs={{0,4},{1,5},{2,6},{3,7},{4,8},{5,9},{6,10},{7,11},{8,12},{9,13},{1... | collective-permute-start | bytes 540680 | tf_op jit(solution)/shard_map/ppermute | solution.py:59
  25.7 6.1 %collective-permute-start.10 = (bf16[64,1408]{1,0:T(8,128)(2,1)}, bf16[64,1408]{1,0:T(8,128)(2,1)S(1)}, u32[]{:S(2)}, u32[]{:S(2)}) collective-permute-start(bf16[64,1408]{1,0:T(8,128)(2,1)} %collective-permute-done.9.refs_1_), channel_id=1, source_target_pairs={{0,28},{1,29},{2,30},{3,31},{4,0},{5,1},{6,2},{7,3},{8,4},{9,5},{1... | collective-permute-start | bytes 540680 | tf_op jit(solution)/shard_map/ppermute | solution.py:59
  31.8 6.0 %collective-permute-start.13 = (bf16[64,1408]{1,0:T(8,128)(2,1)S(1)}, bf16[64,1408]{1,0:T(8,128)(2,1)S(1)}, u32[]{:S(2)}, u32[]{:S(2)}) collective-permute-start(bf16[64,1408]{1,0:T(8,128)(2,1)S(1)} %collective-permute-done.12.refs_6_), channel_id=1, source_target_pairs={{0,4},{1,5},{2,6},{3,7},{4,8},{5,9},{6,10},{7,11},{8,12},{9,13},{1... | collective-permute-start | bytes 540680 | tf_op jit(solution)/shard_map/ppermute | solution.py:59
  31.8 5.9 %collective-permute-start.11 = (bf16[64,1408]{1,0:T(8,128)(2,1)S(1)}, bf16[64,1408]{1,0:T(8,128)(2,1)S(1)}, u32[]{:S(2)}, u32[]{:S(2)}) collective-permute-start(bf16[64,1408]{1,0:T(8,128)(2,1)S(1)} %collective-permute-done.10.refs_2_), channel_id=1, source_target_pairs={{0,28},{1,29},{2,30},{3,31},{4,0},{5,1},{6,2},{7,3},{8,4},{9,5},{1... | collective-permute-start | bytes 540680 | tf_op jit(solution)/shard_map/ppermute | solution.py:59
  37.7 6.0 %collective-permute-start.14 = (bf16[64,1408]{1,0:T(8,128)(2,1)S(1)}, bf16[64,1408]{1,0:T(8,128)(2,1)S(1)}, u32[]{:S(2)}, u32[]{:S(2)}) collective-permute-start(bf16[64,1408]{1,0:T(8,128)(2,1)S(1)} %collective-permute-done.13.refs_5_), channel_id=1, source_target_pairs={{0,4},{1,5},{2,6},{3,7},{4,8},{5,9},{6,10},{7,11},{8,12},{9,13},{1... | collective-permute-start | bytes 540680 | tf_op jit(solution)/shard_map/ppermute | solution.py:59
  46.0 5.0 %copy-start.9 = (f32[1,32]{1,0:T(1,128)S(1)}, f32[1,32]{1,0:T(1,128)}, u32[]{:S(2)}) copy-start(f32[1,32]{1,0:T(1,128)} %param.17) | copy-start | bytes 388
  46.0 5.0 %copy-start.10 = (f32[1,32]{1,0:T(1,128)S(1)}, f32[1,32]{1,0:T(1,128)}, u32[]{:S(2)}) copy-start(f32[1,32]{1,0:T(1,128)} %param.16) | copy-start | bytes 388
  46.0 15.7 %collective-permute-start.18 = (bf16[512,768]{1,0:T(8,128)(2,1)}, bf16[512,768]{1,0:T(8,128)(2,1)}, u32[]{:S(2)}, u32[]{:S(2)}) collective-permute-start(bf16[512,768]{1,0:T(8,128)(2,1)} %get-tuple-element.50.own_ref), channel_id=1, source_target_pairs={{0,32},{1,33},{2,34},{3,35},{4,36},{5,37},{6,38},{7,39},{8,40},{9,... | collective-permute-start | bytes 2359304 | tf_op jit(solution)/shard_map/ppermute | solution.py:59
  47.2 16.4 %collective-permute-start.19 = (bf16[512,768]{1,0:T(8,128)(2,1)}, bf16[512,768]{1,0:T(8,128)(2,1)}, u32[]{:S(2)}, u32[]{:S(2)}) collective-permute-start(bf16[512,768]{1,0:T(8,128)(2,1)} %get-tuple-element.50.own_ref), channel_id=1, source_target_pairs={{0,96},{1,97},{2,98},{3,99},{4,100},{5,101},{6,102},{7,103},{8,104... | collective-permute-start | bytes 2359304 | tf_op jit(solution)/shard_map/ppermute | solution.py:59
  50.9 17.4 %collective-permute-start.7 = (bf16[144,2048]{1,0:T(8,128)(2,1)}, bf16[144,2048]{1,0:T(8,128)(2,1)}, u32[]{:S(2)}, u32[]{:S(2)}) collective-permute-start(bf16[144,2048]{1,0:T(8,128)(2,1)} %shard_map.112), channel_id=1, source_target_pairs={{0,1},{1,2},{2,3},{3,0},{4,5},{5,6},{6,7},{7,4},{8,9},{9,10},{10,1... | collective-permute-start | bytes 1769480 | tf_op jit(solution)/shard_map/ppermute | solution.py:59
  51.9 16.5 %collective-permute-start.8 = (bf16[128,2048]{1,0:T(8,128)(2,1)}, bf16[128,2048]{1,0:T(8,128)(2,1)}, u32[]{:S(2)}, u32[]{:S(2)}) collective-permute-start(bf16[128,2048]{1,0:T(8,128)(2,1)} %shard_map.113), channel_id=1, source_target_pairs={{0,3},{1,0},{2,1},{3,2},{4,7},{5,4},{6,5},{7,6},{8,11},{9,8},{10,9... | collective-permute-start | bytes 1572872 | tf_op jit(solution)/shard_map/ppermute | solution.py:59
  63.6 14.9 %collective-permute-start.20 = (bf16[256,768]{1,0:T(8,128)(2,1)}, bf16[256,768]{1,0:T(8,128)(2,1)}, u32[]{:S(2)}, u32[]{:S(2)}) collective-permute-start(bf16[256,768]{1,0:T(8,128)(2,1)} %shard_map.118), channel_id=1, source_target_pairs={{0,32},{1,33},{2,34},{3,35},{4,36},{5,37},{6,38},{7,39},{8,40},{9,... | collective-permute-start | bytes 1179656 | tf_op jit(solution)/shard_map/ppermute | solution.py:59
  65.5 13.1 %collective-permute-start.21 = (bf16[256,768]{1,0:T(8,128)(2,1)}, bf16[256,768]{1,0:T(8,128)(2,1)}, u32[]{:S(2)}, u32[]{:S(2)}) collective-permute-start(bf16[256,768]{1,0:T(8,128)(2,1)} %shard_map.119), channel_id=1, source_target_pairs={{0,96},{1,97},{2,98},{3,99},{4,100},{5,101},{6,102},{7,103},{8,104... | collective-permute-start | bytes 1179656 | tf_op jit(solution)/shard_map/ppermute | solution.py:59
  68.3 10.3 %copy-start.1 = (bf16[9,128,512]{2,1,0:T(8,128)(2,1)}, bf16[9,128,512]{2,1,0:T(8,128)(2,1)S(1)}, u32[]{:S(2)}) copy-start(bf16[9,128,512]{2,1,0:T(8,128)(2,1)S(1)} %fusion.25.spread_ref) | copy-start | bytes 3538948
  88.8 30.3 %copy-start.11 = (f32[1,32]{1,0:T(1,128)S(1)}, f32[1,32]{1,0:T(1,128)}, u32[]{:S(2)}) copy-start(f32[1,32]{1,0:T(1,128)} %param.18) | copy-start | bytes 388
  88.8 4.0 %collective-permute-start.22 = (bf16[144,512]{1,0:T(8,128)(2,1)S(1)}, bf16[144,512]{1,0:T(8,128)(2,1)S(1)}, u32[]{:S(2)}, u32[]{:S(2)}) collective-permute-start(bf16[144,512]{1,0:T(8,128)(2,1)S(1)} %get-tuple-element.64.own_ref), channel_id=1, source_target_pairs={{0,4},{1,5},{2,6},{3,7},{4,0},{5,1},{6,2},{7,3},{8,12},{9,13},{10,... | collective-permute-start | bytes 442376 | tf_op jit(solution)/shard_map/ppermute | solution.py:59
  92.9 6.4 %collective-permute-start.23 = (bf16[144,512]{1,0:T(8,128)(2,1)S(1)}, bf16[144,512]{1,0:T(8,128)(2,1)S(1)}, u32[]{:S(2)}, u32[]{:S(2)}) collective-permute-start(bf16[144,512]{1,0:T(8,128)(2,1)S(1)} %get-tuple-element.66.own_ref), channel_id=1, source_target_pairs={{0,8},{1,9},{2,10},{3,11},{4,12},{5,13},{6,14},{7,15},{8,0},{9,1},... | collective-permute-start | bytes 442376 | tf_op jit(solution)/shard_map/ppermute | solution.py:59
  93.0 26.9 %collective-permute-start.15 = (bf16[512,640]{1,0:T(8,128)(2,1)}, bf16[512,640]{1,0:T(8,128)(2,1)S(1)}, u32[]{:S(2)}, u32[]{:S(2)}) collective-permute-start(bf16[512,640]{1,0:T(8,128)(2,1)} %get-tuple-element.48.own_ref), channel_id=1, source_target_pairs={{0,32},{1,33},{2,34},{3,35},{4,36},{5,37},{6,38},{7,39},{8,40},{9,... | collective-permute-start | bytes 1966088 | tf_op jit(solution)/shard_map/ppermute | solution.py:59
  93.1 26.8 %collective-permute-start.16 = (bf16[512,640]{1,0:T(8,128)(2,1)}, bf16[512,640]{1,0:T(8,128)(2,1)S(1)}, u32[]{:S(2)}, u32[]{:S(2)}) collective-permute-start(bf16[512,640]{1,0:T(8,128)(2,1)} %get-tuple-element.48.own_ref), channel_id=1, source_target_pairs={{0,96},{1,97},{2,98},{3,99},{4,100},{5,101},{6,102},{7,103},{8,104... | collective-permute-start | bytes 1966088 | tf_op jit(solution)/shard_map/ppermute | solution.py:59
  95.7 31.1 %collective-permute-start.17 = (bf16[512,640]{1,0:T(8,128)(2,1)}, bf16[512,640]{1,0:T(8,128)(2,1)S(1)}, u32[]{:S(2)}, u32[]{:S(2)}) collective-permute-start(bf16[512,640]{1,0:T(8,128)(2,1)} %get-tuple-element.48.own_ref), channel_id=1, source_target_pairs={{0,64},{1,65},{2,66},{3,67},{4,68},{5,69},{6,70},{7,71},{8,72},{9,... | collective-permute-start | bytes 1966088 | tf_op jit(solution)/shard_map/ppermute | solution.py:59
  99.3 6.5 %collective-permute-start.24 = (bf16[144,512]{1,0:T(8,128)(2,1)S(1)}, bf16[144,512]{1,0:T(8,128)(2,1)S(1)}, u32[]{:S(2)}, u32[]{:S(2)}) collective-permute-start(bf16[144,512]{1,0:T(8,128)(2,1)S(1)} %get-tuple-element.68.own_ref), channel_id=1, source_target_pairs={{0,28},{1,29},{2,30},{3,31},{4,24},{5,25},{6,26},{7,27},{8,20},{9,... | collective-permute-start | bytes 442376 | tf_op jit(solution)/shard_map/ppermute | solution.py:59
  105.9 12.4 %collective-permute-start.25 = (bf16[144,512]{1,0:T(8,128)(2,1)S(1)}, bf16[144,512]{1,0:T(8,128)(2,1)S(1)}, u32[]{:S(2)}, u32[]{:S(2)}) collective-permute-start(bf16[144,512]{1,0:T(8,128)(2,1)S(1)} %get-tuple-element.70.own_ref), channel_id=1, source_target_pairs={{0,32},{1,33},{2,34},{3,35},{4,36},{5,37},{6,38},{7,39},{8,40},{9,... | collective-permute-start | bytes 442376 | tf_op jit(solution)/shard_map/ppermute | solution.py:59
  118.4 19.6 %collective-permute-start.26 = (bf16[144,512]{1,0:T(8,128)(2,1)S(1)}, bf16[144,512]{1,0:T(8,128)(2,1)S(1)}, u32[]{:S(2)}, u32[]{:S(2)}) collective-permute-start(bf16[144,512]{1,0:T(8,128)(2,1)S(1)} %get-tuple-element.72.own_ref), channel_id=1, source_target_pairs={{0,96},{1,97},{2,98},{3,99},{4,100},{5,101},{6,102},{7,103},{8,104... | collective-permute-start | bytes 442376 | tf_op jit(solution)/shard_map/ppermute | solution.py:59
  126.9 0.8 copy-start.8
  127.7 11.1 %copy-start.2 = (bf16[9,128,512]{2,1,0:T(8,128)(2,1)S(1)}, bf16[9,128,512]{2,1,0:T(8,128)(2,1)}, u32[]{:S(2)}) copy-start(bf16[9,128,512]{2,1,0:T(8,128)(2,1)} %copy-done.1) | copy-start | bytes 3538948
  138.8 15.2 %copy-start.4 = (bf16[1,256,2048]{2,1,0:T(8,128)(2,1)S(1)}, bf16[1,256,2048]{2,1,0:T(8,128)(2,1)}, u32[]{:S(2)}) copy-start(bf16[1,256,2048]{2,1,0:T(8,128)(2,1)} %param.11) | copy-start | bytes 3145732
  138.8 15.2 %copy-start.7 = (f32[1,2048]{1,0:T(1,128)S(1)}, f32[1,2048]{1,0:T(1,128)}, u32[]{:S(2)}) copy-start(f32[1,2048]{1,0:T(1,128)} %gain_ref.3) | copy-start | bytes 24580
  144.0 9.3 %collective-permute-start.27 = (bf16[256,512]{1,0:T(8,128)(2,1)S(1)}, bf16[256,512]{1,0:T(8,128)(2,1)S(1)}, u32[]{:S(2)}, u32[]{:S(2)}) collective-permute-start(bf16[256,512]{1,0:T(8,128)(2,1)S(1)} %get-tuple-element.76), channel_id=1, source_target_pairs={{0,1},{1,2},{2,3},{3,0},{4,5},{5,6},{6,7},{7,4},{8,9},{9,10},{10,1... | collective-permute-start | bytes 786440 | tf_op jit(solution)/shard_map/ppermute | solution.py:59
  144.1 9.2 %collective-permute-start.28 = (bf16[256,512]{1,0:T(8,128)(2,1)S(1)}, bf16[256,512]{1,0:T(8,128)(2,1)S(1)}, u32[]{:S(2)}, u32[]{:S(2)}) collective-permute-start(bf16[256,512]{1,0:T(8,128)(2,1)S(1)} %get-tuple-element.77), channel_id=1, source_target_pairs={{0,2},{1,3},{2,0},{3,1},{4,6},{5,7},{6,4},{7,5},{8,10},{9,11},{10,... | collective-permute-start | bytes 786440 | tf_op jit(solution)/shard_map/ppermute | solution.py:59
  146.3 7.7 %collective-permute-start.29 = (bf16[256,512]{1,0:T(8,128)(2,1)S(1)}, bf16[256,512]{1,0:T(8,128)(2,1)S(1)}, u32[]{:S(2)}, u32[]{:S(2)}) collective-permute-start(bf16[256,512]{1,0:T(8,128)(2,1)S(1)} %get-tuple-element.78), channel_id=1, source_target_pairs={{0,3},{1,0},{2,1},{3,2},{4,7},{5,4},{6,5},{7,6},{8,11},{9,8},{10,9... | collective-permute-start | bytes 786440 | tf_op jit(solution)/shard_map/ppermute | solution.py:59
  158.9 13.6 %collective-permute-start.30 = (bf16[256,2048]{1,0:T(8,128)(2,1)S(1)}, bf16[256,2048]{1,0:T(8,128)(2,1)S(1)}, u32[]{:S(2)}, u32[]{:S(2)}) collective-permute-start(bf16[256,2048]{1,0:T(8,128)(2,1)S(1)} %gate_out.1), channel_id=1, source_target_pairs={{0,128},{128,0},{1,129},{129,1},{2,130},{130,2},{3,131},{131,3},{4... | collective-permute-start | bytes 3145736 | tf_op jit(solution)/shard_map/ppermute | solution.py:625

commit v3 on v2

--- a/solution.py
+++ b/solution.py
@@ -59,10 +59,12 @@
     return lax.ppermute(getattr(value, "value", value), "seq", pairs)
 
 
-def spread(first, stride):
+def spread_kernel(out_ref):
     row = lax.broadcasted_iota(jnp.int32, (128, XW), 0)
-    col = lax.broadcasted_iota(jnp.int32, (128, XW), 1)
-    return jnp.where(row == first + stride * (col // HD), 1.0, 0.0).astype(BF)
+    head = lax.broadcasted_iota(jnp.int32, (128, XW), 1) // HD
+    for k in range(9):
+        lane = HEADS * 8 + head if k == 8 else k + 8 * head
+        out_ref[k] = jnp.where(row == lane, 1.0, 0.0).astype(BF)
 
 
 def mm(a, b):
@@ -267,9 +269,9 @@
 def intra_kernel(
     part_ref, rows_ref, far_ref, taps_ref, bias_ref, skip_ref,
     xs_ref, b_ref, sp_ref, cum_ref, e2_ref, row_ref, s1_ref, s2_ref, spread_ref,
-    y_ref, c_ref, z_ref, wide_ref,
+    y_ref, c_ref, z_ref, wide_ref, *, base,
 ):
-    j = pl.program_id(0)
+    j = pl.program_id(0) + base
     p = part_ref[0] + jnp.dot(rows_ref[0], far_ref[...], preferred_element_type=F32)
     p = p.astype(BF).astype(F32)
     z_ref[0] = p[HALO:, :XW].astype(BF)
@@ -304,24 +306,26 @@
     y_ref[0] = y
 
 
-def run_intra(part, rows, w_far, taps, bias, skip, xs, b_mat, sp, cum, e2, row, states, pair, spreads):
+def run_intra(base, part, rows, w_far, taps, bias, skip, xs, b_mat, sp, cum, e2, row, states, pair, spreads):
     whole = lambda *shape: pl.BlockSpec(shape, lambda j: (0,) * len(shape))
-    each = lambda a, b: pl.BlockSpec((1, a, b), lambda j: (j, 0, 0))
+    each = lambda a, b: pl.BlockSpec((1, a, b), lambda j: (j + base, 0, 0))
+    own = lambda a, b: pl.BlockSpec((1, a, b), lambda j: (j, 0, 0))
     arrays = (part, rows, w_far, taps, bias, skip, xs, b_mat, sp, cum, e2, row, states, pair, spreads)
     arrays = [v.value if isinstance(v, Kept) else far(v) for v in arrays]
-    outs = [plain(F32, NY, ROWS, XW), plain(BF, NY, ROWS, NS), plain(BF, NY, ROWS, XW)]
+    half = NY // 2
+    outs = [plain(F32, half, ROWS, XW), plain(BF, half, ROWS, NS), plain(BF, half, ROWS, XW)]
     results = pl.pallas_call(
-        intra_kernel,
-        grid=(NY,),
+        functools.partial(intra_kernel, base=base),
+        grid=(half,),
         in_specs=[
             each(EXT, WB), each(EXT, KX), whole(KX, WB),
             whole(4, NS), whole(1, NS), whole(1, XW),
             each(ROWS, XW), each(ROWS, NS), each(ROWS, 128), each(ROWS, 128), each(ROWS, 128),
             each(HEADS, ROWS),
-            pl.BlockSpec((1, NS, XW), lambda j: ((j // 2) * 2, 0, 0)),
+            pl.BlockSpec((1, NS, XW), lambda j: (base, 0, 0)),
             whole(NS, XW), whole(9, 128, XW),
         ],
-        out_specs=[each(ROWS, XW), each(ROWS, NS), each(ROWS, XW)],
+        out_specs=[own(ROWS, XW), own(ROWS, NS), own(ROWS, XW)],
         out_shape=outs,
         scratch_shapes=[pltpu.VMEM((EXT, NS), F32)],
         compiler_params=pltpu.CompilerParams(vmem_limit_bytes=28 << 20),
@@ -359,27 +363,30 @@
 
 
 def cross_kernel(
-    at_ref, y_ref, c_ref, sc_ref, z_ref, g3, g4, g5, g6, g7, logs_ref, spread_ref,
+    at_ref, ya_ref, ca_ref, za_ref, yb_ref, cb_ref, zb_ref, sc_ref, g3, g4, g5, g6, g7, logs_ref, spread_ref,
     q0, q1, q2, q3, bucket_ref,
 ):
     for k, got in enumerate((g3, g4, g5, g6, g7)):
         scaled = got[0:NS, :].astype(F32) * logs_ref[8 + k : 9 + k, :]
         bucket_ref[k] = scaled.astype(BF)
     for k, q_ref in enumerate((q0, q1, q2, q3)):
-        j = at_ref[k]
-        c_mat = c_ref[j]
+        j = (at_ref[0] + k) % NY
+        first = j < NY // 2
+        near_j = j % (NY // 2)
+        c_mat = jnp.where(first, ca_ref[near_j], cb_ref[near_j])
         scale = sc_ref[j]
-        y = y_ref[j]
+        y = jnp.where(first, ya_ref[near_j], yb_ref[near_j])
+        gate = jnp.where(first, za_ref[near_j], zb_ref[near_j]).astype(F32)
         for level in range(3, 8):
             y = y + mm(c_mat, bucket_ref[level - 3]) * mm(scale, spread_ref[level])
-        q_ref[...] = (y * silu(z_ref[j].astype(F32))).astype(BF)
-
-
-def run_cross(at, y, c_mat, sc, z, gots, logs, spreads):
+        q_ref[...] = (y * silu(gate)).astype(BF)
+
+
+def run_cross(at, inner, sc, gots, logs, spreads):
     return run(
         cross_kernel,
         (at,),
-        (y, c_mat, sc, z, *gots, logs, spreads),
+        (*inner, sc, *gots, logs, spreads),
         [shape_of(BF, ROWS, XW)] * NY,
         [pltpu.VMEM((5, NS, XW), BF)],
         place=lambda v: v,
@@ -388,7 +395,9 @@
 
 def out_kernel(at_ref, q0, q1, q2, q3, gain_ref, acts_ref, w_ref, out_ref, acc_ref, w_vmem, sems):
     blocks = (q0, q1, q2, q3)
-    rows = [pl.ds(pl.multiple_of(at_ref[k] * XW, XW), XW) for k in range(NY)]
+    rows = [
+        pl.ds(pl.multiple_of(((at_ref[0] + NY - k) % NY) * XW, XW), XW) for k in range(NY)
+    ]
     copies = [
         pltpu.make_async_copy(w_ref.at[rows[k], :], w_vmem.at[k], sems.at[k]) for k in range(NY)
     ]
@@ -433,8 +442,8 @@
         scale = lax.rsqrt(jnp.mean(v * v, axis=1, keepdims=True) + EPS)
         full_ref[start : start + v.shape[0], :] = v * scale * gain_ref[0:1, :]
     for k in range(NX):
-        start = pl.multiple_of(at_ref[k] * KX, KX)
-        part = pltpu.roll(full_ref[:, pl.ds(start, KX)], at_ref[NX], 1)
+        start = pl.multiple_of(at_ref[1 + k] * KX, KX)
+        part = pltpu.roll(full_ref[:, pl.ds(start, KX)], at_ref[1 + NX], 1)
         out_ref[:, k * KX : (k + 1) * KX] = part.astype(BF)
 
 
@@ -475,7 +484,7 @@
     rows = shard.shape[0]
     return run(
         columns_kernel,
-        (y.reshape(1),),
+        (y,),
         (shard,),
         [shape_of(BF, rows, WA + WB)] * 4,
         [pltpu.VMEM((NY, rows, WA + WB), BF)],
@@ -492,7 +501,7 @@
 
 def run_join(y, blocks):
     rows, width = blocks[0].shape
-    return run(join_kernel, (y.reshape(1),), blocks, [shape_of(BF, NY * rows, width)])[0]
+    return run(join_kernel, (y,), blocks, [shape_of(BF, NY * rows, width)])[0]
 
 
 def gather_kernel(*refs):
@@ -535,8 +544,8 @@
 
 
 def mask_kernel(bits_ref, out_ref):
-    for k in range(8):
-        out_ref[k : k + 1, :] = jnp.full((1, XW), bits_ref[k], jnp.int32)
+    for k in range(5):
+        out_ref[k : k + 1, :] = jnp.full((1, XW), bits_ref[2 + NX + k], jnp.int32)
 
 
 def layer(
@@ -556,24 +565,27 @@
     y = index % NY
     z = (index // NY) % NZ
     x = index // (NY * NZ)
-    w0, w1, w2, w3 = run_columns(y, in_proj[0])
+    bits = [z & 1, (z >> 1) & 1, (z >> 2) & 1, x & 1, (x >> 1) & 1]
+    where = jnp.stack(
+        [y, x, (x + 3) % NX, (x + 1) % NX, (x + 2) % NX, (512 - 64 * z) % 512, *bits]
+    )
+    w0, w1, w2, w3 = run_columns(where, in_proj[0])
     shared = (w0, sent(w1, Y_UP), sent(w2, Y_TWO), sent(w3, Y_DOWN))
-    columns = run_join(y, shared)
+    columns = run_join(where, shared)
     halo = sent(acts[0, ROWS - HALO :], HALO_NEXT)
-    order = jnp.stack([x, (x + 3) % NX, (x + 1) % NX, (x + 2) % NX, (512 - 64 * z) % 512])
-    u = run_norm(order, halo, acts[0], norm_gain)
+    u = run_norm(where, halo, acts[0], norm_gain)
 
     blocks = ring_z(columns)
     below, above = near_pair(u, Y_UP, Y_DOWN)
     far_lo, far_hi = far_pair(below, above, Y_UP, Y_DOWN, SPLIT)
     rows, rows_far = run(
-        stack_kernel, (y.reshape(1),), (u, below, above, far_lo, far_hi),
+        stack_kernel, (where,), (u, below, above, far_lo, far_hi),
         [plain(BF, NY, EXT, 3 * KX), plain(BF, NY, EXT, KX)],
     )
     depth = len(blocks) * blocks[1].shape[0]
     by_a, by_b = run(gather_kernel, (), blocks, [shape_of(BF, depth, WA), plain(BF, depth, WB)])
 
-    y, zero, _ = together(y, jnp.zeros((), jnp.int32), blocks[7])
+    y, _ = together(y, blocks[7])
     piece = lambda v, width: lax.dynamic_slice_in_dim(v, y * width, width, v.ndim - 1)
     taps_a = jnp.concatenate(
         [piece(conv_weight[0, :, :2048], XW), conv_weight[0, :, 2048 : 2048 + NS]], axis=1
@@ -589,10 +601,8 @@
         [jnp.zeros((1, HEADS * 8), F32), piece(decay_rate, HEADS), pad], axis=1
     )
     skip = jnp.repeat(piece(skip_gain, HEADS), HD, axis=1)
-    spreads = jnp.stack([spread(zero + k, 8) for k in range(8)] + [spread(zero + HEADS * 8, 1)])
-
-    bits = jnp.stack([z & 1, (z >> 1) & 1, (z >> 2) & 1, x & 1, (x >> 1) & 1, zero, zero, zero])
-    masks = run(mask_kernel, (bits,), (), [shape_of(jnp.int32, 8, XW)])[0]
+    spreads = run(spread_kernel, (), (), [plain(BF, 9, 128, XW)])[0]
+    masks = run(mask_kernel, (where,), (), [shape_of(jnp.int32, 8, XW)])[0]
 
     a_below, a_above = near_pair(by_a, X_UP, X_DOWN)
     fa_a, fb_a = far_pair(a_below, a_above, X_UP, X_DOWN, KX // 2)
@@ -611,17 +621,16 @@
         message, logs = run_merge(k, masks, got, message, logs)
         gots.append(got)
 
-    y_part, c_mat, z_cols = run_intra(
-        part_b, rows_far, w_far, conv_weight[0, :, 2048 + NS :], conv_bias[:, 2048 + NS :], skip,
-        xs, b_mat, sp, cum, e2, row, states, pair, spreads,
-    )
-    block = lambda k: (y + k) % NY
-    order = jnp.stack([block(k) for k in range(NY)])
-    q0, q1, q2, q3 = run_cross(order, y_part, c_mat, sc, z_cols, gots, logs, spreads)
+    inner = []
+    for base in (0, NY // 2):
+        inner += run_intra(
+            base, part_b, rows_far, w_far, conv_weight[0, :, 2048 + NS :], conv_bias[:, 2048 + NS :], skip,
+            xs, b_mat, sp, cum, e2, row, states, pair, spreads,
+        )
+    q0, q1, q2, q3 = run_cross(where, inner, sc, gots, logs, spreads)
     back_two = sent(q2, Y_TWO)
     blocks = (q0, sent(q1, Y_UP), back_two, sent(q3, Y_DOWN))
-    heads_at = jnp.stack([block(0), block(3), block(2), block(1)])
-    result = run_out(heads_at, blocks, gate_gain, out_proj[0], acts[0])
+    result = run_out(where, blocks, gate_gain, out_proj[0], acts[0])
     return lax.ppermute(result, "section", [(0, 1), (1, 0)])[None]
 
 

time: 174 us -> 173 us (level)
  starting transfers between devices: 48.9 us -> 55.4 us
  waiting for transfers between devices: 53.7 us -> 48.8 us
    ppermute x30, starting transfers between devices: 37.6 us -> 43.5 us  [sent(): return lax.ppermute(getattr(value, 'value', value), 'seq', pairs)]
    ppermute x30, waiting for transfers between devices: 51.4 us -> 46.5 us  [sent(): return lax.ppermute(getattr(value, 'value', value), 'seq', pairs)]
    pallas_call x19 -> x20, Pallas kernels: 45.7 us -> 42.5 us  [run(): pl.pallas_call(kernel, in_specs=[smem] * len(scalars) + [vmem] * len(arra...]
    pallas_call x1 -> x2, Pallas kernels: 10.3 us -> 13.3 us  [run_intra(): pl.pallas_call(functools.partial(intra_kernel, base=base), grid=(half,),...]
  transfers between devices with their start and end apart: 31 -> 31, of which waited for: 11 -> 16; matrix products, arithmetic and copies ran while one was open for 3% -> 2% of each run, Pallas kernels for 23% -> 22%
where the time goes in v3:
time: 173 us
  Pallas kernels  60.7 us (35%)
  starting transfers between devices  55.4 us (32%)
  waiting for transfers between devices  48.8 us (28%)
  local copies, waits for them, and re-layouts  7.78 us (4%)
    ppermute x30, waiting for transfers between devices, sent(): return lax.ppermute(getattr(value, 'value', value), 'seq', pairs)  46.5 us
    ppermute x30, starting transfers between devices, sent(): return lax.ppermute(getattr(value, 'value', value), 'seq', pairs)  43.5 us
    pallas_call x20, Pallas kernels, run(): pl.pallas_call(kernel, in_specs=[smem] * len(scalars) + [vmem] * len(arra...  42.5 us
    pallas_call x2, Pallas kernels, run_intra(): pl.pallas_call(functools.partial(intra_kernel, base=base), grid=(half,),...  13.3 us
    ppermute x1, starting transfers between devices, layer(): return lax.ppermute(result, 'section', [(0, 1), (1, 0)])[None]  11.9 us
    pallas_call x1, Pallas kernels, run_out(): pl.pallas_call(out_kernel, in_specs=[pl.BlockSpec(memory_space=pltpu.SMEM...  4.92 us
    unnamed x25, local copies, waits for them, and re-layouts  4.68 us
  transfers between devices with their start and end apart: 31, of which 16 were waited for; matrix products, arithmetic and copies ran while one was open for 2% of the time, Pallas kernels for 22%

profile of v3, /device:TPU:1, one launch (start us, length us, event | category | flops | bytes accessed | tf_op | source)
XLA Modules:
  0.0 173.0 jit_solution(12967025901351570254)
XLA Ops:
  0.1 0.9 copy-done.3
  1.6 2.2 %collective-permute-start.5 = (bf16[16,1408]{1,0:T(8,128)(2,1)S(1)}, bf16[16,1408]{1,0:T(8,128)(2,1)S(1)}, u32[]{:S(2)}, u32[]{:S(2)}) collective-permute-start(bf16[16,1408]{1,0:T(8,128)(2,1)S(1)} %get-tuple-element.46), channel_id=1, source_target_pairs={{0,1},{1,2},{2,3},{3,0},{4,5},{5,6},{6,7},{7,4},{8,9},{9,10},{10,1... | collective-permute-start | bytes 135176 | tf_op jit(solution)/shard_map/ppermute | solution.py:59
  3.8 2.6 %collective-permute-start.6 = (bf16[16,1408]{1,0:T(8,128)(2,1)S(1)}, bf16[16,1408]{1,0:T(8,128)(2,1)S(1)}, u32[]{:S(2)}, u32[]{:S(2)}) collective-permute-start(bf16[16,1408]{1,0:T(8,128)(2,1)S(1)} %get-tuple-element.47), channel_id=1, source_target_pairs={{0,2},{1,3},{2,0},{3,1},{4,6},{5,7},{6,4},{7,5},{8,10},{9,11},{10,... | collective-permute-start | bytes 135176 | tf_op jit(solution)/shard_map/ppermute | solution.py:59
  6.5 1.1 collective-permute-start.7
  7.5 0.8 collective-permute-done.6.b2
  8.4 1.3 collective-permute-done.7.b3
  10.2 1.7 collective-permute-start.11
  11.9 0.8 slice_bitcast_fusion
  12.8 1.8 %collective-permute-start = (bf16[16,2048]{1,0:T(8,128)(2,1)S(1)}, bf16[16,2048]{1,0:T(8,128)(2,1)S(1)}, u32[]{:S(2)}, u32[]{:S(2)}) collective-permute-start(bf16[16,2048]{1,0:T(8,128)(2,1)S(1)} %slice_bitcast_fusion), channel_id=1, source_target_pairs={{0,1},{1,2},{2,3},{3,4},{4,5},{5,6},{6,7},{7,8},{8,9},{9,10},{10,1... | collective-permute-start | bytes 196616 | tf_op jit(solution)/shard_map/ppermute | solution.py:59
  14.6 1.3 collective-permute-done.halo_ref
  15.9 1.2 copy-done.1
  17.8 1.6 shard_map.109.own_ref
  19.5 1.9 %collective-permute-start.1 = (bf16[272,2048]{1,0:T(8,128)(2,1)S(1)}, bf16[272,2048]{1,0:T(8,128)(2,1)S(1)}, u32[]{:S(2)}, u32[]{:S(2)}) collective-permute-start(bf16[272,2048]{1,0:T(8,128)(2,1)S(1)} %shard_map.109.own_ref), channel_id=1, source_target_pairs={{0,1},{1,2},{2,3},{3,0},{4,5},{5,6},{6,7},{7,4},{8,9},{9,10},{10,1... | collective-permute-start | bytes 3342344 | tf_op jit(solution)/shard_map/ppermute | solution.py:59
  21.3 7.0 %collective-permute-start.8 = (bf16[64,1408]{1,0:T(8,128)(2,1)S(1)}, bf16[64,1408]{1,0:T(8,128)(2,1)S(1)}, u32[]{:S(2)}, u32[]{:S(2)}) collective-permute-start(bf16[64,1408]{1,0:T(8,128)(2,1)S(1)} %shard_map.114.refs_0_), channel_id=1, source_target_pairs={{0,28},{1,29},{2,30},{3,31},{4,0},{5,1},{6,2},{7,3},{8,4},{9,5},{1... | collective-permute-start | bytes 540680 | tf_op jit(solution)/shard_map/ppermute | solution.py:59
  28.3 2.6 %collective-permute-start.2 = (bf16[272,2048]{1,0:T(8,128)(2,1)S(1)}, bf16[272,2048]{1,0:T(8,128)(2,1)S(1)}, u32[]{:S(2)}, u32[]{:S(2)}) collective-permute-start(bf16[272,2048]{1,0:T(8,128)(2,1)S(1)} %shard_map.109.own_ref), channel_id=1, source_target_pairs={{0,3},{1,0},{2,1},{3,2},{4,7},{5,4},{6,5},{7,6},{8,11},{9,8},{10,9... | collective-permute-start | bytes 3342344 | tf_op jit(solution)/shard_map/ppermute | solution.py:59
  30.9 3.0 %collective-permute-start.9 = (bf16[64,1408]{1,0:T(8,128)(2,1)S(1)}, bf16[64,1408]{1,0:T(8,128)(2,1)S(1)}, u32[]{:S(2)}, u32[]{:S(2)}) collective-permute-start(bf16[64,1408]{1,0:T(8,128)(2,1)S(1)} %collective-permute-done.8.refs_1_), channel_id=1, source_target_pairs={{0,28},{1,29},{2,30},{3,31},{4,0},{5,1},{6,2},{7,3},{8,4},{9,5},{1... | collective-permute-start | bytes 540680 | tf_op jit(solution)/shard_map/ppermute | solution.py:59
  34.2 2.1 %collective-permute-done.9.refs_2_ = bf16[64,1408]{1,0:T(8,128)(2,1)S(1)} collective-permute-done((bf16[64,1408]{1,0:T(8,128)(2,1)S(1)}, bf16[64,1408]{1,0:T(8,128)(2,1)S(1)}, u32[]{:S(2)}, u32[]{:S(2)}) %collective-permute-start.9) | collective-permute-done | bytes 180256 | tf_op jit(solution)/shard_map/ppermute | solution.py:59
  36.3 3.4 %collective-permute-start.10 = (bf16[64,1408]{1,0:T(8,128)(2,1)S(1)}, bf16[64,1408]{1,0:T(8,128)(2,1)S(1)}, u32[]{:S(2)}, u32[]{:S(2)}) collective-permute-start(bf16[64,1408]{1,0:T(8,128)(2,1)S(1)} %collective-permute-done.9.refs_2_), channel_id=1, source_target_pairs={{0,28},{1,29},{2,30},{3,31},{4,0},{5,1},{6,2},{7,3},{8,4},{9,5},{1... | collective-permute-start | bytes 540680 | tf_op jit(solution)/shard_map/ppermute | solution.py:59
  40.0 2.4 %collective-permute-done.10.refs_3_ = bf16[64,1408]{1,0:T(8,128)(2,1)S(1)} collective-permute-done((bf16[64,1408]{1,0:T(8,128)(2,1)S(1)}, bf16[64,1408]{1,0:T(8,128)(2,1)S(1)}, u32[]{:S(2)}, u32[]{:S(2)}) %collective-permute-start.10) | collective-permute-done | bytes 180256 | tf_op jit(solution)/shard_map/ppermute | solution.py:59
  42.4 3.7 %collective-permute-done.14.refs_4_ = bf16[64,1408]{1,0:T(8,128)(2,1)S(1)} collective-permute-done((bf16[64,1408]{1,0:T(8,128)(2,1)S(1)}, bf16[64,1408]{1,0:T(8,128)(2,1)S(1)}, u32[]{:S(2)}, u32[]{:S(2)}) %collective-permute-start.14) | collective-permute-done | bytes 180256 | tf_op jit(solution)/shard_map/ppermute | solution.py:59
  46.1 1.2 shard_map.115
  47.3 1.2 collective-permute-start.18
  48.5 1.5 collective-permute-start.19
  50.0 1.2 shard_map.120.spread_ref
  52.3 0.9 shard_map.110
  53.4 2.9 %collective-permute-start.4 = (bf16[128,2048]{1,0:T(8,128)(2,1)S(1)}, bf16[128,2048]{1,0:T(8,128)(2,1)S(1)}, u32[]{:S(2)}, u32[]{:S(2)}) collective-permute-start(bf16[128,2048]{1,0:T(8,128)(2,1)S(1)} %shard_map.111), channel_id=1, source_target_pairs={{0,3},{1,0},{2,1},{3,2},{4,7},{5,4},{6,5},{7,6},{8,11},{9,8},{10,9... | collective-permute-start | bytes 1572872 | tf_op jit(solution)/shard_map/ppermute | solution.py:59
  56.4 6.1 %collective-permute-done.18.below_ref.block_ref = bf16[512,768]{1,0:T(8,128)(2,1)} collective-permute-done((bf16[512,768]{1,0:T(8,128)(2,1)}, bf16[512,768]{1,0:T(8,128)(2,1)}, u32[]{:S(2)}, u32[]{:S(2)}) %collective-permute-start.18) | collective-permute-done | bytes 786464 | tf_op jit(solution)/shard_map/ppermute | solution.py:59
  62.5 1.2 shard_map.118
  63.8 1.2 shard_map.119
  64.9 2.7 %collective-permute-start.21 = (bf16[256,768]{1,0:T(8,128)(2,1)S(1)}, bf16[256,768]{1,0:T(8,128)(2,1)S(1)}, u32[]{:S(2)}, u32[]{:S(2)}) collective-permute-start(bf16[256,768]{1,0:T(8,128)(2,1)S(1)} %shard_map.119), channel_id=1, source_target_pairs={{0,96},{1,97},{2,98},{3,99},{4,100},{5,101},{6,102},{7,103},{8,104... | collective-permute-start | bytes 1179656 | tf_op jit(solution)/shard_map/ppermute | solution.py:59
  67.8 3.5 %shard_map.112 = (bf16[4,272,1536]{2,1,0:T(8,128)(2,1)}, bf16[4,272,512]{2,1,0:T(8,128)(2,1)}) custom-call(s32[11]{0:T(128)S(1)} %stack.47.at_ref.y_ref.bits_ref, bf16[272,2048]{1,0:T(8,128)(2,1)S(1)} %shard_map.109.own_ref, bf16[272,2048]{1,0:T(8,128)(2,1)S(1)} %collective-permute-done.1.block_ref.below_ref, ...), custom_call_target="tpu_custom_call" | custom-call | tf_op jit(solution)/shard_map/pallas_call | solution.py:120
  71.3 5.9 %shard_map.117.part_ref = f32[4,272,768]{2,1,0:T(8,128)S(1)} custom-call(bf16[4,272,1536]{2,1,0:T(8,128)(2,1)} %get-tuple-element.44.rows_ref, bf16[512,768]{1,0:T(8,128)(2,1)} %get-tuple-element.52.own_ref, bf16[512,768]{1,0:T(8,128)(2,1)} %collective-permute-done.18.below_ref.block_ref, bf16[512,768]{1,0:T(8,128)(2,1)} %collective-permute-done.19.above_ref.block_ref), custom_call_target="tpu_custom_call" | custom-call | tf_op jit(solution)/shard_map/pallas_call | solution.py:120
  77.2 10.4 %shard_map.121 = (f32[4,256,512]{2,1,0:T(8,128)}, bf16[4,256,128]{2,1,0:T(8,128)(2,1)}, f32[4,256,128]{2,1,0:T(8,128)}, f32[4,256,128]{2,1,0:T(8,128)}, f32[4,25...) custom-call(f32[4,272,768]{2,1,0:T(8,128)S(1)} %shard_map.117.part_r, ...), custom_call_target="tpu_custom_call" | custom-call | tf_op jit(solution)/shard_map/pallas_call | solution.py:120
  87.6 2.7 %collective-permute-start.16 = (bf16[512,640]{1,0:T(8,128)(2,1)}, bf16[512,640]{1,0:T(8,128)(2,1)S(1)}, u32[]{:S(2)}, u32[]{:S(2)}) collective-permute-start(bf16[512,640]{1,0:T(8,128)(2,1)} %get-tuple-element.49.own_ref), channel_id=1, source_target_pairs={{0,96},{1,97},{2,98},{3,99},{4,100},{5,101},{6,102},{7,103},{8,104... | collective-permute-start | bytes 1966088 | tf_op jit(solution)/shard_map/ppermute | solution.py:59
  92.3 6.0 %collective-permute-done.23.got_ref.g4 = bf16[144,512]{1,0:T(8,128)(2,1)S(1)} collective-permute-done((bf16[144,512]{1,0:T(8,128)(2,1)S(1)}, bf16[144,512]{1,0:T(8,128)(2,1)S(1)}, u32[]{:S(2)}, u32[]{:S(2)}) %collective-permute-start.23) | collective-permute-done | bytes 147488 | tf_op jit(solution)/shard_map/ppermute | solution.py:59
  98.3 1.2 collective-permute-start.24
  99.6 5.8 %collective-permute-done.24.got_ref.g5 = bf16[144,512]{1,0:T(8,128)(2,1)S(1)} collective-permute-done((bf16[144,512]{1,0:T(8,128)(2,1)S(1)}, bf16[144,512]{1,0:T(8,128)(2,1)S(1)}, u32[]{:S(2)}, u32[]{:S(2)}) %collective-permute-start.24) | collective-permute-done | bytes 147488 | tf_op jit(solution)/shard_map/ppermute | solution.py:59
  105.5 8.4 %collective-permute-done.25.got_ref.g6 = bf16[144,512]{1,0:T(8,128)(2,1)S(1)} collective-permute-done((bf16[144,512]{1,0:T(8,128)(2,1)S(1)}, bf16[144,512]{1,0:T(8,128)(2,1)S(1)}, u32[]{:S(2)}, u32[]{:S(2)}) %collective-permute-start.25) | collective-permute-done | bytes 147488 | tf_op jit(solution)/shard_map/ppermute | solution.py:59
  115.3 7.1 %shard_map.116.part_ref = f32[4,272,640]{2,1,0:T(8,128)} custom-call(bf16[4,272,1536]{2,1,0:T(8,128)(2,1)} %get-tuple-element.44.rows_ref, bf16[512,640]{1,0:T(8,128)(2,1)} %get-tuple-element.49.own_ref, bf16[512,640]{1,0:T(8,128)(2,1)S(1)} %collective-permute-done.15.below_ref, bf16[512,640]{1,0:T(8,128)(2,1)S(1)} %collective-permute-done.16.above_ref), custom_call_target="tpu_custom_call" | custom-call | tf_op jit(solution)/shard_map/pallas_call | solution.py:120
  123.2 6.6 %intra_block.2 = (f32[2,256,512]{2,1,0:T(8,128)}, bf16[2,256,128]{2,1,0:T(8,128)(2,1)}, bf16[2,256,512]{2,1,0:T(8,128)(2,1)}) custom-call(f32[4,272,640]{2,1,0:T(8,128)} %shard_map.116.part_ref, bf16[4,272,512]{2,1,0:T(8,128)(2,1)} %get-tuple-element.50.rows_ref, bf16[512,640]{1,0:T(8,128)(2,1)} %copy-done.6, f32[4,128]{1,0:T(4,128)} %get-tuple-element.84.taps_ref, ...), custom_call_target="tpu_custom_call" | custom-call | tf_op jit(solution)/shard_map/intra_block/pallas_call | solution.py:317
  129.9 6.7 %intra_block.3 = (f32[2,256,512]{2,1,0:T(8,128)}, bf16[2,256,128]{2,1,0:T(8,128)(2,1)}, bf16[2,256,512]{2,1,0:T(8,128)(2,1)}) custom-call(f32[4,272,640]{2,1,0:T(8,128)} %shard_map.116.part_ref, bf16[4,272,512]{2,1,0:T(8,128)(2,1)} %get-tuple-element.50.rows_ref, bf16[512,640]{1,0:T(8,128)(2,1)} %copy-done.6, f32[4,128]{1,0:T(4,128)} %get-tuple-element.84.taps_ref, ...), custom_call_target="tpu_custom_call" | custom-call | tf_op jit(solution)/shard_map/intra_block/pallas_call | solution.py:317
  137.3 5.6 %shard_map.128 = (bf16[256,512]{1,0:T(8,128)(2,1)S(1)}, bf16[256,512]{1,0:T(8,128)(2,1)S(1)}, bf16[256,512]{1,0:T(8,128)(2,1)S(1)}, bf16[256,512]{1,0:T(8,128)(2,1)S(1)}) custom-call(s32[11]{0:T(128)S(1)} %stack.47.at_ref.y_ref.bits_ref, f32[2,256,512]{2,1,0:T(8,128)} %get-tuple-element.61.ya_ref, bf16[2,256,128]{2,1,0:T(8,128)(2,1)} %get-tuple-element.62.ca_ref, ...), custom_call_target="tpu_custom_call" | custom-call | tf_op jit(solution)/shard_map/pallas_call | solution.py:120
  143.0 2.3 %collective-permute-start.28 = (bf16[256,512]{1,0:T(8,128)(2,1)S(1)}, bf16[256,512]{1,0:T(8,128)(2,1)S(1)}, u32[]{:S(2)}, u32[]{:S(2)}) collective-permute-start(bf16[256,512]{1,0:T(8,128)(2,1)S(1)} %get-tuple-element.81), channel_id=1, source_target_pairs={{0,2},{1,3},{2,0},{3,1},{4,6},{5,7},{6,4},{7,5},{8,10},{9,11},{10,... | collective-permute-start | bytes 786440 | tf_op jit(solution)/shard_map/ppermute | solution.py:59
  145.7 6.6 %collective-permute-done.27.q1 = bf16[256,512]{1,0:T(8,128)(2,1)S(1)} collective-permute-done((bf16[256,512]{1,0:T(8,128)(2,1)S(1)}, bf16[256,512]{1,0:T(8,128)(2,1)S(1)}, u32[]{:S(2)}, u32[]{:S(2)}) %collective-permute-start.27) | collective-permute-done | bytes 262176 | tf_op jit(solution)/shard_map/ppermute | solution.py:59
  152.9 4.9 %gate_out.1 = bf16[256,2048]{1,0:T(8,128)(2,1)S(1)} custom-call(s32[11]{0:T(128)S(1)} %stack.47.at_ref.y_ref.bits_ref, bf16[256,512]{1,0:T(8,128)(2,1)S(1)} %get-tuple-element.79.q0, bf16[256,512]{1,0:T(8,128)(2,1)S(1)} %collective-permute-done.27.q1, bf16[256,512]{1,0:T(8,128)(2,1)S(1)} %collective-permute-done.28.q2, ...), custom_call_target="tpu_custom_call" | custom-call | tf_op jit(solution)/shard_map/gate_out/pallas_call | solution.py:422
  157.8 11.9 %collective-permute-start.30 = (bf16[256,2048]{1,0:T(8,128)(2,1)S(1)}, bf16[256,2048]{1,0:T(8,128)(2,1)S(1)}, u32[]{:S(2)}, u32[]{:S(2)}) collective-permute-start(bf16[256,2048]{1,0:T(8,128)(2,1)S(1)} %gate_out.1), channel_id=1, source_target_pairs={{0,128},{128,0},{1,129},{129,1},{2,130},{130,2},{3,131},{131,3},{4... | collective-permute-start | bytes 3145736 | tf_op jit(solution)/shard_map/ppermute | solution.py:634
  169.7 2.3 %collective-permute-done.30 = bf16[256,2048]{1,0:T(8,128)(2,1)S(1)} collective-permute-done((bf16[256,2048]{1,0:T(8,128)(2,1)S(1)}, bf16[256,2048]{1,0:T(8,128)(2,1)S(1)}, u32[]{:S(2)}, u32[]{:S(2)}) %collective-permute-start.30) | collective-permute-done | bytes 1048608 | tf_op jit(solution)/shard_map/ppermute | solution.py:634
  172.0 1.0 copy.13
  (82 shorter events, 10.5 us)
Async XLA Ops:
  0.0 56.3 %copy-start = (f32[1,256]{1,0:T(1,128)S(1)}, f32[1,256]{1,0:T(1,128)}, u32[]{:S(2)}) copy-start(f32[1,256]{1,0:T(1,128)} %param.19) | copy-start | bytes 3076
  0.1 0.9 copy-start.3
  1.6 5.9 %collective-permute-start.5 = (bf16[16,1408]{1,0:T(8,128)(2,1)S(1)}, bf16[16,1408]{1,0:T(8,128)(2,1)S(1)}, u32[]{:S(2)}, u32[]{:S(2)}) collective-permute-start(bf16[16,1408]{1,0:T(8,128)(2,1)S(1)} %get-tuple-element.46), channel_id=1, source_target_pairs={{0,1},{1,2},{2,3},{3,0},{4,5},{5,6},{6,7},{7,4},{8,9},{9,10},{10,1... | collective-permute-start | bytes 135176 | tf_op jit(solution)/shard_map/ppermute | solution.py:59
  3.8 4.5 %collective-permute-start.6 = (bf16[16,1408]{1,0:T(8,128)(2,1)S(1)}, bf16[16,1408]{1,0:T(8,128)(2,1)S(1)}, u32[]{:S(2)}, u32[]{:S(2)}) collective-permute-start(bf16[16,1408]{1,0:T(8,128)(2,1)S(1)} %get-tuple-element.47), channel_id=1, source_target_pairs={{0,2},{1,3},{2,0},{3,1},{4,6},{5,7},{6,4},{7,5},{8,10},{9,11},{10,... | collective-permute-start | bytes 135176 | tf_op jit(solution)/shard_map/ppermute | solution.py:59
  6.5 3.2 %collective-permute-start.7 = (bf16[16,1408]{1,0:T(8,128)(2,1)S(1)}, bf16[16,1408]{1,0:T(8,128)(2,1)S(1)}, u32[]{:S(2)}, u32[]{:S(2)}) collective-permute-start(bf16[16,1408]{1,0:T(8,128)(2,1)S(1)} %get-tuple-element.48), channel_id=1, source_target_pairs={{0,3},{1,0},{2,1},{3,2},{4,7},{5,4},{6,5},{7,6},{8,11},{9,8},{10,9... | collective-permute-start | bytes 135176 | tf_op jit(solution)/shard_map/ppermute | solution.py:59
  10.2 18.1 %collective-permute-start.11 = (bf16[64,1408]{1,0:T(8,128)(2,1)S(1)}, bf16[64,1408]{1,0:T(8,128)(2,1)S(1)}, u32[]{:S(2)}, u32[]{:S(2)}) collective-permute-start(bf16[64,1408]{1,0:T(8,128)(2,1)S(1)} %shard_map.114.refs_0_), channel_id=1, source_target_pairs={{0,4},{1,5},{2,6},{3,7},{4,8},{5,9},{6,10},{7,11},{8,12},{9,13},{1... | collective-permute-start | bytes 540680 | tf_op jit(solution)/shard_map/ppermute | solution.py:59
  12.8 3.1 %collective-permute-start = (bf16[16,2048]{1,0:T(8,128)(2,1)S(1)}, bf16[16,2048]{1,0:T(8,128)(2,1)S(1)}, u32[]{:S(2)}, u32[]{:S(2)}) collective-permute-start(bf16[16,2048]{1,0:T(8,128)(2,1)S(1)} %slice_bitcast_fusion), channel_id=1, source_target_pairs={{0,1},{1,2},{2,3},{3,4},{4,5},{5,6},{6,7},{7,8},{8,9},{9,10},{10,1... | collective-permute-start | bytes 196616 | tf_op jit(solution)/shard_map/ppermute | solution.py:59
  15.9 1.2 copy-start.1
  17.1 0.7 copy-start.4
  17.8 33.3 %copy-start.8 = (f32[1,2304]{1,0:T(1,128)S(1)}, f32[1,2304]{1,0:T(1,128)}, u32[]{:S(2)}) copy-start(f32[1,2304]{1,0:T(1,128)} %param.15) | copy-start | bytes 27652
  17.8 33.9 %copy-start.7 = (f32[1,4,2304]{2,1,0:T(4,128)S(1)}, f32[1,4,2304]{2,1,0:T(4,128)}, u32[]{:S(2)}) copy-start(f32[1,4,2304]{2,1,0:T(4,128)} %param.14) | copy-start | bytes 110596
  17.8 34.5 %slice-start.1 = ((f32[1,2304]{1,0:T(1,128)}), f32[1,2048]{1,0:T(1,128)S(1)}, s32[]{:S(2)}) async-start(f32[1,2304]{1,0:T(1,128)} %param.15), calls=%async_computation.1 | async-start | bytes 16384 | tf_op jit(solution)/shard_map/slice | solution.py:594
  19.5 33.8 %copy-start.9 = (f32[1,32]{1,0:T(1,128)S(1)}, f32[1,32]{1,0:T(1,128)}, u32[]{:S(2)}) copy-start(f32[1,32]{1,0:T(1,128)} %param.17) | copy-start | bytes 388
  19.5 33.8 %copy-start.10 = (f32[1,32]{1,0:T(1,128)S(1)}, f32[1,32]{1,0:T(1,128)}, u32[]{:S(2)}) copy-start(f32[1,32]{1,0:T(1,128)} %param.16) | copy-start | bytes 388
  19.5 32.9 %collective-permute-start.1 = (bf16[272,2048]{1,0:T(8,128)(2,1)S(1)}, bf16[272,2048]{1,0:T(8,128)(2,1)S(1)}, u32[]{:S(2)}, u32[]{:S(2)}) collective-permute-start(bf16[272,2048]{1,0:T(8,128)(2,1)S(1)} %shard_map.109.own_ref), channel_id=1, source_target_pairs={{0,1},{1,2},{2,3},{3,0},{4,5},{5,6},{6,7},{7,4},{8,9},{9,10},{10,1... | collective-permute-start | bytes 3342344 | tf_op jit(solution)/shard_map/ppermute | solution.py:59
  21.3 9.6 %collective-permute-start.8 = (bf16[64,1408]{1,0:T(8,128)(2,1)S(1)}, bf16[64,1408]{1,0:T(8,128)(2,1)S(1)}, u32[]{:S(2)}, u32[]{:S(2)}) collective-permute-start(bf16[64,1408]{1,0:T(8,128)(2,1)S(1)} %shard_map.114.refs_0_), channel_id=1, source_target_pairs={{0,28},{1,29},{2,30},{3,31},{4,0},{5,1},{6,2},{7,3},{8,4},{9,5},{1... | collective-permute-start | bytes 540680 | tf_op jit(solution)/shard_map/ppermute | solution.py:59
  28.3 5.9 %collective-permute-start.12 = (bf16[64,1408]{1,0:T(8,128)(2,1)S(1)}, bf16[64,1408]{1,0:T(8,128)(2,1)S(1)}, u32[]{:S(2)}, u32[]{:S(2)}) collective-permute-start(bf16[64,1408]{1,0:T(8,128)(2,1)S(1)} %collective-permute-done.11.refs_7_), channel_id=1, source_target_pairs={{0,4},{1,5},{2,6},{3,7},{4,8},{5,9},{6,10},{7,11},{8,12},{9,13},{1... | collective-permute-start | bytes 540680 | tf_op jit(solution)/shard_map/ppermute | solution.py:59
  28.3 25.0 %collective-permute-start.2 = (bf16[272,2048]{1,0:T(8,128)(2,1)S(1)}, bf16[272,2048]{1,0:T(8,128)(2,1)S(1)}, u32[]{:S(2)}, u32[]{:S(2)}) collective-permute-start(bf16[272,2048]{1,0:T(8,128)(2,1)S(1)} %shard_map.109.own_ref), channel_id=1, source_target_pairs={{0,3},{1,0},{2,1},{3,2},{4,7},{5,4},{6,5},{7,6},{8,11},{9,8},{10,9... | collective-permute-start | bytes 3342344 | tf_op jit(solution)/shard_map/ppermute | solution.py:59
  30.9 5.4 %collective-permute-start.9 = (bf16[64,1408]{1,0:T(8,128)(2,1)S(1)}, bf16[64,1408]{1,0:T(8,128)(2,1)S(1)}, u32[]{:S(2)}, u32[]{:S(2)}) collective-permute-start(bf16[64,1408]{1,0:T(8,128)(2,1)S(1)} %collective-permute-done.8.refs_1_), channel_id=1, source_target_pairs={{0,28},{1,29},{2,30},{3,31},{4,0},{5,1},{6,2},{7,3},{8,4},{9,5},{1... | collective-permute-start | bytes 540680 | tf_op jit(solution)/shard_map/ppermute | solution.py:59
  34.2 5.9 %collective-permute-start.13 = (bf16[64,1408]{1,0:T(8,128)(2,1)S(1)}, bf16[64,1408]{1,0:T(8,128)(2,1)S(1)}, u32[]{:S(2)}, u32[]{:S(2)}) collective-permute-start(bf16[64,1408]{1,0:T(8,128)(2,1)S(1)} %collective-permute-done.12.refs_6_), channel_id=1, source_target_pairs={{0,4},{1,5},{2,6},{3,7},{4,8},{5,9},{6,10},{7,11},{8,12},{9,13},{1... | collective-permute-start | bytes 540680 | tf_op jit(solution)/shard_map/ppermute | solution.py:59
  36.3 6.1 %collective-permute-start.10 = (bf16[64,1408]{1,0:T(8,128)(2,1)S(1)}, bf16[64,1408]{1,0:T(8,128)(2,1)S(1)}, u32[]{:S(2)}, u32[]{:S(2)}) collective-permute-start(bf16[64,1408]{1,0:T(8,128)(2,1)S(1)} %collective-permute-done.9.refs_2_), channel_id=1, source_target_pairs={{0,28},{1,29},{2,30},{3,31},{4,0},{5,1},{6,2},{7,3},{8,4},{9,5},{1... | collective-permute-start | bytes 540680 | tf_op jit(solution)/shard_map/ppermute | solution.py:59
  40.0 6.1 %collective-permute-start.14 = (bf16[64,1408]{1,0:T(8,128)(2,1)S(1)}, bf16[64,1408]{1,0:T(8,128)(2,1)S(1)}, u32[]{:S(2)}, u32[]{:S(2)}) collective-permute-start(bf16[64,1408]{1,0:T(8,128)(2,1)S(1)} %collective-permute-done.13.refs_5_), channel_id=1, source_target_pairs={{0,4},{1,5},{2,6},{3,7},{4,8},{5,9},{6,10},{7,11},{8,12},{9,13},{1... | collective-permute-start | bytes 540680 | tf_op jit(solution)/shard_map/ppermute | solution.py:59
  47.3 15.2 %collective-permute-start.18 = (bf16[512,768]{1,0:T(8,128)(2,1)}, bf16[512,768]{1,0:T(8,128)(2,1)}, u32[]{:S(2)}, u32[]{:S(2)}) collective-permute-start(bf16[512,768]{1,0:T(8,128)(2,1)} %get-tuple-element.52.own_ref), channel_id=1, source_target_pairs={{0,32},{1,33},{2,34},{3,35},{4,36},{5,37},{6,38},{7,39},{8,40},{9,... | collective-permute-start | bytes 2359304 | tf_op jit(solution)/shard_map/ppermute | solution.py:59
  48.5 15.3 %collective-permute-start.19 = (bf16[512,768]{1,0:T(8,128)(2,1)}, bf16[512,768]{1,0:T(8,128)(2,1)}, u32[]{:S(2)}, u32[]{:S(2)}) collective-permute-start(bf16[512,768]{1,0:T(8,128)(2,1)} %get-tuple-element.52.own_ref), channel_id=1, source_target_pairs={{0,96},{1,97},{2,98},{3,99},{4,100},{5,101},{6,102},{7,103},{8,104... | collective-permute-start | bytes 2359304 | tf_op jit(solution)/shard_map/ppermute | solution.py:59
  53.2 14.5 %slice-start = ((f32[1,4,2304]{2,1,0:T(4,128)}), f32[1,4,2048]{2,1,0:T(4,128)S(1)}, s32[]{:S(2)}) async-start(f32[1,4,2304]{2,1,0:T(4,128)} %param.14), calls=%async_computation | async-start | bytes 65536 | tf_op jit(solution)/shard_map/slice | solution.py:591
  53.2 14.6 %collective-permute-start.3 = (bf16[144,2048]{1,0:T(8,128)(2,1)}, bf16[144,2048]{1,0:T(8,128)(2,1)}, u32[]{:S(2)}, u32[]{:S(2)}) collective-permute-start(bf16[144,2048]{1,0:T(8,128)(2,1)} %shard_map.110), channel_id=1, source_target_pairs={{0,1},{1,2},{2,3},{3,0},{4,5},{5,6},{6,7},{7,4},{8,9},{9,10},{10,1... | collective-permute-start | bytes 1769480 | tf_op jit(solution)/shard_map/ppermute | solution.py:59
  53.4 14.4 %collective-permute-start.4 = (bf16[128,2048]{1,0:T(8,128)(2,1)S(1)}, bf16[128,2048]{1,0:T(8,128)(2,1)S(1)}, u32[]{:S(2)}, u32[]{:S(2)}) collective-permute-start(bf16[128,2048]{1,0:T(8,128)(2,1)S(1)} %shard_map.111), channel_id=1, source_target_pairs={{0,3},{1,0},{2,1},{3,2},{4,7},{5,4},{6,5},{7,6},{8,11},{9,8},{10,9... | collective-permute-start | bytes 1572872 | tf_op jit(solution)/shard_map/ppermute | solution.py:59
  63.7 13.5 %collective-permute-start.20 = (bf16[256,768]{1,0:T(8,128)(2,1)S(1)}, bf16[256,768]{1,0:T(8,128)(2,1)S(1)}, u32[]{:S(2)}, u32[]{:S(2)}) collective-permute-start(bf16[256,768]{1,0:T(8,128)(2,1)S(1)} %shard_map.118), channel_id=1, source_target_pairs={{0,32},{1,33},{2,34},{3,35},{4,36},{5,37},{6,38},{7,39},{8,40},{9,... | collective-permute-start | bytes 1179656 | tf_op jit(solution)/shard_map/ppermute | solution.py:59
  64.9 12.2 %collective-permute-start.21 = (bf16[256,768]{1,0:T(8,128)(2,1)S(1)}, bf16[256,768]{1,0:T(8,128)(2,1)S(1)}, u32[]{:S(2)}, u32[]{:S(2)}) collective-permute-start(bf16[256,768]{1,0:T(8,128)(2,1)S(1)} %shard_map.119), channel_id=1, source_target_pairs={{0,96},{1,97},{2,98},{3,99},{4,100},{5,101},{6,102},{7,103},{8,104... | collective-permute-start | bytes 1179656 | tf_op jit(solution)/shard_map/ppermute | solution.py:59
  77.2 37.3 %copy-start.11 = (f32[1,32]{1,0:T(1,128)S(1)}, f32[1,32]{1,0:T(1,128)}, u32[]{:S(2)}) copy-start(f32[1,32]{1,0:T(1,128)} %param.18) | copy-start | bytes 388
  87.6 4.0 %collective-permute-start.22 = (bf16[144,512]{1,0:T(8,128)(2,1)S(1)}, bf16[144,512]{1,0:T(8,128)(2,1)S(1)}, u32[]{:S(2)}, u32[]{:S(2)}) collective-permute-start(bf16[144,512]{1,0:T(8,128)(2,1)S(1)} %get-tuple-element.68.own_ref), channel_id=1, source_target_pairs={{0,4},{1,5},{2,6},{3,7},{4,0},{5,1},{6,2},{7,3},{8,12},{9,13},{10,... | collective-permute-start | bytes 442376 | tf_op jit(solution)/shard_map/ppermute | solution.py:59
  87.6 27.7 %collective-permute-start.15 = (bf16[512,640]{1,0:T(8,128)(2,1)}, bf16[512,640]{1,0:T(8,128)(2,1)S(1)}, u32[]{:S(2)}, u32[]{:S(2)}) collective-permute-start(bf16[512,640]{1,0:T(8,128)(2,1)} %get-tuple-element.49.own_ref), channel_id=1, source_target_pairs={{0,32},{1,33},{2,34},{3,35},{4,36},{5,37},{6,38},{7,39},{8,40},{9,... | collective-permute-start | bytes 1966088 | tf_op jit(solution)/shard_map/ppermute | solution.py:59
  87.6 27.7 %collective-permute-start.16 = (bf16[512,640]{1,0:T(8,128)(2,1)}, bf16[512,640]{1,0:T(8,128)(2,1)S(1)}, u32[]{:S(2)}, u32[]{:S(2)}) collective-permute-start(bf16[512,640]{1,0:T(8,128)(2,1)} %get-tuple-element.49.own_ref), channel_id=1, source_target_pairs={{0,96},{1,97},{2,98},{3,99},{4,100},{5,101},{6,102},{7,103},{8,104... | collective-permute-start | bytes 1966088 | tf_op jit(solution)/shard_map/ppermute | solution.py:59
  90.3 32.1 %collective-permute-start.17 = (bf16[512,640]{1,0:T(8,128)(2,1)}, bf16[512,640]{1,0:T(8,128)(2,1)S(1)}, u32[]{:S(2)}, u32[]{:S(2)}) collective-permute-start(bf16[512,640]{1,0:T(8,128)(2,1)} %get-tuple-element.49.own_ref), channel_id=1, source_target_pairs={{0,64},{1,65},{2,66},{3,67},{4,68},{5,69},{6,70},{7,71},{8,72},{9,... | collective-permute-start | bytes 1966088 | tf_op jit(solution)/shard_map/ppermute | solution.py:59
  91.7 6.6 %collective-permute-start.23 = (bf16[144,512]{1,0:T(8,128)(2,1)S(1)}, bf16[144,512]{1,0:T(8,128)(2,1)S(1)}, u32[]{:S(2)}, u32[]{:S(2)}) collective-permute-start(bf16[144,512]{1,0:T(8,128)(2,1)S(1)} %get-tuple-element.70.own_ref), channel_id=1, source_target_pairs={{0,8},{1,9},{2,10},{3,11},{4,12},{5,13},{6,14},{7,15},{8,0},{9,1},... | collective-permute-start | bytes 442376 | tf_op jit(solution)/shard_map/ppermute | solution.py:59
  98.3 7.0 %collective-permute-start.24 = (bf16[144,512]{1,0:T(8,128)(2,1)S(1)}, bf16[144,512]{1,0:T(8,128)(2,1)S(1)}, u32[]{:S(2)}, u32[]{:S(2)}) collective-permute-start(bf16[144,512]{1,0:T(8,128)(2,1)S(1)} %get-tuple-element.72.own_ref), channel_id=1, source_target_pairs={{0,28},{1,29},{2,30},{3,31},{4,24},{5,25},{6,26},{7,27},{8,20},{9,... | collective-permute-start | bytes 442376 | tf_op jit(solution)/shard_map/ppermute | solution.py:59
  105.4 8.5 %collective-permute-start.25 = (bf16[144,512]{1,0:T(8,128)(2,1)S(1)}, bf16[144,512]{1,0:T(8,128)(2,1)S(1)}, u32[]{:S(2)}, u32[]{:S(2)}) collective-permute-start(bf16[144,512]{1,0:T(8,128)(2,1)S(1)} %get-tuple-element.74.own_ref), channel_id=1, source_target_pairs={{0,32},{1,33},{2,34},{3,35},{4,36},{5,37},{6,38},{7,39},{8,40},{9,... | collective-permute-start | bytes 442376 | tf_op jit(solution)/shard_map/ppermute | solution.py:59
  114.0 22.6 %collective-permute-start.26 = (bf16[144,512]{1,0:T(8,128)(2,1)S(1)}, bf16[144,512]{1,0:T(8,128)(2,1)S(1)}, u32[]{:S(2)}, u32[]{:S(2)}) collective-permute-start(bf16[144,512]{1,0:T(8,128)(2,1)S(1)} %get-tuple-element.76.own_ref), channel_id=1, source_target_pairs={{0,96},{1,97},{2,98},{3,99},{4,100},{5,101},{6,102},{7,103},{8,104... | collective-permute-start | bytes 442376 | tf_op jit(solution)/shard_map/ppermute | solution.py:59
  122.4 0.8 copy-start.6
  137.3 15.6 %copy-start.2 = (bf16[1,256,2048]{2,1,0:T(8,128)(2,1)S(1)}, bf16[1,256,2048]{2,1,0:T(8,128)(2,1)}, u32[]{:S(2)}) copy-start(bf16[1,256,2048]{2,1,0:T(8,128)(2,1)} %param.11) | copy-start | bytes 3145732
  137.3 15.6 %copy-start.5 = (f32[1,2048]{1,0:T(1,128)S(1)}, f32[1,2048]{1,0:T(1,128)}, u32[]{:S(2)}) copy-start(f32[1,2048]{1,0:T(1,128)} %gain_ref.3) | copy-start | bytes 24580
  142.9 9.3 %collective-permute-start.27 = (bf16[256,512]{1,0:T(8,128)(2,1)S(1)}, bf16[256,512]{1,0:T(8,128)(2,1)S(1)}, u32[]{:S(2)}, u32[]{:S(2)}) collective-permute-start(bf16[256,512]{1,0:T(8,128)(2,1)S(1)} %get-tuple-element.80), channel_id=1, source_target_pairs={{0,1},{1,2},{2,3},{3,0},{4,5},{5,6},{6,7},{7,4},{8,9},{9,10},{10,1... | collective-permute-start | bytes 786440 | tf_op jit(solution)/shard_map/ppermute | solution.py:59
  143.0 9.2 %collective-permute-start.28 = (bf16[256,512]{1,0:T(8,128)(2,1)S(1)}, bf16[256,512]{1,0:T(8,128)(2,1)S(1)}, u32[]{:S(2)}, u32[]{:S(2)}) collective-permute-start(bf16[256,512]{1,0:T(8,128)(2,1)S(1)} %get-tuple-element.81), channel_id=1, source_target_pairs={{0,2},{1,3},{2,0},{3,1},{4,6},{5,7},{6,4},{7,5},{8,10},{9,11},{10,... | collective-permute-start | bytes 786440 | tf_op jit(solution)/shard_map/ppermute | solution.py:59
  145.4 7.5 %collective-permute-start.29 = (bf16[256,512]{1,0:T(8,128)(2,1)S(1)}, bf16[256,512]{1,0:T(8,128)(2,1)S(1)}, u32[]{:S(2)}, u32[]{:S(2)}) collective-permute-start(bf16[256,512]{1,0:T(8,128)(2,1)S(1)} %get-tuple-element.82), channel_id=1, source_target_pairs={{0,3},{1,0},{2,1},{3,2},{4,7},{5,4},{6,5},{7,6},{8,11},{9,8},{10,9... | collective-permute-start | bytes 786440 | tf_op jit(solution)/shard_map/ppermute | solution.py:59
  157.8 14.2 %collective-permute-start.30 = (bf16[256,2048]{1,0:T(8,128)(2,1)S(1)}, bf16[256,2048]{1,0:T(8,128)(2,1)S(1)}, u32[]{:S(2)}, u32[]{:S(2)}) collective-permute-start(bf16[256,2048]{1,0:T(8,128)(2,1)S(1)} %gate_out.1), channel_id=1, source_target_pairs={{0,128},{128,0},{1,129},{129,1},{2,130},{130,2},{3,131},{131,3},{4... | collective-permute-start | bytes 3145736 | tf_op jit(solution)/shard_map/ppermute | solution.py:634

commit v4 on v3

--- a/solution.py
+++ b/solution.py
@@ -292,9 +292,13 @@
     parts = []
     for h in range(HEADS):
         lane = HEADS * 8 + h
-        diff = cum[:, lane : lane + 1] - row_ref[0, h : h + 1, :]
-        decay = jnp.exp(jnp.where(causal, diff, -1e30)) * scores
-        parts.append(mm(decay, xd[:, h * HD : (h + 1) * HD]))
+        halves = []
+        for top, width in ((0, ROWS // 2), (ROWS // 2, ROWS)):
+            here = slice(top, top + ROWS // 2)
+            diff = cum[here, lane : lane + 1] - row_ref[0, h : h + 1, :width]
+            decay = jnp.exp(jnp.where(causal[here, :width], diff, -1e30)) * scores[here, :width]
+            halves.append(mm(decay, xd[:width, h * HD : (h + 1) * HD]))
+        parts.append(jnp.concatenate(halves, axis=0))
     y = jnp.concatenate(parts, axis=1) * mm(sp, spread_ref[0])
     y = y + skip_ref[0:1, :] * xs
     odd = (j % 2).astype(F32)
@@ -455,7 +459,7 @@
         (halo, acts, gain),
         [shape_of(BF, EXT, width)],
         [pltpu.VMEM((EXT, width), F32)],
-        place=lambda v: v,
+        place=far,
     )[0]
 
 

time: 173 us -> 172 us (level)
    unnamed x25 -> x23, local copies, waits for them, and re-layouts: 4.68 us -> 3.38 us
where the time goes in v4:
time: 172 us
  Pallas kernels  61.1 us (36%)
  starting transfers between devices  55.4 us (32%)
  waiting for transfers between devices  48.8 us (28%)
  local copies, waits for them, and re-layouts  6.46 us (4%)
    ppermute x30, waiting for transfers between devices, sent(): return lax.ppermute(getattr(value, 'value', value), 'seq', pairs)  46.5 us
    ppermute x30, starting transfers between devices, sent(): return lax.ppermute(getattr(value, 'value', value), 'seq', pairs)  43.5 us
    pallas_call x20, Pallas kernels, run(): pl.pallas_call(kernel, in_specs=[smem] * len(scalars) + [vmem] * len(arra...  43.2 us
    pallas_call x2, Pallas kernels, run_intra(): pl.pallas_call(functools.partial(intra_kernel, base=base), grid=(half,),...  13 us
    ppermute x1, starting transfers between devices, layer(): return lax.ppermute(result, 'section', [(0, 1), (1, 0)])[None]  11.9 us
    pallas_call x1, Pallas kernels, run_out(): pl.pallas_call(out_kernel, in_specs=[pl.BlockSpec(memory_space=pltpu.SMEM...  4.93 us
  transfers between devices with their start and end apart: 31, of which 16 were waited for; matrix products, arithmetic and copies ran while one was open for 2% of the time, Pallas kernels for 22%

profile of v4, /device:TPU:1, one launch (start us, length us, event | category | flops | bytes accessed | tf_op | source)
XLA Modules:
  0.0 172.0 jit_solution(4145813810597796034)
XLA Ops:
  0.1 0.9 copy-done.2
  1.6 2.2 %collective-permute-start.5 = (bf16[16,1408]{1,0:T(8,128)(2,1)S(1)}, bf16[16,1408]{1,0:T(8,128)(2,1)S(1)}, u32[]{:S(2)}, u32[]{:S(2)}) collective-permute-start(bf16[16,1408]{1,0:T(8,128)(2,1)S(1)} %get-tuple-element.46), channel_id=1, source_target_pairs={{0,1},{1,2},{2,3},{3,0},{4,5},{5,6},{6,7},{7,4},{8,9},{9,10},{10,1... | collective-permute-start | bytes 135176 | tf_op jit(solution)/shard_map/ppermute | solution.py:59
  3.8 2.6 %collective-permute-start.6 = (bf16[16,1408]{1,0:T(8,128)(2,1)S(1)}, bf16[16,1408]{1,0:T(8,128)(2,1)S(1)}, u32[]{:S(2)}, u32[]{:S(2)}) collective-permute-start(bf16[16,1408]{1,0:T(8,128)(2,1)S(1)} %get-tuple-element.47), channel_id=1, source_target_pairs={{0,2},{1,3},{2,0},{3,1},{4,6},{5,7},{6,4},{7,5},{8,10},{9,11},{10,... | collective-permute-start | bytes 135176 | tf_op jit(solution)/shard_map/ppermute | solution.py:59
  6.5 1.1 collective-permute-start.7
  7.5 0.8 collective-permute-done.6.b2
  8.4 1.3 collective-permute-done.7.b3
  10.2 1.7 collective-permute-start.11
  11.9 0.8 slice_bitcast_fusion
  12.8 1.8 %collective-permute-start = (bf16[16,2048]{1,0:T(8,128)(2,1)S(1)}, bf16[16,2048]{1,0:T(8,128)(2,1)S(1)}, u32[]{:S(2)}, u32[]{:S(2)}) collective-permute-start(bf16[16,2048]{1,0:T(8,128)(2,1)S(1)} %slice_bitcast_fusion), channel_id=1, source_target_pairs={{0,1},{1,2},{2,3},{3,4},{4,5},{5,6},{6,7},{7,8},{8,9},{9,10},{10,1... | collective-permute-start | bytes 196616 | tf_op jit(solution)/shard_map/ppermute | solution.py:59
  14.6 1.3 collective-permute-done.halo_ref
  16.5 2.3 %shard_map.109.own_ref = bf16[272,2048]{1,0:T(8,128)(2,1)S(1)} custom-call(s32[11]{0:T(128)S(1)} %stack.47.at_ref.y_ref.bits_ref, bf16[16,2048]{1,0:T(8,128)(2,1)} %copy-done.5, bf16[256,2048]{1,0:T(8,128)(2,1)} %bitcast.32, f32[1,2048]{1,0:T(1,128)} %gain_ref.2), custom_call_target="tpu_custom_call" | custom-call | tf_op jit(solution)/shard_map/pallas_call | solution.py:120
  18.9 1.9 %collective-permute-start.1 = (bf16[272,2048]{1,0:T(8,128)(2,1)S(1)}, bf16[272,2048]{1,0:T(8,128)(2,1)S(1)}, u32[]{:S(2)}, u32[]{:S(2)}) collective-permute-start(bf16[272,2048]{1,0:T(8,128)(2,1)S(1)} %shard_map.109.own_ref), channel_id=1, source_target_pairs={{0,1},{1,2},{2,3},{3,0},{4,5},{5,6},{6,7},{7,4},{8,9},{9,10},{10,1... | collective-permute-start | bytes 3342344 | tf_op jit(solution)/shard_map/ppermute | solution.py:59
  20.8 7.0 %collective-permute-start.8 = (bf16[64,1408]{1,0:T(8,128)(2,1)S(1)}, bf16[64,1408]{1,0:T(8,128)(2,1)S(1)}, u32[]{:S(2)}, u32[]{:S(2)}) collective-permute-start(bf16[64,1408]{1,0:T(8,128)(2,1)S(1)} %shard_map.114.refs_0_), channel_id=1, source_target_pairs={{0,28},{1,29},{2,30},{3,31},{4,0},{5,1},{6,2},{7,3},{8,4},{9,5},{1... | collective-permute-start | bytes 540680 | tf_op jit(solution)/shard_map/ppermute | solution.py:59
  27.7 2.6 %collective-permute-start.2 = (bf16[272,2048]{1,0:T(8,128)(2,1)S(1)}, bf16[272,2048]{1,0:T(8,128)(2,1)S(1)}, u32[]{:S(2)}, u32[]{:S(2)}) collective-permute-start(bf16[272,2048]{1,0:T(8,128)(2,1)S(1)} %shard_map.109.own_ref), channel_id=1, source_target_pairs={{0,3},{1,0},{2,1},{3,2},{4,7},{5,4},{6,5},{7,6},{8,11},{9,8},{10,9... | collective-permute-start | bytes 3342344 | tf_op jit(solution)/shard_map/ppermute | solution.py:59
  30.3 3.0 %collective-permute-start.9 = (bf16[64,1408]{1,0:T(8,128)(2,1)S(1)}, bf16[64,1408]{1,0:T(8,128)(2,1)S(1)}, u32[]{:S(2)}, u32[]{:S(2)}) collective-permute-start(bf16[64,1408]{1,0:T(8,128)(2,1)S(1)} %collective-permute-done.8.refs_1_), channel_id=1, source_target_pairs={{0,28},{1,29},{2,30},{3,31},{4,0},{5,1},{6,2},{7,3},{8,4},{9,5},{1... | collective-permute-start | bytes 540680 | tf_op jit(solution)/shard_map/ppermute | solution.py:59
  33.6 2.1 %collective-permute-done.9.refs_2_ = bf16[64,1408]{1,0:T(8,128)(2,1)S(1)} collective-permute-done((bf16[64,1408]{1,0:T(8,128)(2,1)S(1)}, bf16[64,1408]{1,0:T(8,128)(2,1)S(1)}, u32[]{:S(2)}, u32[]{:S(2)}) %collective-permute-start.9) | collective-permute-done | bytes 180256 | tf_op jit(solution)/shard_map/ppermute | solution.py:59
  35.7 3.4 %collective-permute-start.10 = (bf16[64,1408]{1,0:T(8,128)(2,1)S(1)}, bf16[64,1408]{1,0:T(8,128)(2,1)S(1)}, u32[]{:S(2)}, u32[]{:S(2)}) collective-permute-start(bf16[64,1408]{1,0:T(8,128)(2,1)S(1)} %collective-permute-done.9.refs_2_), channel_id=1, source_target_pairs={{0,28},{1,29},{2,30},{3,31},{4,0},{5,1},{6,2},{7,3},{8,4},{9,5},{1... | collective-permute-start | bytes 540680 | tf_op jit(solution)/shard_map/ppermute | solution.py:59
  39.4 2.4 %collective-permute-done.10.refs_3_ = bf16[64,1408]{1,0:T(8,128)(2,1)S(1)} collective-permute-done((bf16[64,1408]{1,0:T(8,128)(2,1)S(1)}, bf16[64,1408]{1,0:T(8,128)(2,1)S(1)}, u32[]{:S(2)}, u32[]{:S(2)}) %collective-permute-start.10) | collective-permute-done | bytes 180256 | tf_op jit(solution)/shard_map/ppermute | solution.py:59
  41.8 3.7 %collective-permute-done.14.refs_4_ = bf16[64,1408]{1,0:T(8,128)(2,1)S(1)} collective-permute-done((bf16[64,1408]{1,0:T(8,128)(2,1)S(1)}, bf16[64,1408]{1,0:T(8,128)(2,1)S(1)}, u32[]{:S(2)}, u32[]{:S(2)}) %collective-permute-start.14) | collective-permute-done | bytes 180256 | tf_op jit(solution)/shard_map/ppermute | solution.py:59
  45.5 1.2 shard_map.115
  46.7 1.2 collective-permute-start.18
  47.9 1.5 collective-permute-start.19
  49.4 1.2 shard_map.120.spread_ref
  51.7 0.9 shard_map.110
  52.8 2.9 %collective-permute-start.4 = (bf16[128,2048]{1,0:T(8,128)(2,1)S(1)}, bf16[128,2048]{1,0:T(8,128)(2,1)S(1)}, u32[]{:S(2)}, u32[]{:S(2)}) collective-permute-start(bf16[128,2048]{1,0:T(8,128)(2,1)S(1)} %shard_map.111), channel_id=1, source_target_pairs={{0,3},{1,0},{2,1},{3,2},{4,7},{5,4},{6,5},{7,6},{8,11},{9,8},{10,9... | collective-permute-start | bytes 1572872 | tf_op jit(solution)/shard_map/ppermute | solution.py:59
  55.8 6.1 %collective-permute-done.18.below_ref.block_ref = bf16[512,768]{1,0:T(8,128)(2,1)} collective-permute-done((bf16[512,768]{1,0:T(8,128)(2,1)}, bf16[512,768]{1,0:T(8,128)(2,1)}, u32[]{:S(2)}, u32[]{:S(2)}) %collective-permute-start.18) | collective-permute-done | bytes 786464 | tf_op jit(solution)/shard_map/ppermute | solution.py:59
  61.9 1.2 shard_map.118
  63.2 1.2 shard_map.119
  64.3 2.7 %collective-permute-start.21 = (bf16[256,768]{1,0:T(8,128)(2,1)S(1)}, bf16[256,768]{1,0:T(8,128)(2,1)S(1)}, u32[]{:S(2)}, u32[]{:S(2)}) collective-permute-start(bf16[256,768]{1,0:T(8,128)(2,1)S(1)} %shard_map.119), channel_id=1, source_target_pairs={{0,96},{1,97},{2,98},{3,99},{4,100},{5,101},{6,102},{7,103},{8,104... | collective-permute-start | bytes 1179656 | tf_op jit(solution)/shard_map/ppermute | solution.py:59
  67.2 3.4 %shard_map.112 = (bf16[4,272,1536]{2,1,0:T(8,128)(2,1)}, bf16[4,272,512]{2,1,0:T(8,128)(2,1)}) custom-call(s32[11]{0:T(128)S(1)} %stack.47.at_ref.y_ref.bits_ref, bf16[272,2048]{1,0:T(8,128)(2,1)S(1)} %shard_map.109.own_ref, bf16[272,2048]{1,0:T(8,128)(2,1)S(1)} %collective-permute-done.1.block_ref.below_ref, ...), custom_call_target="tpu_custom_call" | custom-call | tf_op jit(solution)/shard_map/pallas_call | solution.py:120
  70.7 5.9 %shard_map.117.part_ref = f32[4,272,768]{2,1,0:T(8,128)S(1)} custom-call(bf16[4,272,1536]{2,1,0:T(8,128)(2,1)} %get-tuple-element.44.rows_ref, bf16[512,768]{1,0:T(8,128)(2,1)} %get-tuple-element.52.own_ref, bf16[512,768]{1,0:T(8,128)(2,1)} %collective-permute-done.18.below_ref.block_ref, bf16[512,768]{1,0:T(8,128)(2,1)} %collective-permute-done.19.above_ref.block_ref), custom_call_target="tpu_custom_call" | custom-call | tf_op jit(solution)/shard_map/pallas_call | solution.py:120
  76.6 10.4 %shard_map.121 = (f32[4,256,512]{2,1,0:T(8,128)}, bf16[4,256,128]{2,1,0:T(8,128)(2,1)}, f32[4,256,128]{2,1,0:T(8,128)}, f32[4,256,128]{2,1,0:T(8,128)}, f32[4,25...) custom-call(f32[4,272,768]{2,1,0:T(8,128)S(1)} %shard_map.117.part_r, ...), custom_call_target="tpu_custom_call" | custom-call | tf_op jit(solution)/shard_map/pallas_call | solution.py:120
  87.0 2.7 %collective-permute-start.16 = (bf16[512,640]{1,0:T(8,128)(2,1)}, bf16[512,640]{1,0:T(8,128)(2,1)S(1)}, u32[]{:S(2)}, u32[]{:S(2)}) collective-permute-start(bf16[512,640]{1,0:T(8,128)(2,1)} %get-tuple-element.49.own_ref), channel_id=1, source_target_pairs={{0,96},{1,97},{2,98},{3,99},{4,100},{5,101},{6,102},{7,103},{8,104... | collective-permute-start | bytes 1966088 | tf_op jit(solution)/shard_map/ppermute | solution.py:59
  91.6 6.0 %collective-permute-done.23.got_ref.g4 = bf16[144,512]{1,0:T(8,128)(2,1)S(1)} collective-permute-done((bf16[144,512]{1,0:T(8,128)(2,1)S(1)}, bf16[144,512]{1,0:T(8,128)(2,1)S(1)}, u32[]{:S(2)}, u32[]{:S(2)}) %collective-permute-start.23) | collective-permute-done | bytes 147488 | tf_op jit(solution)/shard_map/ppermute | solution.py:59
  97.7 1.2 collective-permute-start.24
  98.9 5.8 %collective-permute-done.24.got_ref.g5 = bf16[144,512]{1,0:T(8,128)(2,1)S(1)} collective-permute-done((bf16[144,512]{1,0:T(8,128)(2,1)S(1)}, bf16[144,512]{1,0:T(8,128)(2,1)S(1)}, u32[]{:S(2)}, u32[]{:S(2)}) %collective-permute-start.24) | collective-permute-done | bytes 147488 | tf_op jit(solution)/shard_map/ppermute | solution.py:59
  104.9 8.4 %collective-permute-done.25.got_ref.g6 = bf16[144,512]{1,0:T(8,128)(2,1)S(1)} collective-permute-done((bf16[144,512]{1,0:T(8,128)(2,1)S(1)}, bf16[144,512]{1,0:T(8,128)(2,1)S(1)}, u32[]{:S(2)}, u32[]{:S(2)}) %collective-permute-start.25) | collective-permute-done | bytes 147488 | tf_op jit(solution)/shard_map/ppermute | solution.py:59
  114.7 7.1 %shard_map.116.part_ref = f32[4,272,640]{2,1,0:T(8,128)} custom-call(bf16[4,272,1536]{2,1,0:T(8,128)(2,1)} %get-tuple-element.44.rows_ref, bf16[512,640]{1,0:T(8,128)(2,1)} %get-tuple-element.49.own_ref, bf16[512,640]{1,0:T(8,128)(2,1)S(1)} %collective-permute-done.15.below_ref, bf16[512,640]{1,0:T(8,128)(2,1)S(1)} %collective-permute-done.16.above_ref), custom_call_target="tpu_custom_call" | custom-call | tf_op jit(solution)/shard_map/pallas_call | solution.py:120
  121.8 0.8 copy-done.4
  122.6 6.5 %intra_block.2 = (f32[2,256,512]{2,1,0:T(8,128)}, bf16[2,256,128]{2,1,0:T(8,128)(2,1)}, bf16[2,256,512]{2,1,0:T(8,128)(2,1)}) custom-call(f32[4,272,640]{2,1,0:T(8,128)} %shard_map.116.part_ref, bf16[4,272,512]{2,1,0:T(8,128)(2,1)} %get-tuple-element.50.rows_ref, bf16[512,640]{1,0:T(8,128)(2,1)} %copy-done.4, f32[4,128]{1,0:T(4,128)} %get-tuple-element.84.taps_ref, ...), custom_call_target="tpu_custom_call" | custom-call | tf_op jit(solution)/shard_map/intra_block/pallas_call | solution.py:321
  129.1 6.5 %intra_block.3 = (f32[2,256,512]{2,1,0:T(8,128)}, bf16[2,256,128]{2,1,0:T(8,128)(2,1)}, bf16[2,256,512]{2,1,0:T(8,128)(2,1)}) custom-call(f32[4,272,640]{2,1,0:T(8,128)} %shard_map.116.part_ref, bf16[4,272,512]{2,1,0:T(8,128)(2,1)} %get-tuple-element.50.rows_ref, bf16[512,640]{1,0:T(8,128)(2,1)} %copy-done.4, f32[4,128]{1,0:T(4,128)} %get-tuple-element.84.taps_ref, ...), custom_call_target="tpu_custom_call" | custom-call | tf_op jit(solution)/shard_map/intra_block/pallas_call | solution.py:321
  136.4 5.6 %shard_map.128 = (bf16[256,512]{1,0:T(8,128)(2,1)S(1)}, bf16[256,512]{1,0:T(8,128)(2,1)S(1)}, bf16[256,512]{1,0:T(8,128)(2,1)S(1)}, bf16[256,512]{1,0:T(8,128)(2,1)S(1)}) custom-call(s32[11]{0:T(128)S(1)} %stack.47.at_ref.y_ref.bits_ref, f32[2,256,512]{2,1,0:T(8,128)} %get-tuple-element.61.ya_ref, bf16[2,256,128]{2,1,0:T(8,128)(2,1)} %get-tuple-element.62.ca_ref, ...), custom_call_target="tpu_custom_call" | custom-call | tf_op jit(solution)/shard_map/pallas_call | solution.py:120
  142.1 2.4 %collective-permute-start.28 = (bf16[256,512]{1,0:T(8,128)(2,1)S(1)}, bf16[256,512]{1,0:T(8,128)(2,1)S(1)}, u32[]{:S(2)}, u32[]{:S(2)}) collective-permute-start(bf16[256,512]{1,0:T(8,128)(2,1)S(1)} %get-tuple-element.81), channel_id=1, source_target_pairs={{0,2},{1,3},{2,0},{3,1},{4,6},{5,7},{6,4},{7,5},{8,10},{9,11},{10,... | collective-permute-start | bytes 786440 | tf_op jit(solution)/shard_map/ppermute | solution.py:59
  144.7 6.6 %collective-permute-done.27.q1 = bf16[256,512]{1,0:T(8,128)(2,1)S(1)} collective-permute-done((bf16[256,512]{1,0:T(8,128)(2,1)S(1)}, bf16[256,512]{1,0:T(8,128)(2,1)S(1)}, u32[]{:S(2)}, u32[]{:S(2)}) %collective-permute-start.27) | collective-permute-done | bytes 262176 | tf_op jit(solution)/shard_map/ppermute | solution.py:59
  151.9 4.9 %gate_out.1 = bf16[256,2048]{1,0:T(8,128)(2,1)S(1)} custom-call(s32[11]{0:T(128)S(1)} %stack.47.at_ref.y_ref.bits_ref, bf16[256,512]{1,0:T(8,128)(2,1)S(1)} %get-tuple-element.79.q0, bf16[256,512]{1,0:T(8,128)(2,1)S(1)} %collective-permute-done.27.q1, bf16[256,512]{1,0:T(8,128)(2,1)S(1)} %collective-permute-done.28.q2, ...), custom_call_target="tpu_custom_call" | custom-call | tf_op jit(solution)/shard_map/gate_out/pallas_call | solution.py:426
  156.9 11.9 %collective-permute-start.30 = (bf16[256,2048]{1,0:T(8,128)(2,1)S(1)}, bf16[256,2048]{1,0:T(8,128)(2,1)S(1)}, u32[]{:S(2)}, u32[]{:S(2)}) collective-permute-start(bf16[256,2048]{1,0:T(8,128)(2,1)S(1)} %gate_out.1), channel_id=1, source_target_pairs={{0,128},{128,0},{1,129},{129,1},{2,130},{130,2},{3,131},{131,3},{4... | collective-permute-start | bytes 3145736 | tf_op jit(solution)/shard_map/ppermute | solution.py:638
  168.8 2.3 %collective-permute-done.30 = bf16[256,2048]{1,0:T(8,128)(2,1)S(1)} collective-permute-done((bf16[256,2048]{1,0:T(8,128)(2,1)S(1)}, bf16[256,2048]{1,0:T(8,128)(2,1)S(1)}, u32[]{:S(2)}, u32[]{:S(2)}) %collective-permute-start.30) | collective-permute-done | bytes 1048608 | tf_op jit(solution)/shard_map/ppermute | solution.py:638
  171.0 1.0 copy.13
  (80 shorter events, 9.5 us)
Async XLA Ops:
  0.0 55.7 %copy-start = (f32[1,256]{1,0:T(1,128)S(1)}, f32[1,256]{1,0:T(1,128)}, u32[]{:S(2)}) copy-start(f32[1,256]{1,0:T(1,128)} %param.19) | copy-start | bytes 3076
  0.1 0.9 copy-start.2
  1.6 5.9 %collective-permute-start.5 = (bf16[16,1408]{1,0:T(8,128)(2,1)S(1)}, bf16[16,1408]{1,0:T(8,128)(2,1)S(1)}, u32[]{:S(2)}, u32[]{:S(2)}) collective-permute-start(bf16[16,1408]{1,0:T(8,128)(2,1)S(1)} %get-tuple-element.46), channel_id=1, source_target_pairs={{0,1},{1,2},{2,3},{3,0},{4,5},{5,6},{6,7},{7,4},{8,9},{9,10},{10,1... | collective-permute-start | bytes 135176 | tf_op jit(solution)/shard_map/ppermute | solution.py:59
  3.8 4.5 %collective-permute-start.6 = (bf16[16,1408]{1,0:T(8,128)(2,1)S(1)}, bf16[16,1408]{1,0:T(8,128)(2,1)S(1)}, u32[]{:S(2)}, u32[]{:S(2)}) collective-permute-start(bf16[16,1408]{1,0:T(8,128)(2,1)S(1)} %get-tuple-element.47), channel_id=1, source_target_pairs={{0,2},{1,3},{2,0},{3,1},{4,6},{5,7},{6,4},{7,5},{8,10},{9,11},{10,... | collective-permute-start | bytes 135176 | tf_op jit(solution)/shard_map/ppermute | solution.py:59
  6.5 3.2 %collective-permute-start.7 = (bf16[16,1408]{1,0:T(8,128)(2,1)S(1)}, bf16[16,1408]{1,0:T(8,128)(2,1)S(1)}, u32[]{:S(2)}, u32[]{:S(2)}) collective-permute-start(bf16[16,1408]{1,0:T(8,128)(2,1)S(1)} %get-tuple-element.48), channel_id=1, source_target_pairs={{0,3},{1,0},{2,1},{3,2},{4,7},{5,4},{6,5},{7,6},{8,11},{9,8},{10,9... | collective-permute-start | bytes 135176 | tf_op jit(solution)/shard_map/ppermute | solution.py:59
  10.2 17.5 %collective-permute-start.11 = (bf16[64,1408]{1,0:T(8,128)(2,1)S(1)}, bf16[64,1408]{1,0:T(8,128)(2,1)S(1)}, u32[]{:S(2)}, u32[]{:S(2)}) collective-permute-start(bf16[64,1408]{1,0:T(8,128)(2,1)S(1)} %shard_map.114.refs_0_), channel_id=1, source_target_pairs={{0,4},{1,5},{2,6},{3,7},{4,8},{5,9},{6,10},{7,11},{8,12},{9,13},{1... | collective-permute-start | bytes 540680 | tf_op jit(solution)/shard_map/ppermute | solution.py:59
  12.8 3.1 %collective-permute-start = (bf16[16,2048]{1,0:T(8,128)(2,1)S(1)}, bf16[16,2048]{1,0:T(8,128)(2,1)S(1)}, u32[]{:S(2)}, u32[]{:S(2)}) collective-permute-start(bf16[16,2048]{1,0:T(8,128)(2,1)S(1)} %slice_bitcast_fusion), channel_id=1, source_target_pairs={{0,1},{1,2},{2,3},{3,4},{4,5},{5,6},{6,7},{7,8},{8,9},{9,10},{10,1... | collective-permute-start | bytes 196616 | tf_op jit(solution)/shard_map/ppermute | solution.py:59
  15.9 0.6 copy-start.5
  16.5 34.0 %copy-start.7 = (f32[1,2304]{1,0:T(1,128)S(1)}, f32[1,2304]{1,0:T(1,128)}, u32[]{:S(2)}) copy-start(f32[1,2304]{1,0:T(1,128)} %param.15) | copy-start | bytes 27652
  16.5 34.6 %copy-start.6 = (f32[1,4,2304]{2,1,0:T(4,128)S(1)}, f32[1,4,2304]{2,1,0:T(4,128)}, u32[]{:S(2)}) copy-start(f32[1,4,2304]{2,1,0:T(4,128)} %param.14) | copy-start | bytes 110596
  16.5 35.2 %slice-start.1 = ((f32[1,2304]{1,0:T(1,128)}), f32[1,2048]{1,0:T(1,128)S(1)}, s32[]{:S(2)}) async-start(f32[1,2304]{1,0:T(1,128)} %param.15), calls=%async_computation.1 | async-start | bytes 16384 | tf_op jit(solution)/shard_map/slice | solution.py:598
  18.9 33.8 %copy-start.8 = (f32[1,32]{1,0:T(1,128)S(1)}, f32[1,32]{1,0:T(1,128)}, u32[]{:S(2)}) copy-start(f32[1,32]{1,0:T(1,128)} %param.17) | copy-start | bytes 388
  18.9 33.8 %copy-start.9 = (f32[1,32]{1,0:T(1,128)S(1)}, f32[1,32]{1,0:T(1,128)}, u32[]{:S(2)}) copy-start(f32[1,32]{1,0:T(1,128)} %param.16) | copy-start | bytes 388
  18.9 32.8 %collective-permute-start.1 = (bf16[272,2048]{1,0:T(8,128)(2,1)S(1)}, bf16[272,2048]{1,0:T(8,128)(2,1)S(1)}, u32[]{:S(2)}, u32[]{:S(2)}) collective-permute-start(bf16[272,2048]{1,0:T(8,128)(2,1)S(1)} %shard_map.109.own_ref), channel_id=1, source_target_pairs={{0,1},{1,2},{2,3},{3,0},{4,5},{5,6},{6,7},{7,4},{8,9},{9,10},{10,1... | collective-permute-start | bytes 3342344 | tf_op jit(solution)/shard_map/ppermute | solution.py:59
  20.8 9.6 %collective-permute-start.8 = (bf16[64,1408]{1,0:T(8,128)(2,1)S(1)}, bf16[64,1408]{1,0:T(8,128)(2,1)S(1)}, u32[]{:S(2)}, u32[]{:S(2)}) collective-permute-start(bf16[64,1408]{1,0:T(8,128)(2,1)S(1)} %shard_map.114.refs_0_), channel_id=1, source_target_pairs={{0,28},{1,29},{2,30},{3,31},{4,0},{5,1},{6,2},{7,3},{8,4},{9,5},{1... | collective-permute-start | bytes 540680 | tf_op jit(solution)/shard_map/ppermute | solution.py:59
  27.7 5.9 %collective-permute-start.12 = (bf16[64,1408]{1,0:T(8,128)(2,1)S(1)}, bf16[64,1408]{1,0:T(8,128)(2,1)S(1)}, u32[]{:S(2)}, u32[]{:S(2)}) collective-permute-start(bf16[64,1408]{1,0:T(8,128)(2,1)S(1)} %collective-permute-done.11.refs_7_), channel_id=1, source_target_pairs={{0,4},{1,5},{2,6},{3,7},{4,8},{5,9},{6,10},{7,11},{8,12},{9,13},{1... | collective-permute-start | bytes 540680 | tf_op jit(solution)/shard_map/ppermute | solution.py:59
  27.7 25.0 %collective-permute-start.2 = (bf16[272,2048]{1,0:T(8,128)(2,1)S(1)}, bf16[272,2048]{1,0:T(8,128)(2,1)S(1)}, u32[]{:S(2)}, u32[]{:S(2)}) collective-permute-start(bf16[272,2048]{1,0:T(8,128)(2,1)S(1)} %shard_map.109.own_ref), channel_id=1, source_target_pairs={{0,3},{1,0},{2,1},{3,2},{4,7},{5,4},{6,5},{7,6},{8,11},{9,8},{10,9... | collective-permute-start | bytes 3342344 | tf_op jit(solution)/shard_map/ppermute | solution.py:59
  30.3 5.4 %collective-permute-start.9 = (bf16[64,1408]{1,0:T(8,128)(2,1)S(1)}, bf16[64,1408]{1,0:T(8,128)(2,1)S(1)}, u32[]{:S(2)}, u32[]{:S(2)}) collective-permute-start(bf16[64,1408]{1,0:T(8,128)(2,1)S(1)} %collective-permute-done.8.refs_1_), channel_id=1, source_target_pairs={{0,28},{1,29},{2,30},{3,31},{4,0},{5,1},{6,2},{7,3},{8,4},{9,5},{1... | collective-permute-start | bytes 540680 | tf_op jit(solution)/shard_map/ppermute | solution.py:59
  33.6 5.9 %collective-permute-start.13 = (bf16[64,1408]{1,0:T(8,128)(2,1)S(1)}, bf16[64,1408]{1,0:T(8,128)(2,1)S(1)}, u32[]{:S(2)}, u32[]{:S(2)}) collective-permute-start(bf16[64,1408]{1,0:T(8,128)(2,1)S(1)} %collective-permute-done.12.refs_6_), channel_id=1, source_target_pairs={{0,4},{1,5},{2,6},{3,7},{4,8},{5,9},{6,10},{7,11},{8,12},{9,13},{1... | collective-permute-start | bytes 540680 | tf_op jit(solution)/shard_map/ppermute | solution.py:59
  35.7 6.1 %collective-permute-start.10 = (bf16[64,1408]{1,0:T(8,128)(2,1)S(1)}, bf16[64,1408]{1,0:T(8,128)(2,1)S(1)}, u32[]{:S(2)}, u32[]{:S(2)}) collective-permute-start(bf16[64,1408]{1,0:T(8,128)(2,1)S(1)} %collective-permute-done.9.refs_2_), channel_id=1, source_target_pairs={{0,28},{1,29},{2,30},{3,31},{4,0},{5,1},{6,2},{7,3},{8,4},{9,5},{1... | collective-permute-start | bytes 540680 | tf_op jit(solution)/shard_map/ppermute | solution.py:59
  39.4 6.1 %collective-permute-start.14 = (bf16[64,1408]{1,0:T(8,128)(2,1)S(1)}, bf16[64,1408]{1,0:T(8,128)(2,1)S(1)}, u32[]{:S(2)}, u32[]{:S(2)}) collective-permute-start(bf16[64,1408]{1,0:T(8,128)(2,1)S(1)} %collective-permute-done.13.refs_5_), channel_id=1, source_target_pairs={{0,4},{1,5},{2,6},{3,7},{4,8},{5,9},{6,10},{7,11},{8,12},{9,13},{1... | collective-permute-start | bytes 540680 | tf_op jit(solution)/shard_map/ppermute | solution.py:59
  46.7 15.2 %collective-permute-start.18 = (bf16[512,768]{1,0:T(8,128)(2,1)}, bf16[512,768]{1,0:T(8,128)(2,1)}, u32[]{:S(2)}, u32[]{:S(2)}) collective-permute-start(bf16[512,768]{1,0:T(8,128)(2,1)} %get-tuple-element.52.own_ref), channel_id=1, source_target_pairs={{0,32},{1,33},{2,34},{3,35},{4,36},{5,37},{6,38},{7,39},{8,40},{9,... | collective-permute-start | bytes 2359304 | tf_op jit(solution)/shard_map/ppermute | solution.py:59
  47.9 15.3 %collective-permute-start.19 = (bf16[512,768]{1,0:T(8,128)(2,1)}, bf16[512,768]{1,0:T(8,128)(2,1)}, u32[]{:S(2)}, u32[]{:S(2)}) collective-permute-start(bf16[512,768]{1,0:T(8,128)(2,1)} %get-tuple-element.52.own_ref), channel_id=1, source_target_pairs={{0,96},{1,97},{2,98},{3,99},{4,100},{5,101},{6,102},{7,103},{8,104... | collective-permute-start | bytes 2359304 | tf_op jit(solution)/shard_map/ppermute | solution.py:59
  52.6 14.5 %slice-start = ((f32[1,4,2304]{2,1,0:T(4,128)}), f32[1,4,2048]{2,1,0:T(4,128)S(1)}, s32[]{:S(2)}) async-start(f32[1,4,2304]{2,1,0:T(4,128)} %param.14), calls=%async_computation | async-start | bytes 65536 | tf_op jit(solution)/shard_map/slice | solution.py:595
  52.6 14.6 %collective-permute-start.3 = (bf16[144,2048]{1,0:T(8,128)(2,1)}, bf16[144,2048]{1,0:T(8,128)(2,1)}, u32[]{:S(2)}, u32[]{:S(2)}) collective-permute-start(bf16[144,2048]{1,0:T(8,128)(2,1)} %shard_map.110), channel_id=1, source_target_pairs={{0,1},{1,2},{2,3},{3,0},{4,5},{5,6},{6,7},{7,4},{8,9},{9,10},{10,1... | collective-permute-start | bytes 1769480 | tf_op jit(solution)/shard_map/ppermute | solution.py:59
  52.8 14.4 %collective-permute-start.4 = (bf16[128,2048]{1,0:T(8,128)(2,1)S(1)}, bf16[128,2048]{1,0:T(8,128)(2,1)S(1)}, u32[]{:S(2)}, u32[]{:S(2)}) collective-permute-start(bf16[128,2048]{1,0:T(8,128)(2,1)S(1)} %shard_map.111), channel_id=1, source_target_pairs={{0,3},{1,0},{2,1},{3,2},{4,7},{5,4},{6,5},{7,6},{8,11},{9,8},{10,9... | collective-permute-start | bytes 1572872 | tf_op jit(solution)/shard_map/ppermute | solution.py:59
  63.1 13.5 %collective-permute-start.20 = (bf16[256,768]{1,0:T(8,128)(2,1)S(1)}, bf16[256,768]{1,0:T(8,128)(2,1)S(1)}, u32[]{:S(2)}, u32[]{:S(2)}) collective-permute-start(bf16[256,768]{1,0:T(8,128)(2,1)S(1)} %shard_map.118), channel_id=1, source_target_pairs={{0,32},{1,33},{2,34},{3,35},{4,36},{5,37},{6,38},{7,39},{8,40},{9,... | collective-permute-start | bytes 1179656 | tf_op jit(solution)/shard_map/ppermute | solution.py:59
  64.3 12.2 %collective-permute-start.21 = (bf16[256,768]{1,0:T(8,128)(2,1)S(1)}, bf16[256,768]{1,0:T(8,128)(2,1)S(1)}, u32[]{:S(2)}, u32[]{:S(2)}) collective-permute-start(bf16[256,768]{1,0:T(8,128)(2,1)S(1)} %shard_map.119), channel_id=1, source_target_pairs={{0,96},{1,97},{2,98},{3,99},{4,100},{5,101},{6,102},{7,103},{8,104... | collective-permute-start | bytes 1179656 | tf_op jit(solution)/shard_map/ppermute | solution.py:59
  76.6 37.3 %copy-start.10 = (f32[1,32]{1,0:T(1,128)S(1)}, f32[1,32]{1,0:T(1,128)}, u32[]{:S(2)}) copy-start(f32[1,32]{1,0:T(1,128)} %param.18) | copy-start | bytes 388
  87.0 4.0 %collective-permute-start.22 = (bf16[144,512]{1,0:T(8,128)(2,1)S(1)}, bf16[144,512]{1,0:T(8,128)(2,1)S(1)}, u32[]{:S(2)}, u32[]{:S(2)}) collective-permute-start(bf16[144,512]{1,0:T(8,128)(2,1)S(1)} %get-tuple-element.68.own_ref), channel_id=1, source_target_pairs={{0,4},{1,5},{2,6},{3,7},{4,0},{5,1},{6,2},{7,3},{8,12},{9,13},{10,... | collective-permute-start | bytes 442376 | tf_op jit(solution)/shard_map/ppermute | solution.py:59
  87.0 27.7 %collective-permute-start.15 = (bf16[512,640]{1,0:T(8,128)(2,1)}, bf16[512,640]{1,0:T(8,128)(2,1)S(1)}, u32[]{:S(2)}, u32[]{:S(2)}) collective-permute-start(bf16[512,640]{1,0:T(8,128)(2,1)} %get-tuple-element.49.own_ref), channel_id=1, source_target_pairs={{0,32},{1,33},{2,34},{3,35},{4,36},{5,37},{6,38},{7,39},{8,40},{9,... | collective-permute-start | bytes 1966088 | tf_op jit(solution)/shard_map/ppermute | solution.py:59
  87.0 27.7 %collective-permute-start.16 = (bf16[512,640]{1,0:T(8,128)(2,1)}, bf16[512,640]{1,0:T(8,128)(2,1)S(1)}, u32[]{:S(2)}, u32[]{:S(2)}) collective-permute-start(bf16[512,640]{1,0:T(8,128)(2,1)} %get-tuple-element.49.own_ref), channel_id=1, source_target_pairs={{0,96},{1,97},{2,98},{3,99},{4,100},{5,101},{6,102},{7,103},{8,104... | collective-permute-start | bytes 1966088 | tf_op jit(solution)/shard_map/ppermute | solution.py:59
  89.7 32.1 %collective-permute-start.17 = (bf16[512,640]{1,0:T(8,128)(2,1)}, bf16[512,640]{1,0:T(8,128)(2,1)S(1)}, u32[]{:S(2)}, u32[]{:S(2)}) collective-permute-start(bf16[512,640]{1,0:T(8,128)(2,1)} %get-tuple-element.49.own_ref), channel_id=1, source_target_pairs={{0,64},{1,65},{2,66},{3,67},{4,68},{5,69},{6,70},{7,71},{8,72},{9,... | collective-permute-start | bytes 1966088 | tf_op jit(solution)/shard_map/ppermute | solution.py:59
  91.1 6.6 %collective-permute-start.23 = (bf16[144,512]{1,0:T(8,128)(2,1)S(1)}, bf16[144,512]{1,0:T(8,128)(2,1)S(1)}, u32[]{:S(2)}, u32[]{:S(2)}) collective-permute-start(bf16[144,512]{1,0:T(8,128)(2,1)S(1)} %get-tuple-element.70.own_ref), channel_id=1, source_target_pairs={{0,8},{1,9},{2,10},{3,11},{4,12},{5,13},{6,14},{7,15},{8,0},{9,1},... | collective-permute-start | bytes 442376 | tf_op jit(solution)/shard_map/ppermute | solution.py:59
  97.7 7.0 %collective-permute-start.24 = (bf16[144,512]{1,0:T(8,128)(2,1)S(1)}, bf16[144,512]{1,0:T(8,128)(2,1)S(1)}, u32[]{:S(2)}, u32[]{:S(2)}) collective-permute-start(bf16[144,512]{1,0:T(8,128)(2,1)S(1)} %get-tuple-element.72.own_ref), channel_id=1, source_target_pairs={{0,28},{1,29},{2,30},{3,31},{4,24},{5,25},{6,26},{7,27},{8,20},{9,... | collective-permute-start | bytes 442376 | tf_op jit(solution)/shard_map/ppermute | solution.py:59
  104.8 8.5 %collective-permute-start.25 = (bf16[144,512]{1,0:T(8,128)(2,1)S(1)}, bf16[144,512]{1,0:T(8,128)(2,1)S(1)}, u32[]{:S(2)}, u32[]{:S(2)}) collective-permute-start(bf16[144,512]{1,0:T(8,128)(2,1)S(1)} %get-tuple-element.74.own_ref), channel_id=1, source_target_pairs={{0,32},{1,33},{2,34},{3,35},{4,36},{5,37},{6,38},{7,39},{8,40},{9,... | collective-permute-start | bytes 442376 | tf_op jit(solution)/shard_map/ppermute | solution.py:59
  113.4 22.2 %collective-permute-start.26 = (bf16[144,512]{1,0:T(8,128)(2,1)S(1)}, bf16[144,512]{1,0:T(8,128)(2,1)S(1)}, u32[]{:S(2)}, u32[]{:S(2)}) collective-permute-start(bf16[144,512]{1,0:T(8,128)(2,1)S(1)} %get-tuple-element.76.own_ref), channel_id=1, source_target_pairs={{0,96},{1,97},{2,98},{3,99},{4,100},{5,101},{6,102},{7,103},{8,104... | collective-permute-start | bytes 442376 | tf_op jit(solution)/shard_map/ppermute | solution.py:59
  121.8 0.8 copy-start.4
  136.3 15.6 %copy-start.1 = (bf16[1,256,2048]{2,1,0:T(8,128)(2,1)S(1)}, bf16[1,256,2048]{2,1,0:T(8,128)(2,1)}, u32[]{:S(2)}) copy-start(bf16[1,256,2048]{2,1,0:T(8,128)(2,1)} %param.11) | copy-start | bytes 3145732
  136.4 15.6 %copy-start.3 = (f32[1,2048]{1,0:T(1,128)S(1)}, f32[1,2048]{1,0:T(1,128)}, u32[]{:S(2)}) copy-start(f32[1,2048]{1,0:T(1,128)} %gain_ref.3) | copy-start | bytes 24580
  142.0 9.3 %collective-permute-start.27 = (bf16[256,512]{1,0:T(8,128)(2,1)S(1)}, bf16[256,512]{1,0:T(8,128)(2,1)S(1)}, u32[]{:S(2)}, u32[]{:S(2)}) collective-permute-start(bf16[256,512]{1,0:T(8,128)(2,1)S(1)} %get-tuple-element.80), channel_id=1, source_target_pairs={{0,1},{1,2},{2,3},{3,0},{4,5},{5,6},{6,7},{7,4},{8,9},{9,10},{10,1... | collective-permute-start | bytes 786440 | tf_op jit(solution)/shard_map/ppermute | solution.py:59
  142.1 9.2 %collective-permute-start.28 = (bf16[256,512]{1,0:T(8,128)(2,1)S(1)}, bf16[256,512]{1,0:T(8,128)(2,1)S(1)}, u32[]{:S(2)}, u32[]{:S(2)}) collective-permute-start(bf16[256,512]{1,0:T(8,128)(2,1)S(1)} %get-tuple-element.81), channel_id=1, source_target_pairs={{0,2},{1,3},{2,0},{3,1},{4,6},{5,7},{6,4},{7,5},{8,10},{9,11},{10,... | collective-permute-start | bytes 786440 | tf_op jit(solution)/shard_map/ppermute | solution.py:59
  144.4 7.5 %collective-permute-start.29 = (bf16[256,512]{1,0:T(8,128)(2,1)S(1)}, bf16[256,512]{1,0:T(8,128)(2,1)S(1)}, u32[]{:S(2)}, u32[]{:S(2)}) collective-permute-start(bf16[256,512]{1,0:T(8,128)(2,1)S(1)} %get-tuple-element.82), channel_id=1, source_target_pairs={{0,3},{1,0},{2,1},{3,2},{4,7},{5,4},{6,5},{7,6},{8,11},{9,8},{10,9... | collective-permute-start | bytes 786440 | tf_op jit(solution)/shard_map/ppermute | solution.py:59
  156.9 14.2 %collective-permute-start.30 = (bf16[256,2048]{1,0:T(8,128)(2,1)S(1)}, bf16[256,2048]{1,0:T(8,128)(2,1)S(1)}, u32[]{:S(2)}, u32[]{:S(2)}) collective-permute-start(bf16[256,2048]{1,0:T(8,128)(2,1)S(1)} %gate_out.1), channel_id=1, source_target_pairs={{0,128},{128,0},{1,129},{129,1},{2,130},{130,2},{3,131},{131,3},{4... | collective-permute-start | bytes 3145736 | tf_op jit(solution)/shard_map/ppermute | solution.py:638
